TPU v7x, 256 devices: a whole 4x4x8 slice. The times are simulated.
256 devices in a mesh: own: 64 (over y, z, core), split: 4 (over x).
Axes of the slice: x: 4, y: 4, z: 8, core: 2. Of those that a mesh axis runs over, the one named last changes fastest.
Arguments:
- source_coords: float32 [256, 50, 256], P('own'), may hold values from -1.5 to 1.5
- target_coords: float32 [256, 50, 256], P('own'), may hold values from -1.5 to 1.5
- source_logmass: float32 [256, 256], P('own'), may hold values from -3 to 3
- target_logmass: float32 [256, 256], P('own'), may hold values from -3 to 3
- target_prior: float32 [256, 256], P('own'), may hold values from -6 to 121.5
- pair_source: int32 [64, 4, 64, 1], P('own', 'split'), may hold values from 0 to 3, as said below
- pair_target: int32 [64, 4, 64, 1], P('own', 'split'), may hold values from -1 to 3, as said below
Outputs:
- source_potential: float32 [256, 256], P('own')
- target_potential: float32 [256, 256], P('own')
Inputs may be any that keep to these rules, and one draw needn't show every extreme that they name: `pair_source`: names one of the 4 source clusters of owner o. `pair_target`: -1 marks an empty slot. Live (source, target) pairs are all distinct; every source cluster and every target cluster is in some live pair. Bucket b of a device holds at most one pair whose target cluster belongs to owner b, and some device has all its slots live.
All inputs are finite; a program needn't handle non-finite values.
Results may differ from a plain program's by a relative error of at most 0.00011.
Values sent between devices are 32-bit elements; how exact they have to be, the bound alone decides.
No kernel may reach another device: no remote copies, remote signals or barrier semaphores. Data moves between devices by JAX's collectives and lax.ppermute only.
A program may use at most 128 MiB of HBM per device.

v0:
```python
import math

import jax
import jax.numpy as jnp
from jax import lax
from jax.sharding import PartitionSpec as P

EPSILON = 0.5
NEGATIVE = -1e30


def copy_for_each(value, axis):
    copies = jnp.broadcast_to(value, (lax.axis_size(axis), *value.shape))
    return lax.all_to_all(copies, axis, split_axis=0, concat_axis=0, tiled=True)


def all_in_one(value, axis):
    leaves = jax.tree.leaves(value)
    turns = sorted(range(len(leaves)), key=lambda k: -leaves[k].size)
    width = (1, *leaves[turns[0]].shape)[-1]
    lines = [
        jnp.pad(leaves[k].reshape(-1), (0, -leaves[k].size % width)).reshape(-1, width)
        for k in turns
    ]
    both, at, found = (copy_for_each(jnp.concatenate(lines), axis), 0, {})
    for k, line in zip(turns, lines):
        share = both[:, at : at + len(line)].reshape(len(both), -1)
        found[k] = share[:, : leaves[k].size].reshape(-1, *leaves[k].shape)
        at += len(line)
    numbers = iter(range(len(leaves)))
    return jax.tree.map(lambda _: found[next(numbers)], value)


def combined_pairwise(pieces, combine):
    while len(jax.tree.leaves(pieces)[0]) > 1:
        pieces = jax.vmap(combine)(
            *(jax.tree.map(lambda part: part[side::2], pieces) for side in (0, 1))
        )
    return jax.tree.map(lambda part: part[0], pieces)


def merged(value, axis, combine):
    pieces = all_in_one(value, axis)
    return combined_pairwise(pieces, combine)


def sent_together(arrays, axis, split_dim, concat_dim, along):
    widths = [math.prod(a.shape[along:]) for a in arrays]
    both = jnp.concatenate(
        [a.reshape(*a.shape[:along], w) for a, w in zip(arrays, widths)], axis=along
    )
    filled = lax.all_to_all(both, axis, split_axis=split_dim, concat_axis=concat_dim, tiled=True)
    pieces = jnp.split(filled, [sum(widths[:k]) for k in range(1, len(widths))], axis=along)
    return tuple(
        (b.reshape(*filled.shape[:along], *a.shape[along:]) for a, b in zip(arrays, pieces))
    )


def pair_costs(left_part, right_part):
    inner_sum = jnp.einsum("bpi,bpj->bij", left_part, right_part, precision=lax.Precision.HIGHEST)
    source_norm = jnp.sum(left_part * left_part, axis=1)
    target_norm = jnp.sum(right_part * right_part, axis=1)
    return source_norm[:, :, None] + target_norm[:, None, :] - 2.0 * inner_sum


def combine_parts(left_part, right_part):
    ceiling = jnp.maximum(left_part[0], right_part[0])
    amount = left_part[1] * jnp.exp(left_part[0] - ceiling) + right_part[1] * jnp.exp(
        right_part[0] - ceiling
    )
    return (ceiling, amount)


def body(
    source_coords,
    target_coords,
    source_logmass,
    target_logmass,
    target_prior,
    pair_source,
    pair_target,
):
    owner_count = lax.axis_size("own")
    cluster_count = source_coords.shape[0]
    cell_count = source_coords.shape[2]
    targets_here = pair_target.reshape(owner_count, -1)
    bucket_size = targets_here.shape[1]
    slot_count = owner_count * bucket_size
    slot_group = math.gcd(16, slot_count)
    sources_here = pair_source.reshape(-1)
    living = targets_here.reshape(-1) >= 0
    safe_target = jnp.maximum(targets_here, 0)
    all_coords, all_prior = (
        lax.all_gather(target_coords, "own", axis=0, tiled=True),
        lax.all_gather(target_prior, "own", axis=0, tiled=True),
    )
    global_ids = (
        jnp.arange(owner_count, dtype=jnp.int32)[:, None] * cluster_count + safe_target
    ).reshape(-1)
    blocks = all_coords[global_ids]
    priors = all_prior[global_ids]
    ordering = jnp.argsort(jnp.where(living, 0, 1).astype(jnp.int32), stable=True)
    live_count = jnp.sum(living.astype(jnp.int32))
    round_count = (live_count + slot_group - 1) // slot_group
    cluster_range = jnp.arange(cluster_count, dtype=jnp.int32)

    def row_round(round_index, running):
        ceiling, amount, stored = running
        chosen = lax.dynamic_slice_in_dim(ordering, round_index * slot_group, slot_group)
        alive_rows = living[chosen]
        anchor = sources_here[chosen]
        pair_cost = pair_costs(source_coords[anchor], blocks[chosen])
        exponent = (priors[chosen][:, None, :] - pair_cost) / EPSILON
        summit = jnp.max(exponent, axis=2)
        weights = jnp.sum(jnp.exp(exponent - summit[:, :, None]), axis=2)
        belongs = (anchor[:, None] == cluster_range[None, :]) & alive_rows[:, None]
        candidate = jnp.where(belongs[:, :, None], summit[:, None, :], NEGATIVE)
        new_ceiling = jnp.maximum(ceiling, jnp.max(candidate, axis=0))
        scaled = jnp.where(
            belongs[:, :, None], weights[:, None, :] * jnp.exp(candidate - new_ceiling[None]), 0.0
        )
        amount = amount * jnp.exp(ceiling - new_ceiling) + jnp.sum(scaled, axis=0)
        return (new_ceiling, amount, stored)

    empty_store = jnp.zeros((1,), jnp.float32)
    start_ceiling = jnp.full((cluster_count, cell_count), NEGATIVE, jnp.float32)
    start_amount = jnp.zeros((cluster_count, cell_count), jnp.float32)
    row_ceiling, row_amount, stored = lax.fori_loop(
        0, round_count, row_round, (start_ceiling, start_amount, empty_store)
    )
    row_ceiling, row_amount = merged((row_ceiling, row_amount), "split", combine_parts)
    source_potential = EPSILON * source_logmass - EPSILON * (row_ceiling + jnp.log(row_amount))

    def column_round(round_index, running):
        col_ceiling, col_amount = running
        chosen = lax.dynamic_slice_in_dim(ordering, round_index * slot_group, slot_group)
        alive_rows = living[chosen]
        anchor = sources_here[chosen]
        pair_cost = pair_costs(source_coords[anchor], blocks[chosen])
        exponent = (source_potential[anchor][:, :, None] - pair_cost) / EPSILON
        summit = jnp.max(exponent, axis=1)
        weights = jnp.sum(jnp.exp(exponent - summit[:, None, :]), axis=1)
        summit = jnp.where(alive_rows[:, None], summit, NEGATIVE)
        weights = jnp.where(alive_rows[:, None], weights, 0.0)
        return (col_ceiling.at[chosen].set(summit), col_amount.at[chosen].set(weights))

    slot_ceiling = jnp.full((slot_count, cell_count), NEGATIVE, jnp.float32)
    slot_amount = jnp.zeros((slot_count, cell_count), jnp.float32)
    slot_ceiling, slot_amount = lax.fori_loop(
        0, round_count, column_round, (slot_ceiling, slot_amount)
    )
    got_ceiling, got_amount, got_ids = sent_together(
        (
            slot_ceiling.reshape(owner_count, bucket_size, cell_count),
            slot_amount.reshape(owner_count, bucket_size, cell_count),
            targets_here.astype(jnp.float32),
        ),
        "own",
        0,
        0,
        2,
    )
    got_ceiling = got_ceiling.reshape(-1, cell_count)
    got_amount = got_amount.reshape(-1, cell_count)
    belongs = got_ids.reshape(-1)[:, None] == cluster_range.astype(jnp.float32)[None, :]
    candidate = jnp.where(belongs[:, :, None], got_ceiling[:, None, :], NEGATIVE)
    col_ceiling = jnp.max(candidate, axis=0)
    col_amount = jnp.sum(
        jnp.where(
            belongs[:, :, None],
            got_amount[:, None, :] * jnp.exp(candidate - col_ceiling[None]),
            0.0,
        ),
        axis=0,
    )
    col_ceiling, col_amount = merged((col_ceiling, col_amount), "split", combine_parts)
    target_potential = EPSILON * target_logmass - EPSILON * (col_ceiling + jnp.log(col_amount))
    return (source_potential, target_potential)


def solution(mesh):
    return jax.shard_map(
        body,
        mesh=mesh,
        in_specs=(
            P("own", None, None),
            P("own", None, None),
            P("own", None),
            P("own", None),
            P("own", None),
            P("own", "split", None, None),
            P("own", "split", None, None),
        ),
        out_specs=(P("own", None), P("own", None)),
        check_vma=False,
    )
```

profile of v0, /device:TPU:64, one launch (start us, length us, event | category | flops | bytes accessed | tf_op | source)
XLA Modules:
  0.0 267.1 jit_solution(5948735740134215514)
XLA Ops:
  10.9 45.8 %all-gather = f32[64,4,256]{2,1,0:T(4,128)S(1)} all-gather(f32[1,4,256]{2,1,0:T(4,128)} %bitcast.57), channel_id=1, replica_groups=mesh['own'=64,'split'=4] {'own'}, dimensions={0}, use_global_device_ids=true | all-gather | bytes 266240 | tf_op jit(solution)/shard_map/all_gather | solution.py:95
  61.9 44.4 %all-gather.3.cloned.1.call-done = f32[256,50,256]{2,1,0:T(8,128)} async-done(((f32[4,50,256]{2,1,0:T(8,128)}), f32[256,50,256]{2,1,0:T(8,128)}) %all-gather.3.cloned.1.call-update) | async-done | bytes 13107216 | tf_op jit(solution)/shard_map/all_gather | solution.py:94
  106.3 7.7 %gather_fusion.11 = f32[64,50,256]{2,1,0:T(8,128)} fusion(f32[256,50,256]{2,1,0:T(8,128)} %all-gather.3.cloned.1.call-done, s32[1024]{0:T(1024)S(1)} %pad_clamp_fusion.4), kind=kCustom, calls=%fused_computation.11 | custom fusion | bytes 6553856 | tf_op jit(solution)/shard_map/gather | solution.py:100
  114.0 51.8 %while.26 = (s32[]{:T(128)}, f32[4,256]{1,0:T(4,128)S(1)}, f32[4,256]{1,0:T(4,128)S(1)}, s32[]{:T(128)}, s32[64]{0:T(128)S(1)}, /*index=5*/s32[64]{0:T(128)S(1)}...) while((s32[]{:T(128)}, f32[4,256]{1,0:T(4,128)S(1)}, ...), condition=%wide.region_9.10_spmd.clone, body=%wide.region_2.9_spmd.clone.sunk | while | flops 643698944 | bytes 15267111 | solution.py:128
  118.9 5.1 %fusion.66 = (f32[16,256]{1,0:T(8,128)S(1)}, f32[16,256,256]{1,2,0:T(8,128)S(1)}) fusion(f32[16,256]{1,0:T(8,128)S(1)} %get-tuple-element.402, f32[16,256]{1,0:T(8,128)S(1)} %get-tuple-element.403, f32[16,256]{1,0:T(8,128)S(1)} %gather_fusion.8, f32[16,50,256]{2,1,0:T(8,128)S(1)} %gather_fusion.7, f32[16,50,256]{2,1,0:T(8,128)S(1)} %gather_fusion.5), kind=kOutput, calls=%fused_computation.35.clone.1 | convolution fusion | flops 635432960 | bytes 5898240 | tf_op jit(solution)/shard_map/while/body/bpi,bpj->bij/dot_general | solution.py:60
  128.4 2.6 gather_fusion.5
  131.8 5.1 %fusion.66 = (f32[16,256]{1,0:T(8,128)S(1)}, f32[16,256,256]{1,2,0:T(8,128)S(1)}) fusion(f32[16,256]{1,0:T(8,128)S(1)} %get-tuple-element.402, f32[16,256]{1,0:T(8,128)S(1)} %get-tuple-element.403, f32[16,256]{1,0:T(8,128)S(1)} %gather_fusion.8, f32[16,50,256]{2,1,0:T(8,128)S(1)} %gather_fusion.7, f32[16,50,256]{2,1,0:T(8,128)S(1)} %gather_fusion.5), kind=kOutput, calls=%fused_computation.35.clone.1 | convolution fusion | flops 635432960 | bytes 5898240 | tf_op jit(solution)/shard_map/while/body/bpi,bpj->bij/dot_general | solution.py:60
  141.3 2.6 gather_fusion.5
  144.8 5.1 %fusion.66 = (f32[16,256]{1,0:T(8,128)S(1)}, f32[16,256,256]{1,2,0:T(8,128)S(1)}) fusion(f32[16,256]{1,0:T(8,128)S(1)} %get-tuple-element.402, f32[16,256]{1,0:T(8,128)S(1)} %get-tuple-element.403, f32[16,256]{1,0:T(8,128)S(1)} %gather_fusion.8, f32[16,50,256]{2,1,0:T(8,128)S(1)} %gather_fusion.7, f32[16,50,256]{2,1,0:T(8,128)S(1)} %gather_fusion.5), kind=kOutput, calls=%fused_computation.35.clone.1 | convolution fusion | flops 635432960 | bytes 5898240 | tf_op jit(solution)/shard_map/while/body/bpi,bpj->bij/dot_general | solution.py:60
  154.3 2.6 gather_fusion.5
  157.7 5.1 %fusion.66 = (f32[16,256]{1,0:T(8,128)S(1)}, f32[16,256,256]{1,2,0:T(8,128)S(1)}) fusion(f32[16,256]{1,0:T(8,128)S(1)} %get-tuple-element.402, f32[16,256]{1,0:T(8,128)S(1)} %get-tuple-element.403, f32[16,256]{1,0:T(8,128)S(1)} %gather_fusion.8, f32[16,50,256]{2,1,0:T(8,128)S(1)} %gather_fusion.7, f32[16,50,256]{2,1,0:T(8,128)S(1)} %gather_fusion.5), kind=kOutput, calls=%fused_computation.35.clone.1 | convolution fusion | flops 635432960 | bytes 5898240 | tf_op jit(solution)/shard_map/while/body/bpi,bpj->bij/dot_general | solution.py:60
  166.4 3.3 %all-to-all-start = ((f32[4,8,256]{2,1,0:T(8,128)}), f32[4,8,256]{2,1,0:T(8,128)S(1)}, u32[]{:S(2)}, u32[]{:S(2)}) async-start(f32[4,8,256]{2,1,0:T(8,128)} %broadcast_in_dim.148), calls=%async_computation | async-start | bytes 65536 | tf_op jit(solution)/shard_map/all_to_all | solution.py:14
  169.8 5.3 %all-to-all-done = f32[4,8,256]{2,1,0:T(8,128)S(1)} async-done(((f32[4,8,256]{2,1,0:T(8,128)}), f32[4,8,256]{2,1,0:T(8,128)S(1)}, u32[]{:S(2)}, u32[]{:S(2)}) %all-to-all-start) | async-done | bytes 32800 | tf_op jit(solution)/shard_map/all_to_all | solution.py:14
  175.2 56.8 %while.25 = (s32[]{:T(128)}, f32[64,256]{1,0:T(8,128)S(1)}, f32[64,256]{1,0:T(8,128)S(1)}, s32[]{:T(128)}, s32[64]{0:T(128)S(1)}, /*index=5*/pred[64]{0:T(512)(1...) while((s32[]{:T(128)}, f32[64,256]{1,0:T(8,128)S(1)}, ...), condition=%wide.region_17.18_spmd, body=%wide.region_10.17_spmd.sunk | while | flops 643590272 | bytes 15329327 | solution.py:149
  180.1 5.1 %fusion.62 = (f32[16,256]{1,0:T(8,128)S(1)}, f32[16,256,256]{2,1,0:T(8,128)S(1)}) fusion(f32[16,256]{1,0:T(8,128)S(1)} %get-tuple-element.388, f32[16,256]{1,0:T(8,128)S(1)} %get-tuple-element.389, f32[16,256]{1,0:T(8,128)S(1)} %gather_fusion.3, f32[16,50,256]{2,1,0:T(8,128)S(1)} %gather_fusion.2, f32[16,50,256]{2,1,0:T(8,128)S(1)} %gather_fusion), kind=kOutput, calls=%fused_computation.17.clone.1 | convolution fusion | flops 635432960 | bytes 5898240 | tf_op jit(solution)/shard_map/while/body/bpi,bpj->bij/dot_general | solution.py:60
  190.8 2.6 gather_fusion
  194.3 5.1 %fusion.62 = (f32[16,256]{1,0:T(8,128)S(1)}, f32[16,256,256]{2,1,0:T(8,128)S(1)}) fusion(f32[16,256]{1,0:T(8,128)S(1)} %get-tuple-element.388, f32[16,256]{1,0:T(8,128)S(1)} %get-tuple-element.389, f32[16,256]{1,0:T(8,128)S(1)} %gather_fusion.3, f32[16,50,256]{2,1,0:T(8,128)S(1)} %gather_fusion.2, f32[16,50,256]{2,1,0:T(8,128)S(1)} %gather_fusion), kind=kOutput, calls=%fused_computation.17.clone.1 | convolution fusion | flops 635432960 | bytes 5898240 | tf_op jit(solution)/shard_map/while/body/bpi,bpj->bij/dot_general | solution.py:60
  205.1 2.6 gather_fusion
  208.5 5.1 %fusion.62 = (f32[16,256]{1,0:T(8,128)S(1)}, f32[16,256,256]{2,1,0:T(8,128)S(1)}) fusion(f32[16,256]{1,0:T(8,128)S(1)} %get-tuple-element.388, f32[16,256]{1,0:T(8,128)S(1)} %get-tuple-element.389, f32[16,256]{1,0:T(8,128)S(1)} %gather_fusion.3, f32[16,50,256]{2,1,0:T(8,128)S(1)} %gather_fusion.2, f32[16,50,256]{2,1,0:T(8,128)S(1)} %gather_fusion), kind=kOutput, calls=%fused_computation.17.clone.1 | convolution fusion | flops 635432960 | bytes 5898240 | tf_op jit(solution)/shard_map/while/body/bpi,bpj->bij/dot_general | solution.py:60
  219.3 2.6 gather_fusion
  222.7 5.1 %fusion.62 = (f32[16,256]{1,0:T(8,128)S(1)}, f32[16,256,256]{2,1,0:T(8,128)S(1)}) fusion(f32[16,256]{1,0:T(8,128)S(1)} %get-tuple-element.388, f32[16,256]{1,0:T(8,128)S(1)} %get-tuple-element.389, f32[16,256]{1,0:T(8,128)S(1)} %gather_fusion.3, f32[16,50,256]{2,1,0:T(8,128)S(1)} %gather_fusion.2, f32[16,50,256]{2,1,0:T(8,128)S(1)} %gather_fusion), kind=kOutput, calls=%fused_computation.17.clone.1 | convolution fusion | flops 635432960 | bytes 5898240 | tf_op jit(solution)/shard_map/while/body/bpi,bpj->bij/dot_general | solution.py:60
  233.0 6.0 %all-to-all-start.1 = ((f32[64,1,513]{2,1,0:T(1,128)}), f32[64,1,513]{2,1,0:T(1,128)S(1)}, u32[]{:S(2)}, u32[]{:S(2)}) async-start(f32[64,1,513]{2,1,0:T(1,128)} %pad_maximum_fusion), calls=%async_computation.1 | async-start | bytes 327680 | tf_op jit(solution)/shard_map/all_to_all | solution.py:52
  239.0 10.0 %all-to-all-done.1 = f32[64,1,513]{2,1,0:T(1,128)S(1)} async-done(((f32[64,1,513]{2,1,0:T(1,128)}), f32[64,1,513]{2,1,0:T(1,128)S(1)}, u32[]{:S(2)}, u32[]{:S(2)}) %all-to-all-start.1) | async-done | bytes 131360 | tf_op jit(solution)/shard_map/all_to_all | solution.py:52
  250.1 9.5 %all_to_all.15 = f32[4,8,256]{2,1,0:T(8,128)S(1)} all-to-all(f32[4,8,256]{2,1,0:T(8,128)S(1)} %broadcast_in_dim.156), channel_id=1, replica_groups=mesh['own'=64,'split'=4] {'split'}, dimensions={0} | all-to-all | bytes 65536 | tf_op jit(solution)/shard_map/all_to_all | solution.py:14
  (162 shorter events, 62.7 us)
Async XLA Ops:
  7.2 99.1 %all-gather.3.cloned.1.call-start = ((), (), s32[]{:S(2)}) async-start(), calls=%async_computation.3 | async-start | bytes 14909440 | tf_op jit(solution)/shard_map/all_gather | solution.py:94
  56.8 57.2 %copy-start = (s32[1,1,64,1]{2,3,1,0:T(1,128)S(1)}, s32[1,1,64,1]{2,3,1,0:T(1,128)}, u32[]{:S(2)}) copy-start(s32[1,1,64,1]{2,3,1,0:T(1,128)} %param.16) | copy-start | bytes 772
  114.0 55.7 %copy-start.4 = (s32[1,1,64,1]{2,3,1,0:T(1,128)S(1)}, s32[1,1,64,1]{2,3,1,0:T(1,128)}, u32[]{:S(2)}) copy-start(s32[1,1,64,1]{2,3,1,0:T(1,128)} %param.17) | copy-start | bytes 772
  114.0 61.1 %copy-start.2 = (f32[4,256]{1,0:T(4,128)S(1)}, f32[4,256]{1,0:T(4,128)}, u32[]{:S(2)}) copy-start(f32[4,256]{1,0:T(4,128)} %param.13) | copy-start | bytes 12292
  166.4 8.7 %all-to-all-start = ((f32[4,8,256]{2,1,0:T(8,128)}), f32[4,8,256]{2,1,0:T(8,128)S(1)}, u32[]{:S(2)}, u32[]{:S(2)}) async-start(f32[4,8,256]{2,1,0:T(8,128)} %broadcast_in_dim.148), calls=%async_computation | async-start | bytes 65536 | tf_op jit(solution)/shard_map/all_to_all | solution.py:14
  175.2 84.4 %copy-start.3 = (f32[4,256]{1,0:T(4,128)S(1)}, f32[4,256]{1,0:T(4,128)}, u32[]{:S(2)}) copy-start(f32[4,256]{1,0:T(4,128)} %param.14) | copy-start | bytes 12292
  232.1 28.1 %copy-start.1 = (f32[4,256]{1,0:T(4,128)}, f32[4,256]{1,0:T(4,128)S(1)}, u32[]{:S(2)}) copy-start(f32[4,256]{1,0:T(4,128)S(1)} %get-tuple-element.500) | copy-start | bytes 12292
  233.0 16.1 %all-to-all-start.1 = ((f32[64,1,513]{2,1,0:T(1,128)}), f32[64,1,513]{2,1,0:T(1,128)S(1)}, u32[]{:S(2)}, u32[]{:S(2)}) async-start(f32[64,1,513]{2,1,0:T(1,128)} %pad_maximum_fusion), calls=%async_computation.1 | async-start | bytes 327680 | tf_op jit(solution)/shard_map/all_to_all | solution.py:52
Sparse Core Ops, SparseCore 0:
  10.7 95.4 all-gather.2
where the time goes:
time: 269 us; the launch traced here: 267 us
  waiting for transfers between devices  59.7 us (22%)
  blocking collectives  55.3 us (21%)
  local copies, waits for them, and re-layouts  53.8 us (20%)
  matrix products  40.8 us (15%)
  other arithmetic  32.4 us (12%)
  between operations  14.9 us (6%)
  starting transfers between devices  9.31 us (3%)
    all_gather x1, blocking collectives, body(): lax.all_gather(target_prior, 'own', axis=0, tiled=True)  45.8 us
    all_gather x1, waiting for transfers between devices, body(): lax.all_gather(target_coords, 'own', axis=0, tiled=True)  44.4 us
    dot_general x8, matrix products, pair_costs(): jnp.einsum('bpi,bpj->bij', left_part, right_part, precision=lax.Precision...  40.8 us
    gather x8, local copies, waits for them, and re-layouts, row_round(): pair_cost = pair_costs(source_coords[anchor], blocks[chosen])  13 us
    gather x8, local copies, waits for them, and re-layouts, column_round(): pair_cost = pair_costs(source_coords[anchor], blocks[chosen])  13 us
    all_to_all x1, waiting for transfers between devices, sent_together(): lax.all_to_all(both, axis, split_axis=split_dim, concat_axis=concat_dim,...  10 us
    all_to_all x1, blocking collectives, copy_for_each(): return lax.all_to_all(copies, axis, split_axis=0, concat_axis=0, tiled=True)  9.5 us
    reduce_sum x4, other arithmetic, column_round(): weights = jnp.sum(jnp.exp(exponent - summit[:, None, :]), axis=1)  8.21 us
  transfers between devices with their start and end apart: 3, of which 3 were waited for; matrix products, arithmetic and copies ran while one was open for 2% of the time, Pallas kernels for 0%

commit v1 on v0

v1 whole, which is shorter than its diff:
```python
import math

import jax
import jax.numpy as jnp
from jax import lax
from jax.experimental import pallas as pl
from jax.experimental.pallas import tpu as pltpu
from jax.sharding import PartitionSpec as P

EPSILON = 0.5
NEGATIVE = -1e30
LN2 = math.log(2.0)
SCALE = 1.0 / (EPSILON * LN2)

COMP = 50
CL = 4
CELLS = 256
NY, NZ, NC, NX = 4, 8, 2, 4
AXES = ("own", "split")

Z_FIRST = (0, 1, 2, 3)
Z_SECOND = (4, -1, -2, -3)

BLOCK = 64
PRODUCTS = ((0, 0), (0, 1), (1, 0), (1, 1), (0, 2), (2, 0))
DEPTH = BLOCK * len(PRODUCTS)
SLOTS = 64
GROUP = 2
LIST = SLOTS + 8

f32, bf16 = jnp.float32, jnp.bfloat16


def device(x, y, z, c):
    return (((y % NY) * NZ + z % NZ) * NC + c % NC) * NX + x % NX


def fetched(value, source):
    pairs = [
        (device(*source(x, y, z, c)), device(x, y, z, c))
        for y in range(NY)
        for z in range(NZ)
        for c in range(NC)
        for x in range(NX)
    ]
    return lax.ppermute(value, AXES, pairs)


def from_x(value, k):
    return fetched(value, lambda x, y, z, c: (x + k, y, z, c))


def from_y(value, k):
    return fetched(value, lambda x, y, z, c: (x, y + k, z, c))


def from_core(value):
    return fetched(value, lambda x, y, z, c: (x, y, z, c + 1))


def three_parts(v):
    high = v.astype(bf16).astype(f32)
    rest = v - high
    middle = rest.astype(bf16).astype(f32)
    return high, middle, rest - middle


def load_cluster(ref, a):
    top = ref[a, 0:48, :]
    tail = ref[a, 48:56, :]
    row = lax.broadcasted_iota(jnp.int32, (8, CELLS), 0)
    extra = tail[2:3, :]
    tail = jnp.where(row < 2, tail, 0.0)
    square = jnp.sum(top * top, axis=0, keepdims=True) + jnp.sum(tail * tail, axis=0, keepdims=True)
    return top, tail, extra, square


def with_rows(tail, first, second):
    row = lax.broadcasted_iota(jnp.int32, (8, CELLS), 0)
    for k in range(3):
        tail = jnp.where(row == 2 + k, first[k], tail)
        tail = jnp.where(row == 5 + k, second[k], tail)
    return tail


def store_operand(put, top, tail, side, first, second):
    tops, tails = three_parts(top), three_parts(tail)
    zeros = jnp.zeros((8, CELLS), f32)
    for n, product in enumerate(PRODUCTS):
        part = product[side]
        end = with_rows(tails[part], first, second) if n == 0 else tails[part]
        put(n * BLOCK, tops[part].astype(bf16))
        put(n * BLOCK + 48, jnp.concatenate([end, zeros], axis=0).astype(bf16))


def logsum(top, total):
    return jnp.where(total > 0.0, top + jnp.log2(total), NEGATIVE)


def merged(parts):
    top = parts[0]
    for part in parts[1:]:
        top = jnp.maximum(top, part)
    total = sum(jnp.exp2(part - top) for part in parts)
    return top + jnp.log2(total)


def over_pairs(count, list_ref, left_ref, right_ref, pick, top_ref, sum_ref):
    def step(q, carry):
        for r in range(GROUP):
            pair = list_ref[q * GROUP + r]
            source, target = pair >> 8, pair & 255
            left, right, place = pick(source, target)
            e = jnp.dot(left_ref[left], right_ref[right], preferred_element_type=f32)
            e = e.reshape(CELLS // 8, 8, CELLS)
            old = top_ref[place]
            new = jnp.maximum(old, jnp.max(e, axis=0))
            total = jnp.sum(jnp.exp2(e - new[None]), axis=0)
            sum_ref[place] = sum_ref[place] * jnp.exp2(old - new) + total
            top_ref[place] = new
        return carry

    lax.fori_loop(0, (count + GROUP - 1) // GROUP, step, 0)


def finish(top_ref, sum_ref):
    tops, sums = top_ref[0 : 4 * CL], sum_ref[0 : 4 * CL]
    top = jnp.max(tops, axis=1, keepdims=True)
    total = jnp.sum(sums * jnp.exp2(tops - top), axis=1)
    return logsum(top[:, 0, :], total)


def row_kernel(codes, owners, s0, s1, s2, s3, t0, t1, t2, t3, out, list_ref, xn, yn, yt, top, tot):
    one = jnp.ones((1, CELLS), f32)
    ones = (one, one, one)
    for k, ref in enumerate((s0, s1, s2, s3)):
        for a in range(CL):
            head, tail, _, square = load_cluster(ref, a)

            def put(at, v, n=k * CL + a):
                xn[n, at : at + v.shape[0], :] = v

            weight = three_parts(-square * SCALE)
            store_operand(put, head * (2.0 * SCALE), tail * (2.0 * SCALE), 0, weight, ones)
    xn[4 * CL] = jnp.zeros((DEPTH, CELLS), bf16)
    for k, ref in enumerate((t0, t1, t2, t3)):
        for a in range(CL):
            head, tail, prior, square = load_cluster(ref, a)

            def put(at, v):
                yn[at : at + v.shape[0], :] = v

            weight = three_parts((prior - square) * SCALE)
            store_operand(put, head, tail, 1, ones, weight)
            yt[k * CL + a] = yn[...].T
    count = jnp.int32(0)
    for k in range(4):
        for d in range(NX):
            for t in range(4):
                code = codes[k * NX + d, owners[t]]
                source = k * CL + (code >> 2)
                list_ref[count] = source * 256 + t * CL + (code & 3)
                count = count + (code >= 0).astype(jnp.int32)
    for k in range(GROUP):
        list_ref[count + k] = 4 * CL * 256
    list_ref[LIST - 1] = count
    top[...] = jnp.full(top.shape, NEGATIVE, f32)
    tot[...] = jnp.zeros(tot.shape, f32)
    over_pairs(count, list_ref, yt, xn, lambda s, t: (t, s, s), top, tot)
    out[...] = finish(top, tot)


def column_kernel(list_ref, m0, m1, m2, m3, s0, s1, s2, s3, t0, t1, t2, t3, out, potential, xn, xt, yn, top, tot):
    one = jnp.ones((1, CELLS), f32)
    ones = (one, one, one)
    came = (m0, m1, m2, m3)
    for k, ref in enumerate((s0, s1, s2, s3)):
        for a in range(CL):
            head, tail, mass, square = load_cluster(ref, a)
            rows = [came[d][((k - d) % 4) * CL + a : ((k - d) % 4) * CL + a + 1, :] for d in range(4)]
            p = EPSILON * mass - (EPSILON * LN2) * merged(rows)
            if k == 0:
                potential[a : a + 1, :] = p

            def put(at, v):
                xn[at : at + v.shape[0], :] = v

            weight = three_parts((p - square) * SCALE)
            store_operand(put, head * (2.0 * SCALE), tail * (2.0 * SCALE), 0, weight, ones)
            xt[k * CL + a] = xn[...].T
    for k, ref in enumerate((t0, t1, t2, t3)):
        for a in range(CL):
            head, tail, _, square = load_cluster(ref, a)

            def put(at, v, n=k * CL + a):
                yn[n, at : at + v.shape[0], :] = v

            weight = three_parts(-square * SCALE)
            store_operand(put, head, tail, 1, ones, weight)
    xt[4 * CL] = jnp.zeros((CELLS, DEPTH), bf16)
    top[...] = jnp.full(top.shape, NEGATIVE, f32)
    tot[...] = jnp.zeros(tot.shape, f32)

    def pick(s, t):
        return s, t, jnp.where(s == 4 * CL, 4 * CL, t)

    over_pairs(list_ref[LIST - 1], list_ref, xt, yn, pick, top, tot)
    out[...] = finish(top, tot)


VMEM = pl.BlockSpec(memory_space=pltpu.VMEM)
SMEM = pl.BlockSpec(memory_space=pltpu.SMEM)


def body(source_coords, target_coords, source_logmass, target_logmass, target_prior, pair_source, pair_target):
    x = lax.axis_index("split")
    own = lax.axis_index("own")
    y, z, c = own // (NZ * NC), (own // NC) % NZ, own % NC
    shifts = jnp.array((Z_FIRST, Z_SECOND), jnp.int32)[:, x]
    near = y * (NZ * NC) + ((z + shifts) % NZ) * NC
    owners = jnp.stack([near + c, near + (1 - c)], axis=1).reshape(4).astype(jnp.int32)

    codes = pair_source * 4 + pair_target
    codes = jnp.where(pair_target >= 0, codes, -1).reshape(1, -1)
    codes = jnp.concatenate([codes] + [from_x(codes, k) for k in (1, 2, 3)], axis=0)
    codes = jnp.concatenate([codes] + [from_y(codes, k) for k in (1, 2, 3)], axis=0)

    def packed(coords, extra):
        zeros = jnp.zeros((CL, 5, CELLS), f32)
        return jnp.concatenate([coords, extra[:, None, :], zeros], axis=1)

    s0 = packed(source_coords, source_logmass)
    t = packed(target_coords, target_prior)
    t0 = fetched(t, lambda x, y, z, c: (x, y, z + Z_FIRST[x], c))
    t2 = fetched(t, lambda x, y, z, c: (x, y, z + Z_SECOND[x], c))
    s1, s2, s3 = (from_y(s0, k) for k in (1, 2, 3))
    t1, t3 = from_core(t0), from_core(t2)
    shards = (s0, s1, s2, s3, t0, t1, t2, t3)

    accumulators = [pltpu.VMEM((4 * CL + 1, 8, CELLS), f32)] * 2
    params = pltpu.CompilerParams(vmem_limit_bytes=56 * 2**20)
    rows, pairs = pl.pallas_call(
        row_kernel,
        out_shape=(
            jax.ShapeDtypeStruct((4 * CL, CELLS), f32),
            jax.ShapeDtypeStruct((LIST,), jnp.int32),
        ),
        in_specs=[SMEM, SMEM] + [VMEM] * 8,
        out_specs=(VMEM, SMEM),
        scratch_shapes=[
            pltpu.VMEM((4 * CL + 1, DEPTH, CELLS), bf16),
            pltpu.VMEM((DEPTH, CELLS), bf16),
            pltpu.VMEM((4 * CL, CELLS, DEPTH), bf16),
        ]
        + accumulators,
        compiler_params=params,
        name="rows",
    )(codes, owners, *shards)

    rows = merged([rows] + [from_x(rows, k) for k in (1, 2, 3)])
    others = [from_y(rows, k) for k in (1, 2, 3)]

    columns, source_potential = pl.pallas_call(
        column_kernel,
        out_shape=(
            jax.ShapeDtypeStruct((4 * CL, CELLS), f32),
            jax.ShapeDtypeStruct((CL, CELLS), f32),
        ),
        in_specs=[SMEM] + [VMEM] * 12,
        out_specs=(VMEM, VMEM),
        scratch_shapes=[
            pltpu.VMEM((DEPTH, CELLS), bf16),
            pltpu.VMEM((4 * CL + 1, CELLS, DEPTH), bf16),
            pltpu.VMEM((4 * CL, DEPTH, CELLS), bf16),
        ]
        + accumulators,
        compiler_params=params,
        name="columns",
    )(pairs, rows, *others, *shards)

    columns = columns.reshape(2, 2, CL, CELLS)
    kept = merged([columns[:, 0], from_core(columns[:, 1])])
    first = fetched(kept[0], lambda x, y, z, c: (x, y, z - Z_FIRST[x], c))
    second = fetched(kept[1], lambda x, y, z, c: (x, y, z - Z_SECOND[x], c))
    part = merged([first, second])
    part = merged([part] + [from_x(part, k) for k in (1, 2, 3)])
    target_potential = EPSILON * target_logmass - (EPSILON * LN2) * part
    return source_potential, target_potential


def solution(mesh):
    return jax.shard_map(
        body,
        mesh=mesh,
        in_specs=(
            P("own", None, None),
            P("own", None, None),
            P("own", None),
            P("own", None),
            P("own", None),
            P("own", "split", None, None),
            P("own", "split", None, None),
        ),
        out_specs=(P("own", None), P("own", None)),
        check_vma=False,
    )
```

time: 269 us -> 95.4 us (0.35)
  blocking collectives: 55.3 us -> 0 us
  local copies, waits for them, and re-layouts: 53.8 us -> 6.45 us
  matrix products: 40.8 us -> 0 us
  waiting for transfers between devices: 59.7 us -> 22.2 us
  starting transfers between devices: 9.31 us -> 44.6 us
  other arithmetic: 32.4 us -> 1.7 us
  Pallas kernels: 0 us -> 19 us
  between operations: 14.9 us -> 0.9 us
    gather x42 -> x0, local copies, waits for them, and re-layouts: 49.6 us -> none  [the longest x8 13 us: row_round(): pair_cost = pair_costs(source_coords[anchor], blocks[chosen])]
    all_gather x1 -> x0, blocking collectives: 45.8 us -> none  [body(): lax.all_gather(target_prior, 'own', axis=0, tiled=True)]
    ppermute x0 -> x25, starting transfers between devices: none -> 44.6 us  [fetched(): return lax.ppermute(value, AXES, pairs)]
    all_gather x1 -> x0, waiting for transfers between devices: 44.4 us -> none  [body(): lax.all_gather(target_coords, 'own', axis=0, tiled=True)]
    dot_general x8 -> x0, matrix products: 40.8 us -> none  [pair_costs(): jnp.einsum('bpi,bpj->bij', left_part, right_part, precision=lax.Precision...]
    ppermute x0 -> x25, waiting for transfers between devices: none -> 22.2 us  [fetched(): return lax.ppermute(value, AXES, pairs)]
    pallas_call x0 -> x2, Pallas kernels: none -> 19 us  [the longest x1 9.52 us: body(): pl.pallas_call(column_kernel, out_shape=(jax.ShapeDtypeStruct((4 * CL, CE...]
    reduce_sum x21 -> x0, other arithmetic: 18.5 us -> none  [the longest x4 8.21 us: column_round(): weights = jnp.sum(jnp.exp(exponent - summit[:, None, :]), axis=1)]
  transfers between devices with their start and end apart: 3 -> 25, of which waited for: 3 -> 14; matrix products, arithmetic and copies ran while one was open for 2% -> 2% of each run, Pallas kernels for 0% -> 0%
where the time goes in v1:
time: 95.4 us; the launch traced here: 94.9 us
  starting transfers between devices  44.6 us (47%)
  waiting for transfers between devices  22.2 us (23%)
  Pallas kernels  19 us (20%)
  local copies, waits for them, and re-layouts  6.45 us (7%)
  other arithmetic  1.7 us (2%)
    ppermute x25, starting transfers between devices, fetched(): return lax.ppermute(value, AXES, pairs)  44.6 us
    ppermute x25, waiting for transfers between devices, fetched(): return lax.ppermute(value, AXES, pairs)  22.2 us
    pallas_call x1, Pallas kernels, body(): pl.pallas_call(column_kernel, out_shape=(jax.ShapeDtypeStruct((4 * CL, CE...  9.52 us
    pallas_call x1, Pallas kernels, body(): pl.pallas_call(row_kernel, out_shape=(jax.ShapeDtypeStruct((4 * CL, CELLS...  9.5 us
    unnamed x38, local copies, waits for them, and re-layouts  3.13 us
  transfers between devices with their start and end apart: 25, of which 14 were waited for; matrix products, arithmetic and copies ran while one was open for 2% of the time, Pallas kernels for 0%

profile of v1, /device:TPU:64, one launch (start us, length us, event | category | flops | bytes accessed | tf_op | source)
XLA Modules:
  0.0 94.9 jit_solution(17559126179795304352)
XLA Ops:
  1.4 1.0 %copy.10 = f32[4,50,256]{2,1,0:T(8,128)S(1)} copy(f32[4,50,256]{2,0,1:T(4,128)} %param.8) | data formatting | bytes 409600 | tf_op args[0]
  2.7 5.5 %collective-permute-start.11 = (f32[4,56,256]{2,1,0:T(8,128)S(1)}, f32[4,56,256]{2,1,0:T(8,128)S(1)}, u32[]{:S(2)}, u32[]{:S(2)}) collective-permute-start(f32[4,56,256]{2,1,0:T(8,128)S(1)} %get-tuple-element.14), channel_id=1, source_target_pairs={{32,0},{57,1},{50,2},{43,3},{36,4},{61,5},{54,6},{47,7},{40,8},{1,... | collective-permute-start | bytes 688136 | tf_op jit(solution)/shard_map/ppermute | solution.py:46
  8.9 5.1 %collective-permute-start.1 = (s32[1,64]{1,0:T(1,128)S(1)}, s32[1,64]{1,0:T(1,128)S(1)}, u32[]{:S(2)}, u32[]{:S(2)}) collective-permute-start(s32[1,64]{1,0:T(1,128)S(1)} %fusion.7), channel_id=1, source_target_pairs={{2,0},{3,1},{0,2},{1,3},{6,4},{7,5},{4,6},{5,7},{10,8},{11,9},{8,1... | collective-permute-start | bytes 776 | tf_op jit(solution)/shard_map/ppermute | solution.py:46
  15.6 2.0 %collective-permute-done = s32[1,64]{1,0:T(1,128)S(1)} collective-permute-done((s32[1,64]{1,0:T(1,128)S(1)}, s32[1,64]{1,0:T(1,128)S(1)}, u32[]{:S(2)}, u32[]{:S(2)}) %collective-permute-start) | collective-permute-done | bytes 288 | tf_op jit(solution)/shard_map/ppermute | solution.py:46
  17.6 1.7 %collective-permute-start.5 = (s32[4,64]{1,0:T(4,128)S(1)}, s32[4,64]{1,0:T(4,128)S(1)}, u32[]{:S(2)}, u32[]{:S(2)}) collective-permute-start(s32[4,64]{1,0:T(4,128)S(1)} %pad_add_fusion), channel_id=1, source_target_pairs={{192,0},{193,1},{194,2},{195,3},{196,4},{197,5},{198,6},{199,7},{2... | collective-permute-start | bytes 3080 | tf_op jit(solution)/shard_map/ppermute | solution.py:46
  19.2 2.9 %collective-permute-start.4 = (s32[4,64]{1,0:T(4,128)S(1)}, s32[4,64]{1,0:T(4,128)S(1)}, u32[]{:S(2)}, u32[]{:S(2)}) collective-permute-start(s32[4,64]{1,0:T(4,128)S(1)} %pad_add_fusion), channel_id=1, source_target_pairs={{128,0},{129,1},{130,2},{131,3},{132,4},{133,5},{134,6},{135,7},{1... | collective-permute-start | bytes 3080 | tf_op jit(solution)/shard_map/ppermute | solution.py:46
  22.1 1.3 %collective-permute-start.3 = (s32[4,64]{1,0:T(4,128)S(1)}, s32[4,64]{1,0:T(4,128)S(1)}, u32[]{:S(2)}, u32[]{:S(2)}) collective-permute-start(s32[4,64]{1,0:T(4,128)S(1)} %pad_add_fusion), channel_id=1, source_target_pairs={{64,0},{65,1},{66,2},{67,3},{68,4},{69,5},{70,6},{71,7},{72,8},{73... | collective-permute-start | bytes 3080 | tf_op jit(solution)/shard_map/ppermute | solution.py:46
  24.4 2.9 %collective-permute-start.7 = (f32[4,56,256]{2,1,0:T(8,128)S(1)}, f32[4,56,256]{2,1,0:T(8,128)S(1)}, u32[]{:S(2)}, u32[]{:S(2)}) collective-permute-start(f32[4,56,256]{2,1,0:T(8,128)S(1)} %get-tuple-element.15.s0), channel_id=1, source_target_pairs={{128,0},{129,1},{130,2},{131,3},{132,4},{133,5},{134,6},{135,7},{1... | collective-permute-start | bytes 688136 | tf_op jit(solution)/shard_map/ppermute | solution.py:46
  27.3 1.3 %collective-permute-start.6 = (f32[4,56,256]{2,1,0:T(8,128)S(1)}, f32[4,56,256]{2,1,0:T(8,128)S(1)}, u32[]{:S(2)}, u32[]{:S(2)}) collective-permute-start(f32[4,56,256]{2,1,0:T(8,128)S(1)} %get-tuple-element.15.s0), channel_id=1, source_target_pairs={{64,0},{65,1},{66,2},{67,3},{68,4},{69,5},{70,6},{71,7},{72,8},{73... | collective-permute-start | bytes 688136 | tf_op jit(solution)/shard_map/ppermute | solution.py:46
  29.8 1.2 %concatenate.14.codes = s32[16,64]{1,0:T(8,128)} concatenate(s32[1,64]{1,0:T(1,128)S(1)} %fusion.7, s32[1,64]{1,0:T(1,128)S(1)} %collective-permute-done, s32[1,64]{1,0:T(1,128)S(1)} %collective-permute-done.1, s32[1,64]{1,0:T(1,128)S(1)} %collective-permute-done.2, s32[4,64]{1,0:T(4,128)S(1)} %collective-permute-done.3, s32[4,64]{1,0:T(4,128)S(1)} %collective-permute-done.4, ...), dimensions={0} | concatenate | bytes 8192 | tf_op jit(solution)/shard_map/concatenate | solution.py:226
  31.0 3.5 %collective-permute-done.8.s3 = f32[4,56,256]{2,1,0:T(8,128)S(1)} collective-permute-done((f32[4,56,256]{2,1,0:T(8,128)S(1)}, f32[4,56,256]{2,1,0:T(8,128)S(1)}, u32[]{:S(2)}, u32[]{:S(2)}) %collective-permute-start.8) | collective-permute-done | bytes 229408 | tf_op jit(solution)/shard_map/ppermute | solution.py:46
  36.7 9.5 %rows.1 = (f32[16,256]{1,0:T(8,128)}, s32[72]{0:T(128)}) custom-call(s32[16,64]{1,0:T(8,128)} %concatenate.14.codes, s32[4]{0:T(128)} %reshape.14.owners, f32[4,56,256]{2,1,0:T(8,128)} %copy-done, f32[4,56,256]{2,1,0:T(8,128)} %copy-done.5, f32[4,56,256]{2,1,0:T(8,128)} %copy-done.4, f32[4,56,256]{2,1,0:T(8,128)} %copy-done.3, f32[4,56,256]{2,1,0:T(8,128)} %copy-done.2, ...), custom_call_target="tpu_custom_call" | custom-call | tf_op jit(solution)/shard_map/rows/pallas_call | solution.py:242
  46.3 4.4 %collective-permute-start.14 = (f32[16,256]{1,0:T(8,128)}, f32[16,256]{1,0:T(8,128)S(1)}, u32[]{:S(2)}, u32[]{:S(2)}) collective-permute-start(f32[16,256]{1,0:T(8,128)} %get-tuple-element.7), channel_id=1, source_target_pairs={{2,0},{3,1},{0,2},{1,3},{6,4},{7,5},{4,6},{5,7},{10,8},{11,9},{8,1... | collective-permute-start | bytes 49160 | tf_op jit(solution)/shard_map/ppermute | solution.py:46
  51.4 1.3 %collective-permute-done.14 = f32[16,256]{1,0:T(8,128)S(1)} collective-permute-done((f32[16,256]{1,0:T(8,128)}, f32[16,256]{1,0:T(8,128)S(1)}, u32[]{:S(2)}, u32[]{:S(2)}) %collective-permute-start.14) | collective-permute-done | bytes 16416 | tf_op jit(solution)/shard_map/ppermute | solution.py:46
  52.8 1.9 %collective-permute-done.13 = f32[16,256]{1,0:T(8,128)S(1)} collective-permute-done((f32[16,256]{1,0:T(8,128)}, f32[16,256]{1,0:T(8,128)S(1)}, u32[]{:S(2)}, u32[]{:S(2)}) %collective-permute-start.13) | collective-permute-done | bytes 16416 | tf_op jit(solution)/shard_map/ppermute | solution.py:46
  55.9 3.7 %collective-permute-start.17 = (f32[16,256]{1,0:T(8,128)S(1)}, f32[16,256]{1,0:T(8,128)S(1)}, u32[]{:S(2)}, u32[]{:S(2)}) collective-permute-start(f32[16,256]{1,0:T(8,128)S(1)} %multiply_add_fusion.m0), channel_id=1, source_target_pairs={{128,0},{129,1},{130,2},{131,3},{132,4},{133,5},{134,6},{135,7},{1... | collective-permute-start | bytes 49160 | tf_op jit(solution)/shard_map/ppermute | solution.py:46
  60.4 1.0 %collective-permute-done.17.m2 = f32[16,256]{1,0:T(8,128)S(1)} collective-permute-done((f32[16,256]{1,0:T(8,128)S(1)}, f32[16,256]{1,0:T(8,128)S(1)}, u32[]{:S(2)}, u32[]{:S(2)}) %collective-permute-start.17) | collective-permute-done | bytes 16416 | tf_op jit(solution)/shard_map/ppermute | solution.py:46
  61.4 1.8 %collective-permute-done.16.m1 = f32[16,256]{1,0:T(8,128)S(1)} collective-permute-done((f32[16,256]{1,0:T(8,128)S(1)}, f32[16,256]{1,0:T(8,128)S(1)}, u32[]{:S(2)}, u32[]{:S(2)}) %collective-permute-start.16) | collective-permute-done | bytes 16416 | tf_op jit(solution)/shard_map/ppermute | solution.py:46
  63.9 9.5 %columns.1 = (f32[16,256]{1,0:T(8,128)}, f32[4,256]{1,0:T(4,128)}) custom-call(s32[72]{0:T(128)} %get-tuple-element.6.list_ref, f32[16,256]{1,0:T(8,128)} %copy-done.9, f32[16,256]{1,0:T(8,128)} %copy-done.12, f32[16,256]{1,0:T(8,128)} %copy-done.11, f32[16,256]{1,0:T(8,128)} %copy-done.10, f32[4,56,256]{2,1,0:T(8,128)} %copy-done, f32[4,56,256]{2,1,0:T(8,128)} %copy-done.5, ...), custom_call_target="tpu_custom_call" | custom-call | tf_op jit(solution)/shard_map/columns/pallas_call | solution.py:263
  76.0 3.5 %collective-permute-start.21 = (f32[4,256]{1,0:T(4,128)S(1)}, f32[4,256]{1,0:T(4,128)S(1)}, u32[]{:S(2)}, u32[]{:S(2)}) collective-permute-start(f32[4,256]{1,0:T(4,128)S(1)} %get-tuple-element.13), channel_id=1, source_target_pairs={{32,0},{9,1},{18,2},{27,3},{36,4},{13,5},{22,6},{31,7},{40,8},{17,... | collective-permute-start | bytes 12296 | tf_op jit(solution)/shard_map/ppermute | solution.py:46
  79.5 4.1 %collective-permute-done.21 = f32[4,256]{1,0:T(4,128)S(1)} collective-permute-done((f32[4,256]{1,0:T(4,128)S(1)}, f32[4,256]{1,0:T(4,128)S(1)}, u32[]{:S(2)}, u32[]{:S(2)}) %collective-permute-start.21) | collective-permute-done | bytes 4128 | tf_op jit(solution)/shard_map/ppermute | solution.py:46
  83.7 7.0 %collective-permute-start.23 = (f32[4,256]{1,0:T(4,128)S(1)}, f32[4,256]{1,0:T(4,128)S(1)}, u32[]{:S(2)}, u32[]{:S(2)}) collective-permute-start(f32[4,256]{1,0:T(4,128)S(1)} %multiply_add_fusion.2), channel_id=1, source_target_pairs={{2,0},{3,1},{0,2},{1,3},{6,4},{7,5},{4,6},{5,7},{10,8},{11,9},{8,1... | collective-permute-start | bytes 12296 | tf_op jit(solution)/shard_map/ppermute | solution.py:46
  90.8 1.5 %collective-permute-done.23 = f32[4,256]{1,0:T(4,128)S(1)} collective-permute-done((f32[4,256]{1,0:T(4,128)S(1)}, f32[4,256]{1,0:T(4,128)S(1)}, u32[]{:S(2)}, u32[]{:S(2)}) %collective-permute-start.23) | collective-permute-done | bytes 4128 | tf_op jit(solution)/shard_map/ppermute | solution.py:46
  92.3 2.0 %collective-permute-done.22 = f32[4,256]{1,0:T(4,128)S(1)} collective-permute-done((f32[4,256]{1,0:T(4,128)S(1)}, f32[4,256]{1,0:T(4,128)S(1)}, u32[]{:S(2)}, u32[]{:S(2)}) %collective-permute-start.22) | collective-permute-done | bytes 4128 | tf_op jit(solution)/shard_map/ppermute | solution.py:46
  (85 shorter events, 14.4 us)
Async XLA Ops:
  2.7 25.9 %collective-permute-start.11 = (f32[4,56,256]{2,1,0:T(8,128)S(1)}, f32[4,56,256]{2,1,0:T(8,128)S(1)}, u32[]{:S(2)}, u32[]{:S(2)}) collective-permute-start(f32[4,56,256]{2,1,0:T(8,128)S(1)} %get-tuple-element.14), channel_id=1, source_target_pairs={{32,0},{57,1},{50,2},{43,3},{36,4},{61,5},{54,6},{47,7},{40,8},{1,... | collective-permute-start | bytes 688136 | tf_op jit(solution)/shard_map/ppermute | solution.py:46
  8.1 20.5 %collective-permute-start.9 = (f32[4,56,256]{2,1,0:T(8,128)S(1)}, f32[4,56,256]{2,1,0:T(8,128)S(1)}, u32[]{:S(2)}, u32[]{:S(2)}) collective-permute-start(f32[4,56,256]{2,1,0:T(8,128)S(1)} %get-tuple-element.14), channel_id=1, source_target_pairs={{0,0},{9,1},{18,2},{27,3},{4,4},{13,5},{22,6},{31,7},{8,8},{17,9},... | collective-permute-start | bytes 688136 | tf_op jit(solution)/shard_map/ppermute | solution.py:46
  8.8 6.1 %collective-permute-start.2 = (s32[1,64]{1,0:T(1,128)S(1)}, s32[1,64]{1,0:T(1,128)S(1)}, u32[]{:S(2)}, u32[]{:S(2)}) collective-permute-start(s32[1,64]{1,0:T(1,128)S(1)} %fusion.7), channel_id=1, source_target_pairs={{3,0},{0,1},{1,2},{2,3},{7,4},{4,5},{5,6},{6,7},{11,8},{8,9},{9,10... | collective-permute-start | bytes 776 | tf_op jit(solution)/shard_map/ppermute | solution.py:46
  8.9 6.6 %collective-permute-start.1 = (s32[1,64]{1,0:T(1,128)S(1)}, s32[1,64]{1,0:T(1,128)S(1)}, u32[]{:S(2)}, u32[]{:S(2)}) collective-permute-start(s32[1,64]{1,0:T(1,128)S(1)} %fusion.7), channel_id=1, source_target_pairs={{2,0},{3,1},{0,2},{1,3},{6,4},{7,5},{4,6},{5,7},{10,8},{11,9},{8,1... | collective-permute-start | bytes 776 | tf_op jit(solution)/shard_map/ppermute | solution.py:46
  14.0 3.6 %collective-permute-start = (s32[1,64]{1,0:T(1,128)S(1)}, s32[1,64]{1,0:T(1,128)S(1)}, u32[]{:S(2)}, u32[]{:S(2)}) collective-permute-start(s32[1,64]{1,0:T(1,128)S(1)} %fusion.7), channel_id=1, source_target_pairs={{1,0},{2,1},{3,2},{0,3},{5,4},{6,5},{7,6},{4,7},{9,8},{10,9},{11,1... | collective-permute-start | bytes 776 | tf_op jit(solution)/shard_map/ppermute | solution.py:46
  17.6 6.0 %collective-permute-start.5 = (s32[4,64]{1,0:T(4,128)S(1)}, s32[4,64]{1,0:T(4,128)S(1)}, u32[]{:S(2)}, u32[]{:S(2)}) collective-permute-start(s32[4,64]{1,0:T(4,128)S(1)} %pad_add_fusion), channel_id=1, source_target_pairs={{192,0},{193,1},{194,2},{195,3},{196,4},{197,5},{198,6},{199,7},{2... | collective-permute-start | bytes 3080 | tf_op jit(solution)/shard_map/ppermute | solution.py:46
  19.2 5.1 %collective-permute-start.4 = (s32[4,64]{1,0:T(4,128)S(1)}, s32[4,64]{1,0:T(4,128)S(1)}, u32[]{:S(2)}, u32[]{:S(2)}) collective-permute-start(s32[4,64]{1,0:T(4,128)S(1)} %pad_add_fusion), channel_id=1, source_target_pairs={{128,0},{129,1},{130,2},{131,3},{132,4},{133,5},{134,6},{135,7},{1... | collective-permute-start | bytes 3080 | tf_op jit(solution)/shard_map/ppermute | solution.py:46
  22.1 5.1 %collective-permute-start.3 = (s32[4,64]{1,0:T(4,128)S(1)}, s32[4,64]{1,0:T(4,128)S(1)}, u32[]{:S(2)}, u32[]{:S(2)}) collective-permute-start(s32[4,64]{1,0:T(4,128)S(1)} %pad_add_fusion), channel_id=1, source_target_pairs={{64,0},{65,1},{66,2},{67,3},{68,4},{69,5},{70,6},{71,7},{72,8},{73... | collective-permute-start | bytes 3080 | tf_op jit(solution)/shard_map/ppermute | solution.py:46
  23.6 10.9 %collective-permute-start.8 = (f32[4,56,256]{2,1,0:T(8,128)S(1)}, f32[4,56,256]{2,1,0:T(8,128)S(1)}, u32[]{:S(2)}, u32[]{:S(2)}) collective-permute-start(f32[4,56,256]{2,1,0:T(8,128)S(1)} %get-tuple-element.15.s0), channel_id=1, source_target_pairs={{192,0},{193,1},{194,2},{195,3},{196,4},{197,5},{198,6},{199,7},{2... | collective-permute-start | bytes 688136 | tf_op jit(solution)/shard_map/ppermute | solution.py:46
  24.4 10.2 %collective-permute-start.7 = (f32[4,56,256]{2,1,0:T(8,128)S(1)}, f32[4,56,256]{2,1,0:T(8,128)S(1)}, u32[]{:S(2)}, u32[]{:S(2)}) collective-permute-start(f32[4,56,256]{2,1,0:T(8,128)S(1)} %get-tuple-element.15.s0), channel_id=1, source_target_pairs={{128,0},{129,1},{130,2},{131,3},{132,4},{133,5},{134,6},{135,7},{1... | collective-permute-start | bytes 688136 | tf_op jit(solution)/shard_map/ppermute | solution.py:46
  27.3 7.9 %collective-permute-start.6 = (f32[4,56,256]{2,1,0:T(8,128)S(1)}, f32[4,56,256]{2,1,0:T(8,128)S(1)}, u32[]{:S(2)}, u32[]{:S(2)}) collective-permute-start(f32[4,56,256]{2,1,0:T(8,128)S(1)} %get-tuple-element.15.s0), channel_id=1, source_target_pairs={{64,0},{65,1},{66,2},{67,3},{68,4},{69,5},{70,6},{71,7},{72,8},{73... | collective-permute-start | bytes 688136 | tf_op jit(solution)/shard_map/ppermute | solution.py:46
  28.6 6.6 %collective-permute-start.12 = (f32[4,56,256]{2,1,0:T(8,128)S(1)}, f32[4,56,256]{2,1,0:T(8,128)S(1)}, u32[]{:S(2)}, u32[]{:S(2)}) collective-permute-start(f32[4,56,256]{2,1,0:T(8,128)S(1)} %collective-permute-done.11.t2), channel_id=1, source_target_pairs={{4,0},{5,1},{6,2},{7,3},{0,4},{1,5},{2,6},{3,7},{12,8},{13,9},{14,... | collective-permute-start | bytes 688136 | tf_op jit(solution)/shard_map/ppermute | solution.py:46
  28.6 6.6 %collective-permute-start.10 = (f32[4,56,256]{2,1,0:T(8,128)S(1)}, f32[4,56,256]{2,1,0:T(8,128)S(1)}, u32[]{:S(2)}, u32[]{:S(2)}) collective-permute-start(f32[4,56,256]{2,1,0:T(8,128)S(1)} %collective-permute-done.9.t0), channel_id=1, source_target_pairs={{4,0},{5,1},{6,2},{7,3},{0,4},{1,5},{2,6},{3,7},{12,8},{13,9},{14,... | collective-permute-start | bytes 688136 | tf_op jit(solution)/shard_map/ppermute | solution.py:46
  46.2 5.2 %collective-permute-start.15 = (f32[16,256]{1,0:T(8,128)}, f32[16,256]{1,0:T(8,128)S(1)}, u32[]{:S(2)}, u32[]{:S(2)}) collective-permute-start(f32[16,256]{1,0:T(8,128)} %get-tuple-element.7), channel_id=1, source_target_pairs={{3,0},{0,1},{1,2},{2,3},{7,4},{4,5},{5,6},{6,7},{11,8},{8,9},{9,10... | collective-permute-start | bytes 49160 | tf_op jit(solution)/shard_map/ppermute | solution.py:46
  46.3 6.5 %collective-permute-start.14 = (f32[16,256]{1,0:T(8,128)}, f32[16,256]{1,0:T(8,128)S(1)}, u32[]{:S(2)}, u32[]{:S(2)}) collective-permute-start(f32[16,256]{1,0:T(8,128)} %get-tuple-element.7), channel_id=1, source_target_pairs={{2,0},{3,1},{0,2},{1,3},{6,4},{7,5},{4,6},{5,7},{10,8},{11,9},{8,1... | collective-permute-start | bytes 49160 | tf_op jit(solution)/shard_map/ppermute | solution.py:46
  50.7 4.0 %collective-permute-start.13 = (f32[16,256]{1,0:T(8,128)}, f32[16,256]{1,0:T(8,128)S(1)}, u32[]{:S(2)}, u32[]{:S(2)}) collective-permute-start(f32[16,256]{1,0:T(8,128)} %get-tuple-element.7), channel_id=1, source_target_pairs={{1,0},{2,1},{3,2},{0,3},{5,4},{6,5},{7,6},{4,7},{9,8},{10,9},{11,1... | collective-permute-start | bytes 49160 | tf_op jit(solution)/shard_map/ppermute | solution.py:46
  55.4 5.0 %collective-permute-start.18 = (f32[16,256]{1,0:T(8,128)S(1)}, f32[16,256]{1,0:T(8,128)S(1)}, u32[]{:S(2)}, u32[]{:S(2)}) collective-permute-start(f32[16,256]{1,0:T(8,128)S(1)} %multiply_add_fusion.m0), channel_id=1, source_target_pairs={{192,0},{193,1},{194,2},{195,3},{196,4},{197,5},{198,6},{199,7},{2... | collective-permute-start | bytes 49160 | tf_op jit(solution)/shard_map/ppermute | solution.py:46
  55.9 5.6 %collective-permute-start.17 = (f32[16,256]{1,0:T(8,128)S(1)}, f32[16,256]{1,0:T(8,128)S(1)}, u32[]{:S(2)}, u32[]{:S(2)}) collective-permute-start(f32[16,256]{1,0:T(8,128)S(1)} %multiply_add_fusion.m0), channel_id=1, source_target_pairs={{128,0},{129,1},{130,2},{131,3},{132,4},{133,5},{134,6},{135,7},{1... | collective-permute-start | bytes 49160 | tf_op jit(solution)/shard_map/ppermute | solution.py:46
  59.5 3.7 %collective-permute-start.16 = (f32[16,256]{1,0:T(8,128)S(1)}, f32[16,256]{1,0:T(8,128)S(1)}, u32[]{:S(2)}, u32[]{:S(2)}) collective-permute-start(f32[16,256]{1,0:T(8,128)S(1)} %multiply_add_fusion.m0), channel_id=1, source_target_pairs={{64,0},{65,1},{66,2},{67,3},{68,4},{69,5},{70,6},{71,7},{72,8},{73... | collective-permute-start | bytes 49160 | tf_op jit(solution)/shard_map/ppermute | solution.py:46
  75.3 4.2 %collective-permute-start.20 = (f32[4,256]{1,0:T(4,128)S(1)}, f32[4,256]{1,0:T(4,128)S(1)}, u32[]{:S(2)}, u32[]{:S(2)}) collective-permute-start(f32[4,256]{1,0:T(4,128)S(1)} %get-tuple-element.12), channel_id=1, source_target_pairs={{0,0},{57,1},{50,2},{43,3},{4,4},{61,5},{54,6},{47,7},{8,8},{1,9},... | collective-permute-start | bytes 12296 | tf_op jit(solution)/shard_map/ppermute | solution.py:46
  76.0 7.6 %collective-permute-start.21 = (f32[4,256]{1,0:T(4,128)S(1)}, f32[4,256]{1,0:T(4,128)S(1)}, u32[]{:S(2)}, u32[]{:S(2)}) collective-permute-start(f32[4,256]{1,0:T(4,128)S(1)} %get-tuple-element.13), channel_id=1, source_target_pairs={{32,0},{9,1},{18,2},{27,3},{36,4},{13,5},{22,6},{31,7},{40,8},{17,... | collective-permute-start | bytes 12296 | tf_op jit(solution)/shard_map/ppermute | solution.py:46
  83.6 7.2 %collective-permute-start.24 = (f32[4,256]{1,0:T(4,128)S(1)}, f32[4,256]{1,0:T(4,128)S(1)}, u32[]{:S(2)}, u32[]{:S(2)}) collective-permute-start(f32[4,256]{1,0:T(4,128)S(1)} %multiply_add_fusion.2), channel_id=1, source_target_pairs={{3,0},{0,1},{1,2},{2,3},{7,4},{4,5},{5,6},{6,7},{11,8},{8,9},{9,10... | collective-permute-start | bytes 12296 | tf_op jit(solution)/shard_map/ppermute | solution.py:46
  83.7 8.6 %collective-permute-start.23 = (f32[4,256]{1,0:T(4,128)S(1)}, f32[4,256]{1,0:T(4,128)S(1)}, u32[]{:S(2)}, u32[]{:S(2)}) collective-permute-start(f32[4,256]{1,0:T(4,128)S(1)} %multiply_add_fusion.2), channel_id=1, source_target_pairs={{2,0},{3,1},{0,2},{1,3},{6,4},{7,5},{4,6},{5,7},{10,8},{11,9},{8,1... | collective-permute-start | bytes 12296 | tf_op jit(solution)/shard_map/ppermute | solution.py:46
  90.7 3.6 %collective-permute-start.22 = (f32[4,256]{1,0:T(4,128)S(1)}, f32[4,256]{1,0:T(4,128)S(1)}, u32[]{:S(2)}, u32[]{:S(2)}) collective-permute-start(f32[4,256]{1,0:T(4,128)S(1)} %multiply_add_fusion.2), channel_id=1, source_target_pairs={{1,0},{2,1},{3,2},{0,3},{5,4},{6,5},{7,6},{4,7},{9,8},{10,9},{11,1... | collective-permute-start | bytes 12296 | tf_op jit(solution)/shard_map/ppermute | solution.py:46
  (19 other events, 104.8 us)

commit v2 on v1

v2 whole, which is shorter than its diff:
```python
import math

import jax
import jax.numpy as jnp
from jax import lax
from jax.experimental import pallas as pl
from jax.experimental.pallas import tpu as pltpu
from jax.sharding import PartitionSpec as P


EPSILON = 0.5
NEGATIVE = -1e30
LN2 = math.log(2.0)
SCALE = 1.0 / (EPSILON * LN2)

CL = 4
CELLS = 256
NY, NZ, NC, NX = 4, 8, 2, 4
AXES = ("own", "split")

FAR = NZ // 2

BLOCK = 64
PRODUCTS = ((0, 0), (0, 1), (1, 0), (1, 1))
DEPTH = BLOCK * len(PRODUCTS)
SLOTS = 64
LIST = SLOTS + 8

f32, bf16 = jnp.float32, jnp.bfloat16


def device(x, y, z, c):
    return (((y % NY) * NZ + z % NZ) * NC + c % NC) * NX + x % NX


def fetched(value, source):
    pairs = [
        (device(*source(x, y, z, c)), device(x, y, z, c))
        for y in range(NY)
        for z in range(NZ)
        for c in range(NC)
        for x in range(NX)
    ]
    return lax.ppermute(value, AXES, pairs)


def from_x(value, k):
    return fetched(value, lambda x, y, z, c: (x + k, y, z, c))


def from_y(value, k):
    return fetched(value, lambda x, y, z, c: (x, y + k, z, c))


def from_core(value):
    return fetched(value, lambda x, y, z, c: (x, y, z, c + 1))


def three_parts(v):
    high = v.astype(bf16).astype(f32)
    rest = v - high
    middle = rest.astype(bf16).astype(f32)
    return high, middle, rest - middle


def target_owners():
    own, x = lax.axis_index("own"), lax.axis_index("split")
    row, z, c = (own // (NZ * NC)) * (NZ * NC), (own // NC) % NZ, own % NC
    near = row + ((z + x) % NZ) * NC
    far = row + ((z + x + NZ // 2) % NZ) * NC
    return near + c, near + 1 - c, far + c, far + 1 - c


def centre(ref):
    middle = jnp.mean(ref[0], axis=1, keepdims=True)
    return jnp.broadcast_to(middle, (56, CELLS))


def load_cluster(ref, a, middle):
    top = ref[a, 0:48, :] - middle[0:48]
    tail = ref[a, 48:56, :]
    row = lax.broadcasted_iota(jnp.int32, (8, CELLS), 0)
    extra = tail[2:3, :]
    tail = jnp.where(row < 2, tail - middle[48:56], 0.0)
    square = jnp.sum(top * top, axis=0, keepdims=True) + jnp.sum(tail * tail, axis=0, keepdims=True)
    return top, tail, extra, square


def with_rows(tail, first, second):
    row = lax.broadcasted_iota(jnp.int32, (8, CELLS), 0)
    for k in range(3):
        tail = jnp.where(row == 2 + k, first[k], tail)
        tail = jnp.where(row == 5 + k, second[k], tail)
    return tail


def store_operand(put, top, tail, side, first, second):
    tops, tails = three_parts(top), three_parts(tail)
    zeros = jnp.zeros((8, CELLS), f32)
    for n, product in enumerate(PRODUCTS):
        part = product[side]
        end = with_rows(tails[part], first, second) if n == 0 else tails[part]
        put(n * BLOCK, tops[part].astype(bf16))
        put(n * BLOCK + 48, jnp.concatenate([end, zeros], axis=0).astype(bf16))


def logsum(top, total):
    return jnp.where(total > 0.0, top + jnp.log2(total), NEGATIVE)


def merged(parts):
    top = parts[0]
    for part in parts[1:]:
        top = jnp.maximum(top, part)
    total = sum(jnp.exp2(part - top) for part in parts)
    return top + jnp.log2(total)


def over_pairs(count, list_ref, left_ref, right_ref, pick, top_ref, sum_ref, even, odd):
    def multiply(n, e_ref):
        pair = list_ref[n]
        left, right, _ = pick(pair >> 8, pair & 255)
        e_ref[...] = jnp.dot(left_ref[left], right_ref[right], preferred_element_type=f32)

    def absorb(n, e_ref):
        pair = list_ref[n]
        _, _, place = pick(pair >> 8, pair & 255)
        e = e_ref[...].reshape(CELLS // 8, 8, CELLS)
        top = jnp.max(e, axis=0)
        total = jnp.sum(jnp.exp2(e - top[None]), axis=0)
        old = top_ref[place]
        new = jnp.maximum(old, top)
        sum_ref[place] = sum_ref[place] * jnp.exp2(old - new) + total * jnp.exp2(top - new)
        top_ref[place] = new

    def step(q, carry):
        multiply(2 * q + 1, odd)
        absorb(2 * q, even)
        multiply(2 * q + 2, even)
        absorb(2 * q + 1, odd)
        return carry

    multiply(0, even)
    lax.fori_loop(0, (count + 1) // 2, step, 0)


def finish(top_ref, sum_ref):
    tops, sums = top_ref[0 : 4 * CL], sum_ref[0 : 4 * CL]
    top = jnp.max(tops, axis=1, keepdims=True)
    total = jnp.sum(sums * jnp.exp2(tops - top), axis=1)
    return logsum(top[:, 0, :], total)


def row_kernel(c0, c1, c2, c3, s0, s1, s2, s3, t0, t1, t2, t3, out, list_ref, xn, yn, yt, top, tot, even, odd):
    one = jnp.ones((1, CELLS), f32)
    ones = (one, one, one)
    middle = centre(s0)
    for k, ref in enumerate((s0, s1, s2, s3)):
        for a in range(CL):
            head, tail, _, square = load_cluster(ref, a, middle)

            def put(at, v, n=k * CL + a):
                xn[n, at : at + v.shape[0], :] = v

            weight = three_parts(-square * SCALE)
            store_operand(put, head * (2.0 * SCALE), tail * (2.0 * SCALE), 0, weight, ones)
    xn[4 * CL] = jnp.zeros((DEPTH, CELLS), bf16)
    for k, ref in enumerate((t0, t1, t2, t3)):
        for a in range(CL):
            head, tail, prior, square = load_cluster(ref, a, middle)

            def put(at, v):
                yn[at : at + v.shape[0], :] = v

            weight = three_parts((prior - square) * SCALE)
            store_operand(put, head, tail, 1, ones, weight)
            yt[k * CL + a] = yn[...].T
    owners = target_owners()
    count = jnp.int32(0)
    for k, codes in enumerate((c0, c1, c2, c3)):
        for d in range(NX):
            for t in range(4):
                code = codes[d, owners[t]]
                source = k * CL + (code >> 2)
                list_ref[count] = source * 256 + t * CL + (code & 3)
                count = count + (code >= 0).astype(jnp.int32)
    for k in range(2):
        list_ref[count + k] = 4 * CL * 256
    list_ref[LIST - 1] = count
    top[...] = jnp.full(top.shape, NEGATIVE, f32)
    tot[...] = jnp.zeros(tot.shape, f32)
    over_pairs(count, list_ref, yt, xn, lambda s, t: (t, s, s), top, tot, even, odd)
    out[...] = finish(top, tot)


def column_kernel(list_ref, m0, m1, m2, m3, s0, s1, s2, s3, t0, t1, t2, t3, kept, given, potential, xn, xt, yn, top, tot, even, odd):
    one = jnp.ones((1, CELLS), f32)
    ones = (one, one, one)
    middle = centre(s0)
    came = (m0, m1, m2, m3)
    for k, ref in enumerate((s0, s1, s2, s3)):
        for a in range(CL):
            head, tail, mass, square = load_cluster(ref, a, middle)
            rows = [came[d][((k - d) % 4) * CL + a : ((k - d) % 4) * CL + a + 1, :] for d in range(4)]
            p = EPSILON * mass - (EPSILON * LN2) * merged(rows)
            if k == 0:
                potential[a : a + 1, :] = p

            def put(at, v):
                xn[at : at + v.shape[0], :] = v

            weight = three_parts((p - square) * SCALE)
            store_operand(put, head * (2.0 * SCALE), tail * (2.0 * SCALE), 0, weight, ones)
            xt[k * CL + a] = xn[...].T
    for k, ref in enumerate((t0, t1, t2, t3)):
        for a in range(CL):
            head, tail, _, square = load_cluster(ref, a, middle)

            def put(at, v, n=k * CL + a):
                yn[n, at : at + v.shape[0], :] = v

            weight = three_parts(-square * SCALE)
            store_operand(put, head, tail, 1, ones, weight)
    xt[4 * CL] = jnp.zeros((CELLS, DEPTH), bf16)
    top[...] = jnp.full(top.shape, NEGATIVE, f32)
    tot[...] = jnp.zeros(tot.shape, f32)

    def pick(s, t):
        return s, t, jnp.where(s == 4 * CL, 4 * CL, t)

    over_pairs(list_ref[LIST - 1], list_ref, xt, yn, pick, top, tot, even, odd)
    columns = finish(top, tot)
    for k in range(2):
        kept[k * CL : (k + 1) * CL, :] = columns[2 * k * CL : (2 * k + 1) * CL]
        given[k * CL : (k + 1) * CL, :] = columns[(2 * k + 1) * CL : (2 * k + 2) * CL]


VMEM = pl.BlockSpec(memory_space=pltpu.VMEM)
SMEM = pl.BlockSpec(memory_space=pltpu.SMEM)


def work(source_coords, target_coords, source_logmass, target_logmass, target_prior, pair_source, pair_target):
    codes = pair_source * 4 + pair_target
    codes = jnp.where(pair_target >= 0, codes, -1).reshape(1, -1)
    codes = jnp.concatenate([codes] + [from_x(codes, k) for k in (1, 2, 3)], axis=0)
    codes = (codes,) + tuple(from_y(codes, k) for k in (1, 2, 3))

    def packed(coords, extra):
        zeros = jnp.zeros((CL, 5, CELLS), f32)
        return jnp.concatenate([coords, extra[:, None, :], zeros], axis=1)

    s0 = packed(source_coords, source_logmass)
    t = packed(target_coords, target_prior)
    t2 = fetched(t, lambda x, y, z, c: (x, y, z + x + FAR, c))
    t0 = fetched(t, lambda x, y, z, c: (x, y, z + x, c))
    s1, s2, s3 = (from_y(s0, k) for k in (1, 2, 3))
    t1, t3 = from_core(t0), from_core(t2)
    shards = (s0, s1, s2, s3, t0, t1, t2, t3)

    accumulators = [pltpu.VMEM((4 * CL + 1, 8, CELLS), f32)] * 2 + [pltpu.VMEM((CELLS, CELLS), f32)] * 2
    params = pltpu.CompilerParams(vmem_limit_bytes=16 * 2**20)
    rows, pairs = pl.pallas_call(
        row_kernel,
        out_shape=(
            jax.ShapeDtypeStruct((4 * CL, CELLS), f32),
            jax.ShapeDtypeStruct((LIST,), jnp.int32),
        ),
        in_specs=[SMEM] * 4 + [VMEM] * 8,
        out_specs=(VMEM, SMEM),
        scratch_shapes=[
            pltpu.VMEM((4 * CL + 1, DEPTH, CELLS), bf16),
            pltpu.VMEM((DEPTH, CELLS), bf16),
            pltpu.VMEM((4 * CL, CELLS, DEPTH), bf16),
        ]
        + accumulators,
        compiler_params=params,
        name="rows",
    )(*codes, *shards)

    rows = merged([rows] + [from_x(rows, k) for k in (1, 2, 3)])
    others = [from_y(rows, k) for k in (1, 2, 3)]

    kept, given, source_potential = pl.pallas_call(
        column_kernel,
        out_shape=(
            jax.ShapeDtypeStruct((2 * CL, CELLS), f32),
            jax.ShapeDtypeStruct((2 * CL, CELLS), f32),
            jax.ShapeDtypeStruct((CL, CELLS), f32),
        ),
        in_specs=[SMEM] + [VMEM] * 12,
        out_specs=(VMEM, VMEM, VMEM),
        scratch_shapes=[
            pltpu.VMEM((DEPTH, CELLS), bf16),
            pltpu.VMEM((4 * CL + 1, CELLS, DEPTH), bf16),
            pltpu.VMEM((4 * CL, DEPTH, CELLS), bf16),
        ]
        + accumulators,
        compiler_params=params,
        name="columns",
    )(pairs, rows, *others, *shards)

    kept = merged([kept, from_core(given)])
    first = fetched(kept[:CL], lambda x, y, z, c: (x, y, z - x, c))
    second = fetched(kept[CL:], lambda x, y, z, c: (x, y, z - x - FAR, c))
    part = merged([first, second])
    part = merged([part] + [from_x(part, k) for k in (1, 2, 3)])
    target_potential = EPSILON * target_logmass - (EPSILON * LN2) * part
    return source_potential, target_potential


def solution(mesh):
    return jax.shard_map(
        work,
        mesh=mesh,
        in_specs=(
            P("own", None, None),
            P("own", None, None),
            P("own", None),
            P("own", None),
            P("own", None),
            P("own", "split", None, None),
            P("own", "split", None, None),
        ),
        out_specs=(P("own", None), P("own", None)),
        check_vma=False,
    )
```

time: 95.4 us -> 84.9 us (0.89)
  Pallas kernels: 19 us -> 10.1 us
  starting transfers between devices: 44.6 us -> 50.8 us
  local copies, waits for them, and re-layouts: 6.45 us -> 1.87 us
  waiting for transfers between devices: 22.2 us -> 19.6 us
    pallas_call x2, Pallas kernels: 19 us -> 10.1 us  [the longest x1 5.15 us: work(): pl.pallas_call(row_kernel, out_shape=(jax.ShapeDtypeStruct((4 * CL, CELLS...]
    ppermute x25, starting transfers between devices: 44.6 us -> 50.8 us  [fetched(): return lax.ppermute(value, AXES, pairs)]
    ppermute x25, waiting for transfers between devices: 22.2 us -> 19.6 us  [fetched(): return lax.ppermute(value, AXES, pairs)]
    unnamed x38 -> x12, local copies, waits for them, and re-layouts: 3.13 us -> 1.09 us
    reshape x2 -> x0, local copies, waits for them, and re-layouts: 1.32 us -> none  [the longest x1 0.73 us: body(): columns = columns.reshape(2, 2, CL, CELLS)]
    concatenate x1 -> x0, local copies, waits for them, and re-layouts: 1.21 us -> none  [body(): jnp.concatenate([codes] + [from_y(codes, k) for k in (1, 2, 3)], axis=0)]
  transfers between devices with their start and end apart: 25 -> 25, of which waited for: 14 -> 14; matrix products, arithmetic and copies ran while one was open for 2% -> 0% of each run, Pallas kernels for 0% -> 0%
where the time goes in v2:
time: 84.9 us; the launch traced here: 83.9 us
  starting transfers between devices  50.8 us (60%)
  waiting for transfers between devices  19.6 us (23%)
  Pallas kernels  10.1 us (12%)
  local copies, waits for them, and re-layouts  1.87 us (2%)
    ppermute x25, starting transfers between devices, fetched(): return lax.ppermute(value, AXES, pairs)  50.8 us
    ppermute x25, waiting for transfers between devices, fetched(): return lax.ppermute(value, AXES, pairs)  19.6 us
    pallas_call x1, Pallas kernels, work(): pl.pallas_call(row_kernel, out_shape=(jax.ShapeDtypeStruct((4 * CL, CELLS...  5.15 us
    pallas_call x1, Pallas kernels, work(): pl.pallas_call(column_kernel, out_shape=(jax.ShapeDtypeStruct((2 * CL, CE...  4.93 us
  transfers between devices with their start and end apart: 25, of which 14 were waited for; matrix products, arithmetic and copies ran while one was open for 0% of the time, Pallas kernels for 0%

profile of v2, /device:TPU:64, one launch (start us, length us, event | category | flops | bytes accessed | tf_op | source)
XLA Modules:
  0.0 83.9 jit_solution(16593042488003323213)
XLA Ops:
  2.6 5.5 %collective-permute-start.11 = (f32[4,56,256]{2,1,0:T(8,128)S(1)}, f32[4,56,256]{2,1,0:T(8,128)S(1)}, u32[]{:S(2)}, u32[]{:S(2)}) collective-permute-start(f32[4,56,256]{2,1,0:T(8,128)S(1)} %get-tuple-element.14), channel_id=1, source_target_pairs={{32,0},{41,1},{50,2},{59,3},{36,4},{45,5},{54,6},{63,7},{40,8},{49... | collective-permute-start | bytes 688136 | tf_op jit(solution)/shard_map/ppermute | solution.py:44
  8.8 3.4 %collective-permute-start.2 = (s32[1,64]{1,0:T(1,128)S(1)}, s32[1,64]{1,0:T(1,128)S(1)}, u32[]{:S(2)}, u32[]{:S(2)}) collective-permute-start(s32[1,64]{1,0:T(1,128)S(1)} %fusion.4), channel_id=1, source_target_pairs={{3,0},{0,1},{1,2},{2,3},{7,4},{4,5},{5,6},{6,7},{11,8},{8,9},{9,10... | collective-permute-start | bytes 776 | tf_op jit(solution)/shard_map/ppermute | solution.py:44
  12.2 1.8 %collective-permute-start.1 = (s32[1,64]{1,0:T(1,128)S(1)}, s32[1,64]{1,0:T(1,128)S(1)}, u32[]{:S(2)}, u32[]{:S(2)}) collective-permute-start(s32[1,64]{1,0:T(1,128)S(1)} %fusion.4), channel_id=1, source_target_pairs={{2,0},{3,1},{0,2},{1,3},{6,4},{7,5},{4,6},{5,7},{10,8},{11,9},{8,1... | collective-permute-start | bytes 776 | tf_op jit(solution)/shard_map/ppermute | solution.py:44
  15.0 2.3 %collective-permute-done.1 = s32[1,64]{1,0:T(1,128)S(1)} collective-permute-done((s32[1,64]{1,0:T(1,128)S(1)}, s32[1,64]{1,0:T(1,128)S(1)}, u32[]{:S(2)}, u32[]{:S(2)}) %collective-permute-start.1) | collective-permute-done | bytes 288 | tf_op jit(solution)/shard_map/ppermute | solution.py:44
  17.5 1.7 %collective-permute-start.5 = (s32[4,64]{1,0:T(4,128)S(1)}, s32[4,64]{1,0:T(4,128)S(1)}, u32[]{:S(2)}, u32[]{:S(2)}) collective-permute-start(s32[4,64]{1,0:T(4,128)S(1)} %pad_add_fusion.c0), channel_id=1, source_target_pairs={{192,0},{193,1},{194,2},{195,3},{196,4},{197,5},{198,6},{199,7},{2... | collective-permute-start | bytes 3080 | tf_op jit(solution)/shard_map/ppermute | solution.py:44
  19.2 2.9 %collective-permute-start.4 = (s32[4,64]{1,0:T(4,128)S(1)}, s32[4,64]{1,0:T(4,128)S(1)}, u32[]{:S(2)}, u32[]{:S(2)}) collective-permute-start(s32[4,64]{1,0:T(4,128)S(1)} %pad_add_fusion.c0), channel_id=1, source_target_pairs={{128,0},{129,1},{130,2},{131,3},{132,4},{133,5},{134,6},{135,7},{1... | collective-permute-start | bytes 3080 | tf_op jit(solution)/shard_map/ppermute | solution.py:44
  22.1 1.3 %collective-permute-start.3 = (s32[4,64]{1,0:T(4,128)S(1)}, s32[4,64]{1,0:T(4,128)S(1)}, u32[]{:S(2)}, u32[]{:S(2)}) collective-permute-start(s32[4,64]{1,0:T(4,128)S(1)} %pad_add_fusion.c0), channel_id=1, source_target_pairs={{64,0},{65,1},{66,2},{67,3},{68,4},{69,5},{70,6},{71,7},{72,8},{73... | collective-permute-start | bytes 3080 | tf_op jit(solution)/shard_map/ppermute | solution.py:44
  24.3 2.9 %collective-permute-start.7 = (f32[4,56,256]{2,1,0:T(8,128)S(1)}, f32[4,56,256]{2,1,0:T(8,128)S(1)}, u32[]{:S(2)}, u32[]{:S(2)}) collective-permute-start(f32[4,56,256]{2,1,0:T(8,128)S(1)} %get-tuple-element.15.s0), channel_id=1, source_target_pairs={{128,0},{129,1},{130,2},{131,3},{132,4},{133,5},{134,6},{135,7},{1... | collective-permute-start | bytes 688136 | tf_op jit(solution)/shard_map/ppermute | solution.py:44
  27.2 1.3 %collective-permute-start.6 = (f32[4,56,256]{2,1,0:T(8,128)S(1)}, f32[4,56,256]{2,1,0:T(8,128)S(1)}, u32[]{:S(2)}, u32[]{:S(2)}) collective-permute-start(f32[4,56,256]{2,1,0:T(8,128)S(1)} %get-tuple-element.15.s0), channel_id=1, source_target_pairs={{64,0},{65,1},{66,2},{67,3},{68,4},{69,5},{70,6},{71,7},{72,8},{73... | collective-permute-start | bytes 688136 | tf_op jit(solution)/shard_map/ppermute | solution.py:44
  29.0 5.3 %collective-permute-done.8.s3 = f32[4,56,256]{2,1,0:T(8,128)S(1)} collective-permute-done((f32[4,56,256]{2,1,0:T(8,128)S(1)}, f32[4,56,256]{2,1,0:T(8,128)S(1)}, u32[]{:S(2)}, u32[]{:S(2)}) %collective-permute-start.8) | collective-permute-done | bytes 229408 | tf_op jit(solution)/shard_map/ppermute | solution.py:44
  35.0 5.2 %rows.1 = (f32[16,256]{1,0:T(8,128)S(1)}, s32[72]{0:T(128)S(1)}) custom-call(s32[4,64]{1,0:T(4,128)S(1)} %pad_add_fusion.c0, s32[4,64]{1,0:T(4,128)S(1)} %collective-permute-done.3.c1, s32[4,64]{1,0:T(4,128)S(1)} %collective-permute-done.4.c2, s32[4,64]{1,0:T(4,128)S(1)} %collective-permute-done.5.c3, f32[4,56,256]{2,1,0:T(8,128)S(1)} %get-tuple-element.15.s0, ...), custom_call_target="tpu_custom_call" | custom-call | tf_op jit(solution)/shard_map/rows/pallas_call | solution.py:262
  40.3 3.7 %collective-permute-start.14 = (f32[16,256]{1,0:T(8,128)S(1)}, f32[16,256]{1,0:T(8,128)S(1)}, u32[]{:S(2)}, u32[]{:S(2)}) collective-permute-start(f32[16,256]{1,0:T(8,128)S(1)} %get-tuple-element.8), channel_id=1, source_target_pairs={{2,0},{3,1},{0,2},{1,3},{6,4},{7,5},{4,6},{5,7},{10,8},{11,9},{8,1... | collective-permute-start | bytes 49160 | tf_op jit(solution)/shard_map/ppermute | solution.py:44
  43.9 1.3 %collective-permute-done.15 = f32[16,256]{1,0:T(8,128)S(1)} collective-permute-done((f32[16,256]{1,0:T(8,128)S(1)}, f32[16,256]{1,0:T(8,128)S(1)}, u32[]{:S(2)}, u32[]{:S(2)}) %collective-permute-start.15) | collective-permute-done | bytes 16416 | tf_op jit(solution)/shard_map/ppermute | solution.py:44
  45.8 1.9 %collective-permute-done.13 = f32[16,256]{1,0:T(8,128)S(1)} collective-permute-done((f32[16,256]{1,0:T(8,128)S(1)}, f32[16,256]{1,0:T(8,128)S(1)}, u32[]{:S(2)}, u32[]{:S(2)}) %collective-permute-start.13) | collective-permute-done | bytes 16416 | tf_op jit(solution)/shard_map/ppermute | solution.py:44
  47.7 1.4 %collective-permute-start.18 = (f32[16,256]{1,0:T(8,128)S(1)}, f32[16,256]{1,0:T(8,128)S(1)}, u32[]{:S(2)}, u32[]{:S(2)}) collective-permute-start(f32[16,256]{1,0:T(8,128)S(1)} %multiply_add_fusion.m0), channel_id=1, source_target_pairs={{192,0},{193,1},{194,2},{195,3},{196,4},{197,5},{198,6},{199,7},{2... | collective-permute-start | bytes 49160 | tf_op jit(solution)/shard_map/ppermute | solution.py:44
  49.1 2.4 %collective-permute-start.17 = (f32[16,256]{1,0:T(8,128)S(1)}, f32[16,256]{1,0:T(8,128)S(1)}, u32[]{:S(2)}, u32[]{:S(2)}) collective-permute-start(f32[16,256]{1,0:T(8,128)S(1)} %multiply_add_fusion.m0), channel_id=1, source_target_pairs={{128,0},{129,1},{130,2},{131,3},{132,4},{133,5},{134,6},{135,7},{1... | collective-permute-start | bytes 49160 | tf_op jit(solution)/shard_map/ppermute | solution.py:44
  52.9 1.4 %collective-permute-done.17.m2 = f32[16,256]{1,0:T(8,128)S(1)} collective-permute-done((f32[16,256]{1,0:T(8,128)S(1)}, f32[16,256]{1,0:T(8,128)S(1)}, u32[]{:S(2)}, u32[]{:S(2)}) %collective-permute-start.17) | collective-permute-done | bytes 16416 | tf_op jit(solution)/shard_map/ppermute | solution.py:44
  55.2 4.9 %columns.1 = (f32[8,256]{1,0:T(8,128)S(1)}, f32[8,256]{1,0:T(8,128)S(1)}, f32[4,256]{1,0:T(4,128)}) custom-call(s32[72]{0:T(128)S(1)} %get-tuple-element.7.list_ref, f32[16,256]{1,0:T(8,128)S(1)} %multiply_add_fusion.m0, f32[16,256]{1,0:T(8,128)S(1)} %collective-permute-done.16.m1, f32[16,256]{1,0:T(8,128)S(1)} %collective-permute-done.17.m2, ...), custom_call_target="tpu_custom_call" | custom-call | tf_op jit(solution)/shard_map/columns/pallas_call | solution.py:283
  62.0 7.0 %collective-permute-start.21 = (f32[4,256]{1,0:T(4,128)S(1)}, f32[4,256]{1,0:T(4,128)S(1)}, u32[]{:S(2)}, u32[]{:S(2)}) collective-permute-start(f32[4,256]{1,0:T(4,128)S(1)} %get-tuple-element.13), channel_id=1, source_target_pairs={{32,0},{25,1},{18,2},{11,3},{36,4},{29,5},{22,6},{15,7},{40,8},{33... | collective-permute-start | bytes 12296 | tf_op jit(solution)/shard_map/ppermute | solution.py:44
  69.1 1.6 %collective-permute-done.21 = f32[4,256]{1,0:T(4,128)S(1)} collective-permute-done((f32[4,256]{1,0:T(4,128)S(1)}, f32[4,256]{1,0:T(4,128)S(1)}, u32[]{:S(2)}, u32[]{:S(2)}) %collective-permute-start.21) | collective-permute-done | bytes 4128 | tf_op jit(solution)/shard_map/ppermute | solution.py:44
  70.7 5.7 %collective-permute-start.24 = (f32[4,256]{1,0:T(4,128)S(1)}, f32[4,256]{1,0:T(4,128)S(1)}, u32[]{:S(2)}, u32[]{:S(2)}) collective-permute-start(f32[4,256]{1,0:T(4,128)S(1)} %multiply_add_fusion.2), channel_id=1, source_target_pairs={{3,0},{0,1},{1,2},{2,3},{7,4},{4,5},{5,6},{6,7},{11,8},{8,9},{9,10... | collective-permute-start | bytes 12296 | tf_op jit(solution)/shard_map/ppermute | solution.py:44
  76.4 3.0 %collective-permute-start.23 = (f32[4,256]{1,0:T(4,128)S(1)}, f32[4,256]{1,0:T(4,128)S(1)}, u32[]{:S(2)}, u32[]{:S(2)}) collective-permute-start(f32[4,256]{1,0:T(4,128)S(1)} %multiply_add_fusion.2), channel_id=1, source_target_pairs={{2,0},{3,1},{0,2},{1,3},{6,4},{7,5},{4,6},{5,7},{10,8},{11,9},{8,1... | collective-permute-start | bytes 12296 | tf_op jit(solution)/shard_map/ppermute | solution.py:44
  79.4 2.5 %collective-permute-start.22 = (f32[4,256]{1,0:T(4,128)S(1)}, f32[4,256]{1,0:T(4,128)S(1)}, u32[]{:S(2)}, u32[]{:S(2)}) collective-permute-start(f32[4,256]{1,0:T(4,128)S(1)} %multiply_add_fusion.2), channel_id=1, source_target_pairs={{1,0},{2,1},{3,2},{0,3},{5,4},{6,5},{7,6},{4,7},{9,8},{10,9},{11,1... | collective-permute-start | bytes 12296 | tf_op jit(solution)/shard_map/ppermute | solution.py:44
  82.0 1.3 %collective-permute-done.22 = f32[4,256]{1,0:T(4,128)S(1)} collective-permute-done((f32[4,256]{1,0:T(4,128)S(1)}, f32[4,256]{1,0:T(4,128)S(1)}, u32[]{:S(2)}, u32[]{:S(2)}) %collective-permute-start.22) | collective-permute-done | bytes 4128 | tf_op jit(solution)/shard_map/ppermute | solution.py:44
  (52 shorter events, 11.5 us)
Async XLA Ops:
  2.6 25.9 %collective-permute-start.11 = (f32[4,56,256]{2,1,0:T(8,128)S(1)}, f32[4,56,256]{2,1,0:T(8,128)S(1)}, u32[]{:S(2)}, u32[]{:S(2)}) collective-permute-start(f32[4,56,256]{2,1,0:T(8,128)S(1)} %get-tuple-element.14), channel_id=1, source_target_pairs={{32,0},{41,1},{50,2},{59,3},{36,4},{45,5},{54,6},{63,7},{40,8},{49... | collective-permute-start | bytes 688136 | tf_op jit(solution)/shard_map/ppermute | solution.py:44
  8.1 20.4 %collective-permute-start.9 = (f32[4,56,256]{2,1,0:T(8,128)S(1)}, f32[4,56,256]{2,1,0:T(8,128)S(1)}, u32[]{:S(2)}, u32[]{:S(2)}) collective-permute-start(f32[4,56,256]{2,1,0:T(8,128)S(1)} %get-tuple-element.14), channel_id=1, source_target_pairs={{0,0},{9,1},{18,2},{27,3},{4,4},{13,5},{22,6},{31,7},{8,8},{17,9},... | collective-permute-start | bytes 688136 | tf_op jit(solution)/shard_map/ppermute | solution.py:44
  8.8 6.1 %collective-permute-start.2 = (s32[1,64]{1,0:T(1,128)S(1)}, s32[1,64]{1,0:T(1,128)S(1)}, u32[]{:S(2)}, u32[]{:S(2)}) collective-permute-start(s32[1,64]{1,0:T(1,128)S(1)} %fusion.4), channel_id=1, source_target_pairs={{3,0},{0,1},{1,2},{2,3},{7,4},{4,5},{5,6},{6,7},{11,8},{8,9},{9,10... | collective-permute-start | bytes 776 | tf_op jit(solution)/shard_map/ppermute | solution.py:44
  12.2 5.1 %collective-permute-start.1 = (s32[1,64]{1,0:T(1,128)S(1)}, s32[1,64]{1,0:T(1,128)S(1)}, u32[]{:S(2)}, u32[]{:S(2)}) collective-permute-start(s32[1,64]{1,0:T(1,128)S(1)} %fusion.4), channel_id=1, source_target_pairs={{2,0},{3,1},{0,2},{1,3},{6,4},{7,5},{4,6},{5,7},{10,8},{11,9},{8,1... | collective-permute-start | bytes 776 | tf_op jit(solution)/shard_map/ppermute | solution.py:44
  13.9 3.6 %collective-permute-start = (s32[1,64]{1,0:T(1,128)S(1)}, s32[1,64]{1,0:T(1,128)S(1)}, u32[]{:S(2)}, u32[]{:S(2)}) collective-permute-start(s32[1,64]{1,0:T(1,128)S(1)} %fusion.4), channel_id=1, source_target_pairs={{1,0},{2,1},{3,2},{0,3},{5,4},{6,5},{7,6},{4,7},{9,8},{10,9},{11,1... | collective-permute-start | bytes 776 | tf_op jit(solution)/shard_map/ppermute | solution.py:44
  17.5 5.9 %collective-permute-start.5 = (s32[4,64]{1,0:T(4,128)S(1)}, s32[4,64]{1,0:T(4,128)S(1)}, u32[]{:S(2)}, u32[]{:S(2)}) collective-permute-start(s32[4,64]{1,0:T(4,128)S(1)} %pad_add_fusion.c0), channel_id=1, source_target_pairs={{192,0},{193,1},{194,2},{195,3},{196,4},{197,5},{198,6},{199,7},{2... | collective-permute-start | bytes 3080 | tf_op jit(solution)/shard_map/ppermute | solution.py:44
  19.2 5.1 %collective-permute-start.4 = (s32[4,64]{1,0:T(4,128)S(1)}, s32[4,64]{1,0:T(4,128)S(1)}, u32[]{:S(2)}, u32[]{:S(2)}) collective-permute-start(s32[4,64]{1,0:T(4,128)S(1)} %pad_add_fusion.c0), channel_id=1, source_target_pairs={{128,0},{129,1},{130,2},{131,3},{132,4},{133,5},{134,6},{135,7},{1... | collective-permute-start | bytes 3080 | tf_op jit(solution)/shard_map/ppermute | solution.py:44
  22.1 5.1 %collective-permute-start.3 = (s32[4,64]{1,0:T(4,128)S(1)}, s32[4,64]{1,0:T(4,128)S(1)}, u32[]{:S(2)}, u32[]{:S(2)}) collective-permute-start(s32[4,64]{1,0:T(4,128)S(1)} %pad_add_fusion.c0), channel_id=1, source_target_pairs={{64,0},{65,1},{66,2},{67,3},{68,4},{69,5},{70,6},{71,7},{72,8},{73... | collective-permute-start | bytes 3080 | tf_op jit(solution)/shard_map/ppermute | solution.py:44
  23.4 10.9 %collective-permute-start.8 = (f32[4,56,256]{2,1,0:T(8,128)S(1)}, f32[4,56,256]{2,1,0:T(8,128)S(1)}, u32[]{:S(2)}, u32[]{:S(2)}) collective-permute-start(f32[4,56,256]{2,1,0:T(8,128)S(1)} %get-tuple-element.15.s0), channel_id=1, source_target_pairs={{192,0},{193,1},{194,2},{195,3},{196,4},{197,5},{198,6},{199,7},{2... | collective-permute-start | bytes 688136 | tf_op jit(solution)/shard_map/ppermute | solution.py:44
  24.3 10.1 %collective-permute-start.7 = (f32[4,56,256]{2,1,0:T(8,128)S(1)}, f32[4,56,256]{2,1,0:T(8,128)S(1)}, u32[]{:S(2)}, u32[]{:S(2)}) collective-permute-start(f32[4,56,256]{2,1,0:T(8,128)S(1)} %get-tuple-element.15.s0), channel_id=1, source_target_pairs={{128,0},{129,1},{130,2},{131,3},{132,4},{133,5},{134,6},{135,7},{1... | collective-permute-start | bytes 688136 | tf_op jit(solution)/shard_map/ppermute | solution.py:44
  27.2 7.8 %collective-permute-start.6 = (f32[4,56,256]{2,1,0:T(8,128)S(1)}, f32[4,56,256]{2,1,0:T(8,128)S(1)}, u32[]{:S(2)}, u32[]{:S(2)}) collective-permute-start(f32[4,56,256]{2,1,0:T(8,128)S(1)} %get-tuple-element.15.s0), channel_id=1, source_target_pairs={{64,0},{65,1},{66,2},{67,3},{68,4},{69,5},{70,6},{71,7},{72,8},{73... | collective-permute-start | bytes 688136 | tf_op jit(solution)/shard_map/ppermute | solution.py:44
  28.5 6.5 %collective-permute-start.12 = (f32[4,56,256]{2,1,0:T(8,128)S(1)}, f32[4,56,256]{2,1,0:T(8,128)S(1)}, u32[]{:S(2)}, u32[]{:S(2)}) collective-permute-start(f32[4,56,256]{2,1,0:T(8,128)S(1)} %collective-permute-done.11.t2), channel_id=1, source_target_pairs={{4,0},{5,1},{6,2},{7,3},{0,4},{1,5},{2,6},{3,7},{12,8},{13,9},{14,... | collective-permute-start | bytes 688136 | tf_op jit(solution)/shard_map/ppermute | solution.py:44
  28.5 6.5 %collective-permute-start.10 = (f32[4,56,256]{2,1,0:T(8,128)S(1)}, f32[4,56,256]{2,1,0:T(8,128)S(1)}, u32[]{:S(2)}, u32[]{:S(2)}) collective-permute-start(f32[4,56,256]{2,1,0:T(8,128)S(1)} %collective-permute-done.9.t0), channel_id=1, source_target_pairs={{4,0},{5,1},{6,2},{7,3},{0,4},{1,5},{2,6},{3,7},{12,8},{13,9},{14,... | collective-permute-start | bytes 688136 | tf_op jit(solution)/shard_map/ppermute | solution.py:44
  40.2 5.0 %collective-permute-start.15 = (f32[16,256]{1,0:T(8,128)S(1)}, f32[16,256]{1,0:T(8,128)S(1)}, u32[]{:S(2)}, u32[]{:S(2)}) collective-permute-start(f32[16,256]{1,0:T(8,128)S(1)} %get-tuple-element.8), channel_id=1, source_target_pairs={{3,0},{0,1},{1,2},{2,3},{7,4},{4,5},{5,6},{6,7},{11,8},{8,9},{9,10... | collective-permute-start | bytes 49160 | tf_op jit(solution)/shard_map/ppermute | solution.py:44
  40.3 5.6 %collective-permute-start.14 = (f32[16,256]{1,0:T(8,128)S(1)}, f32[16,256]{1,0:T(8,128)S(1)}, u32[]{:S(2)}, u32[]{:S(2)}) collective-permute-start(f32[16,256]{1,0:T(8,128)S(1)} %get-tuple-element.8), channel_id=1, source_target_pairs={{2,0},{3,1},{0,2},{1,3},{6,4},{7,5},{4,6},{5,7},{10,8},{11,9},{8,1... | collective-permute-start | bytes 49160 | tf_op jit(solution)/shard_map/ppermute | solution.py:44
  43.9 3.7 %collective-permute-start.13 = (f32[16,256]{1,0:T(8,128)S(1)}, f32[16,256]{1,0:T(8,128)S(1)}, u32[]{:S(2)}, u32[]{:S(2)}) collective-permute-start(f32[16,256]{1,0:T(8,128)S(1)} %get-tuple-element.8), channel_id=1, source_target_pairs={{1,0},{2,1},{3,2},{0,3},{5,4},{6,5},{7,6},{4,7},{9,8},{10,9},{11,1... | collective-permute-start | bytes 49160 | tf_op jit(solution)/shard_map/ppermute | solution.py:44
  47.7 5.2 %collective-permute-start.18 = (f32[16,256]{1,0:T(8,128)S(1)}, f32[16,256]{1,0:T(8,128)S(1)}, u32[]{:S(2)}, u32[]{:S(2)}) collective-permute-start(f32[16,256]{1,0:T(8,128)S(1)} %multiply_add_fusion.m0), channel_id=1, source_target_pairs={{192,0},{193,1},{194,2},{195,3},{196,4},{197,5},{198,6},{199,7},{2... | collective-permute-start | bytes 49160 | tf_op jit(solution)/shard_map/ppermute | solution.py:44
  49.1 5.2 %collective-permute-start.17 = (f32[16,256]{1,0:T(8,128)S(1)}, f32[16,256]{1,0:T(8,128)S(1)}, u32[]{:S(2)}, u32[]{:S(2)}) collective-permute-start(f32[16,256]{1,0:T(8,128)S(1)} %multiply_add_fusion.m0), channel_id=1, source_target_pairs={{128,0},{129,1},{130,2},{131,3},{132,4},{133,5},{134,6},{135,7},{1... | collective-permute-start | bytes 49160 | tf_op jit(solution)/shard_map/ppermute | solution.py:44
  51.5 3.7 %collective-permute-start.16 = (f32[16,256]{1,0:T(8,128)S(1)}, f32[16,256]{1,0:T(8,128)S(1)}, u32[]{:S(2)}, u32[]{:S(2)}) collective-permute-start(f32[16,256]{1,0:T(8,128)S(1)} %multiply_add_fusion.m0), channel_id=1, source_target_pairs={{64,0},{65,1},{66,2},{67,3},{68,4},{69,5},{70,6},{71,7},{72,8},{73... | collective-permute-start | bytes 49160 | tf_op jit(solution)/shard_map/ppermute | solution.py:44
  61.4 7.7 %collective-permute-start.20 = (f32[4,256]{1,0:T(4,128)S(1)}, f32[4,256]{1,0:T(4,128)S(1)}, u32[]{:S(2)}, u32[]{:S(2)}) collective-permute-start(f32[4,256]{1,0:T(4,128)S(1)} %get-tuple-element.12), channel_id=1, source_target_pairs={{0,0},{57,1},{50,2},{43,3},{4,4},{61,5},{54,6},{47,7},{8,8},{1,9},... | collective-permute-start | bytes 12296 | tf_op jit(solution)/shard_map/ppermute | solution.py:44
  62.0 8.6 %collective-permute-start.21 = (f32[4,256]{1,0:T(4,128)S(1)}, f32[4,256]{1,0:T(4,128)S(1)}, u32[]{:S(2)}, u32[]{:S(2)}) collective-permute-start(f32[4,256]{1,0:T(4,128)S(1)} %get-tuple-element.13), channel_id=1, source_target_pairs={{32,0},{25,1},{18,2},{11,3},{36,4},{29,5},{22,6},{15,7},{40,8},{33... | collective-permute-start | bytes 12296 | tf_op jit(solution)/shard_map/ppermute | solution.py:44
  70.7 11.3 %collective-permute-start.24 = (f32[4,256]{1,0:T(4,128)S(1)}, f32[4,256]{1,0:T(4,128)S(1)}, u32[]{:S(2)}, u32[]{:S(2)}) collective-permute-start(f32[4,256]{1,0:T(4,128)S(1)} %multiply_add_fusion.2), channel_id=1, source_target_pairs={{3,0},{0,1},{1,2},{2,3},{7,4},{4,5},{5,6},{6,7},{11,8},{8,9},{9,10... | collective-permute-start | bytes 12296 | tf_op jit(solution)/shard_map/ppermute | solution.py:44
  76.4 5.6 %collective-permute-start.23 = (f32[4,256]{1,0:T(4,128)S(1)}, f32[4,256]{1,0:T(4,128)S(1)}, u32[]{:S(2)}, u32[]{:S(2)}) collective-permute-start(f32[4,256]{1,0:T(4,128)S(1)} %multiply_add_fusion.2), channel_id=1, source_target_pairs={{2,0},{3,1},{0,2},{1,3},{6,4},{7,5},{4,6},{5,7},{10,8},{11,9},{8,1... | collective-permute-start | bytes 12296 | tf_op jit(solution)/shard_map/ppermute | solution.py:44
  79.4 3.9 %collective-permute-start.22 = (f32[4,256]{1,0:T(4,128)S(1)}, f32[4,256]{1,0:T(4,128)S(1)}, u32[]{:S(2)}, u32[]{:S(2)}) collective-permute-start(f32[4,256]{1,0:T(4,128)S(1)} %multiply_add_fusion.2), channel_id=1, source_target_pairs={{1,0},{2,1},{3,2},{0,3},{5,4},{6,5},{7,6},{4,7},{9,8},{10,9},{11,1... | collective-permute-start | bytes 12296 | tf_op jit(solution)/shard_map/ppermute | solution.py:44
  (6 other events, 36.5 us)

commit v3 on v2

--- a/solution.py
+++ b/solution.py
@@ -44,12 +44,21 @@
     return lax.ppermute(value, AXES, pairs)
 
 
-def from_x(value, k):
-    return fetched(value, lambda x, y, z, c: (x + k, y, z, c))
-
-
 def from_y(value, k):
     return fetched(value, lambda x, y, z, c: (x, y + k, z, c))
+
+
+PLANES = [[device(x, y, z, c) for x in range(NX) for y in range(NY)] for z in range(NZ) for c in range(NC)]
+SHARERS = [
+    [device(x, y, z - x + FAR * e, c) for x in range(NX) for e in range(2) for c in range(NC)]
+    for y in range(NY)
+    for z in range(FAR)
+]
+MEMBERS = 16
+
+
+def exchanged(value, groups):
+    return lax.all_to_all(value, AXES, 0, 0, axis_index_groups=groups, tiled=True)
 
 
 def from_core(value):
@@ -63,9 +72,14 @@
     return high, middle, rest - middle
 
 
+def place():
+    own, x = lax.axis_index("own"), lax.axis_index("split")
+    return x, own // (NZ * NC), (own // NC) % NZ, own % NC
+
+
 def target_owners():
-    own, x = lax.axis_index("own"), lax.axis_index("split")
-    row, z, c = (own // (NZ * NC)) * (NZ * NC), (own // NC) % NZ, own % NC
+    x, y, z, c = place()
+    row = y * (NZ * NC)
     near = row + ((z + x) % NZ) * NC
     far = row + ((z + x + NZ // 2) % NZ) * NC
     return near + c, near + 1 - c, far + c, far + 1 - c
@@ -151,7 +165,7 @@
     return logsum(top[:, 0, :], total)
 
 
-def row_kernel(c0, c1, c2, c3, s0, s1, s2, s3, t0, t1, t2, t3, out, list_ref, xn, yn, yt, top, tot, even, odd):
+def row_kernel(codes, s0, s1, s2, s3, t0, t1, t2, t3, out, list_ref, xn, yn, yt, top, tot, even, odd):
     one = jnp.ones((1, CELLS), f32)
     ones = (one, one, one)
     middle = centre(s0)
@@ -177,10 +191,11 @@
             yt[k * CL + a] = yn[...].T
     owners = target_owners()
     count = jnp.int32(0)
-    for k, codes in enumerate((c0, c1, c2, c3)):
+    y = place()[1]
+    for k in range(4):
         for d in range(NX):
             for t in range(4):
-                code = codes[d, owners[t]]
+                code = codes[d * NY + (y + k) % NY, owners[t]]
                 source = k * CL + (code >> 2)
                 list_ref[count] = source * 256 + t * CL + (code & 3)
                 count = count + (code >= 0).astype(jnp.int32)
@@ -190,19 +205,23 @@
     top[...] = jnp.full(top.shape, NEGATIVE, f32)
     tot[...] = jnp.zeros(tot.shape, f32)
     over_pairs(count, list_ref, yt, xn, lambda s, t: (t, s, s), top, tot, even, odd)
-    out[...] = finish(top, tot)
-
-
-def column_kernel(list_ref, m0, m1, m2, m3, s0, s1, s2, s3, t0, t1, t2, t3, kept, given, potential, xn, xt, yn, top, tot, even, odd):
+    rows = finish(top, tot).reshape(4, CL, CELLS)
+    for k in range(4):
+        for m in range(MEMBERS):
+            out[m, (y + k) % NY] = rows[k]
+
+
+def column_kernel(list_ref, came, s0, s1, s2, s3, t0, t1, t2, t3, out, potential, xn, xt, yn, top, tot, even, odd, four):
     one = jnp.ones((1, CELLS), f32)
     ones = (one, one, one)
     middle = centre(s0)
-    came = (m0, m1, m2, m3)
+    x, y, z, c = place()
+    four[...] = merged([came[m] for m in range(MEMBERS)])
     for k, ref in enumerate((s0, s1, s2, s3)):
+        rows = four[(y + k) % NY]
         for a in range(CL):
             head, tail, mass, square = load_cluster(ref, a, middle)
-            rows = [came[d][((k - d) % 4) * CL + a : ((k - d) % 4) * CL + a + 1, :] for d in range(4)]
-            p = EPSILON * mass - (EPSILON * LN2) * merged(rows)
+            p = EPSILON * mass - (EPSILON * LN2) * rows[a : a + 1]
             if k == 0:
                 potential[a : a + 1, :] = p
 
@@ -229,10 +248,13 @@
         return s, t, jnp.where(s == 4 * CL, 4 * CL, t)
 
     over_pairs(list_ref[LIST - 1], list_ref, xt, yn, pick, top, tot, even, odd)
-    columns = finish(top, tot)
-    for k in range(2):
-        kept[k * CL : (k + 1) * CL, :] = columns[2 * k * CL : (2 * k + 1) * CL]
-        given[k * CL : (k + 1) * CL, :] = columns[(2 * k + 1) * CL : (2 * k + 2) * CL]
+    four[...] = finish(top, tot).reshape(4, CL, CELLS)
+    half = ((z + x) // FAR) % 2
+    for f in range(2):
+        for core in range(NC):
+            part = four[2 * (f ^ half) + (core ^ c)]
+            for d in range(NX):
+                out[(d * 2 + f) * NC + core] = part
 
 
 VMEM = pl.BlockSpec(memory_space=pltpu.VMEM)
@@ -242,8 +264,7 @@
 def work(source_coords, target_coords, source_logmass, target_logmass, target_prior, pair_source, pair_target):
     codes = pair_source * 4 + pair_target
     codes = jnp.where(pair_target >= 0, codes, -1).reshape(1, -1)
-    codes = jnp.concatenate([codes] + [from_x(codes, k) for k in (1, 2, 3)], axis=0)
-    codes = (codes,) + tuple(from_y(codes, k) for k in (1, 2, 3))
+    codes = exchanged(jnp.broadcast_to(codes, (MEMBERS, codes.shape[1])), PLANES)
 
     def packed(coords, extra):
         zeros = jnp.zeros((CL, 5, CELLS), f32)
@@ -262,10 +283,10 @@
     rows, pairs = pl.pallas_call(
         row_kernel,
         out_shape=(
-            jax.ShapeDtypeStruct((4 * CL, CELLS), f32),
+            jax.ShapeDtypeStruct((MEMBERS, 4, CL, CELLS), f32),
             jax.ShapeDtypeStruct((LIST,), jnp.int32),
         ),
-        in_specs=[SMEM] * 4 + [VMEM] * 8,
+        in_specs=[SMEM] + [VMEM] * 8,
         out_specs=(VMEM, SMEM),
         scratch_shapes=[
             pltpu.VMEM((4 * CL + 1, DEPTH, CELLS), bf16),
@@ -275,35 +296,31 @@
         + accumulators,
         compiler_params=params,
         name="rows",
-    )(*codes, *shards)
-
-    rows = merged([rows] + [from_x(rows, k) for k in (1, 2, 3)])
-    others = [from_y(rows, k) for k in (1, 2, 3)]
-
-    kept, given, source_potential = pl.pallas_call(
+    )(codes, *shards)
+
+    rows = exchanged(rows, PLANES)
+
+    columns, source_potential = pl.pallas_call(
         column_kernel,
         out_shape=(
-            jax.ShapeDtypeStruct((2 * CL, CELLS), f32),
-            jax.ShapeDtypeStruct((2 * CL, CELLS), f32),
+            jax.ShapeDtypeStruct((MEMBERS, CL, CELLS), f32),
             jax.ShapeDtypeStruct((CL, CELLS), f32),
         ),
-        in_specs=[SMEM] + [VMEM] * 12,
-        out_specs=(VMEM, VMEM, VMEM),
+        in_specs=[SMEM] + [VMEM] * 9,
+        out_specs=(VMEM, VMEM),
         scratch_shapes=[
             pltpu.VMEM((DEPTH, CELLS), bf16),
             pltpu.VMEM((4 * CL + 1, CELLS, DEPTH), bf16),
             pltpu.VMEM((4 * CL, DEPTH, CELLS), bf16),
         ]
-        + accumulators,
+        + accumulators
+        + [pltpu.VMEM((4, CL, CELLS), f32)],
         compiler_params=params,
         name="columns",
-    )(pairs, rows, *others, *shards)
-
-    kept = merged([kept, from_core(given)])
-    first = fetched(kept[:CL], lambda x, y, z, c: (x, y, z - x, c))
-    second = fetched(kept[CL:], lambda x, y, z, c: (x, y, z - x - FAR, c))
-    part = merged([first, second])
-    part = merged([part] + [from_x(part, k) for k in (1, 2, 3)])
+    )(pairs, rows, *shards)
+
+    part = merged(list(exchanged(columns, SHARERS)))
+    part = fetched(part, lambda x, y, z, c: (x, y, z - x, c))
     target_potential = EPSILON * target_logmass - (EPSILON * LN2) * part
     return source_potential, target_potential
 

time: 84.9 us -> 89.1 us (1.049)
  the two profiles are of different devices: /device:TPU:64 before, /device:TPU:6 now
where the time goes in v3:
time: 89.1 us; the launch traced here: 88.8 us
  blocking collectives  43.1 us (48%)
  starting transfers between devices  20.3 us (23%)
  waiting for transfers between devices  11.8 us (13%)
  Pallas kernels  10.2 us (11%)
  local copies, waits for them, and re-layouts  1.87 us (2%)
    all_to_all x3, blocking collectives, exchanged(): lax.all_to_all(value, AXES, 0, 0, axis_index_groups=groups, tiled=True)  43.1 us
    ppermute x8, starting transfers between devices, fetched(): return lax.ppermute(value, AXES, pairs)  20.3 us
    ppermute x8, waiting for transfers between devices, fetched(): return lax.ppermute(value, AXES, pairs)  11.8 us
    pallas_call x1, Pallas kernels, work(): pl.pallas_call(row_kernel, out_shape=(jax.ShapeDtypeStruct((MEMBERS, 4, C...  5.22 us
    pallas_call x1, Pallas kernels, work(): pl.pallas_call(column_kernel, out_shape=(jax.ShapeDtypeStruct((MEMBERS, C...  4.99 us
  transfers between devices with their start and end apart: 8, of which 2 were waited for; matrix products, arithmetic and copies ran while one was open for 0% of the time, Pallas kernels for 0%

profile of v3, /device:TPU:6, one launch (start us, length us, event | category | flops | bytes accessed | tf_op | source)
XLA Modules:
  0.0 88.8 jit_solution(9230301517853402803)
XLA Ops:
  0.6 0.7 broadcast_in_dim.20
  1.3 0.0 copy-start
  1.4 1.0 %copy.11 = f32[4,50,256]{2,1,0:T(8,128)S(1)} copy(f32[4,50,256]{2,0,1:T(4,128)} %param.7) | data formatting | bytes 409600 | tf_op args[0]
  2.4 0.0 copy-done
  2.4 0.1 pad.5.clone
  2.5 0.1 maximum_maximum_fusion.1
  2.6 0.0 copy-start.3
  2.6 0.0 copy-start.4
  2.7 2.0 %collective-permute-start.5 = (f32[4,56,256]{2,1,0:T(8,128)S(1)}, f32[4,56,256]{2,1,0:T(8,128)S(1)}, u32[]{:S(2)}, u32[]{:S(2)}) collective-permute-start(f32[4,56,256]{2,1,0:T(8,128)S(1)} %get-tuple-element.10), channel_id=1, source_target_pairs={{32,0},{41,1},{50,2},{59,3},{36,4},{45,5},{54,6},{63,7},{40,8},{49... | collective-permute-start | bytes 688136 | tf_op jit(solution)/shard_map/ppermute | solution.py:44
  4.6 7.7 %collective-permute-start.3 = (f32[4,56,256]{2,1,0:T(8,128)S(1)}, f32[4,56,256]{2,1,0:T(8,128)S(1)}, u32[]{:S(2)}, u32[]{:S(2)}) collective-permute-start(f32[4,56,256]{2,1,0:T(8,128)S(1)} %get-tuple-element.10), channel_id=1, source_target_pairs={{0,0},{9,1},{18,2},{27,3},{4,4},{13,5},{22,6},{31,7},{8,8},{17,9},... | collective-permute-start | bytes 688136 | tf_op jit(solution)/shard_map/ppermute | solution.py:44
  12.4 1.7 %collective-permute-start.2 = (f32[4,56,256]{2,1,0:T(8,128)S(1)}, f32[4,56,256]{2,1,0:T(8,128)S(1)}, u32[]{:S(2)}, u32[]{:S(2)}) collective-permute-start(f32[4,56,256]{2,1,0:T(8,128)S(1)} %get-tuple-element.11.s0), channel_id=1, source_target_pairs={{192,0},{193,1},{194,2},{195,3},{196,4},{197,5},{198,6},{199,7},{2... | collective-permute-start | bytes 688136 | tf_op jit(solution)/shard_map/ppermute | solution.py:44
  14.0 2.9 %collective-permute-start.1 = (f32[4,56,256]{2,1,0:T(8,128)S(1)}, f32[4,56,256]{2,1,0:T(8,128)S(1)}, u32[]{:S(2)}, u32[]{:S(2)}) collective-permute-start(f32[4,56,256]{2,1,0:T(8,128)S(1)} %get-tuple-element.11.s0), channel_id=1, source_target_pairs={{128,0},{129,1},{130,2},{131,3},{132,4},{133,5},{134,6},{135,7},{1... | collective-permute-start | bytes 688136 | tf_op jit(solution)/shard_map/ppermute | solution.py:44
  16.9 1.3 %collective-permute-start = (f32[4,56,256]{2,1,0:T(8,128)S(1)}, f32[4,56,256]{2,1,0:T(8,128)S(1)}, u32[]{:S(2)}, u32[]{:S(2)}) collective-permute-start(f32[4,56,256]{2,1,0:T(8,128)S(1)} %get-tuple-element.11.s0), channel_id=1, source_target_pairs={{64,0},{65,1},{66,2},{67,3},{68,4},{69,5},{70,6},{71,7},{72,8},{73... | collective-permute-start | bytes 688136 | tf_op jit(solution)/shard_map/ppermute | solution.py:44
  18.3 7.9 %collective-permute-done.3.t0 = f32[4,56,256]{2,1,0:T(8,128)S(1)} collective-permute-done((f32[4,56,256]{2,1,0:T(8,128)S(1)}, f32[4,56,256]{2,1,0:T(8,128)S(1)}, u32[]{:S(2)}, u32[]{:S(2)}) %collective-permute-start.3) | collective-permute-done | bytes 229408 | tf_op jit(solution)/shard_map/ppermute | solution.py:44
  26.3 12.6 %all_to_all.18 = s32[16,1,64]{2,1,0:T(1,128)S(1)} all-to-all(s32[16,1,64]{2,1,0:T(1,128)S(1)} %broadcast_in_dim.19), channel_id=1, replica_groups={{0,64,128,192,1,65,129,193,2,66,130,194,3,67,131,195},{4,68,132,196,5,6..., dimensions={0} | all-to-all | bytes 8192 | tf_op jit(solution)/shard_map/all_to_all | solution.py:61
  38.8 0.0 collective-permute-done.2.s3
  38.9 5.2 %rows.1 = (f32[16,4,4,256]{3,2,1,0:T(4,128)S(1)}, s32[72]{0:T(128)S(1)}) custom-call(s32[16,64]{1,0:T(8,128)S(1)} %bitcast.67, f32[4,56,256]{2,1,0:T(8,128)S(1)} %get-tuple-element.11.s0, f32[4,56,256]{2,1,0:T(8,128)S(1)} %collective-permute-done.s1, f32[4,56,256]{2,1,0:T(8,128)S(1)} %collective-permute-done.1.s2, ...), custom_call_target="tpu_custom_call" | custom-call | tf_op jit(solution)/shard_map/rows/pallas_call | solution.py:283
  44.1 13.3 %all_to_all.19.came = f32[16,4,4,256]{3,2,1,0:T(4,128)S(1)} all-to-all(f32[16,4,4,256]{3,2,1,0:T(4,128)S(1)} %get-tuple-element.7), channel_id=1, replica_groups={{0,64,128,192,1,65,129,193,2,66,130,194,3,67,131,195},{4,68,132,196,5,6..., dimensions={0} | all-to-all | bytes 524288 | tf_op jit(solution)/shard_map/all_to_all | solution.py:61
  57.4 5.0 %columns.1 = (f32[16,4,256]{2,1,0:T(4,128)S(1)}, f32[4,256]{1,0:T(4,128)}) custom-call(s32[72]{0:T(128)S(1)} %get-tuple-element.6.list_ref, f32[16,4,4,256]{3,2,1,0:T(4,128)S(1)} %all_to_all.19.came, f32[4,56,256]{2,1,0:T(8,128)S(1)} %get-tuple-element.11.s0, f32[4,56,256]{2,1,0:T(8,128)S(1)} %collective-permute-done.s1, ...), custom_call_target="tpu_custom_call" | custom-call | tf_op jit(solution)/shard_map/columns/pallas_call | solution.py:303
  62.4 17.2 %all_to_all.20 = f32[16,4,256]{2,1,0:T(4,128)S(1)} all-to-all(f32[16,4,256]{2,1,0:T(4,128)S(1)} %get-tuple-element.9), channel_id=1, replica_groups={{0,4,32,36,57,61,25,29,50,54,18,22,43,47,11,15},{8,12,40,44,1,5,33,37,5..., dimensions={0} | all-to-all | bytes 131072 | tf_op jit(solution)/shard_map/all_to_all | solution.py:61
  79.6 0.1 multiply_add_fusion
  79.7 4.7 %collective-permute-start.7 = (f32[4,256]{1,0:T(4,128)S(1)}, f32[4,256]{1,0:T(4,128)S(1)}, u32[]{:S(2)}, u32[]{:S(2)}) collective-permute-start(f32[4,256]{1,0:T(4,128)S(1)} %multiply_add_fusion), channel_id=1, source_target_pairs={{0,0},{57,1},{50,2},{43,3},{4,4},{61,5},{54,6},{47,7},{8,8},{1,9},... | collective-permute-start | bytes 12296 | tf_op jit(solution)/shard_map/ppermute | solution.py:44
  84.3 3.9 %collective-permute-done.7 = f32[4,256]{1,0:T(4,128)S(1)} collective-permute-done((f32[4,256]{1,0:T(4,128)S(1)}, f32[4,256]{1,0:T(4,128)S(1)}, u32[]{:S(2)}, u32[]{:S(2)}) %collective-permute-start.7) | collective-permute-done | bytes 4128 | tf_op jit(solution)/shard_map/ppermute | solution.py:44
  88.2 0.6 multiply_subtract_fusion
  (18 shorter events, 0.1 us)
Async XLA Ops:
  0.6 0.7 copy-start.2
  1.3 1.0 %copy-start = (f32[4,50,256]{2,0,1:T(4,128)S(1)}, f32[4,50,256]{2,0,1:T(4,128)}, u32[]{:S(2)}) copy-start(f32[4,50,256]{2,0,1:T(4,128)} %param.8) | copy-start | bytes 614404
  2.6 23.6 %copy-start.3 = (s32[1,1,64,1]{2,3,1,0:T(1,128)S(1)}, s32[1,1,64,1]{2,3,1,0:T(1,128)}, u32[]{:S(2)}) copy-start(s32[1,1,64,1]{2,3,1,0:T(1,128)} %param.13) | copy-start | bytes 772
  2.6 23.6 %copy-start.4 = (s32[1,1,64,1]{2,3,1,0:T(1,128)S(1)}, s32[1,1,64,1]{2,3,1,0:T(1,128)}, u32[]{:S(2)}) copy-start(s32[1,1,64,1]{2,3,1,0:T(1,128)} %param.12) | copy-start | bytes 772
  2.7 15.6 %collective-permute-start.5 = (f32[4,56,256]{2,1,0:T(8,128)S(1)}, f32[4,56,256]{2,1,0:T(8,128)S(1)}, u32[]{:S(2)}, u32[]{:S(2)}) collective-permute-start(f32[4,56,256]{2,1,0:T(8,128)S(1)} %get-tuple-element.10), channel_id=1, source_target_pairs={{32,0},{41,1},{50,2},{59,3},{36,4},{45,5},{54,6},{63,7},{40,8},{49... | collective-permute-start | bytes 688136 | tf_op jit(solution)/shard_map/ppermute | solution.py:44
  4.6 21.6 %collective-permute-start.3 = (f32[4,56,256]{2,1,0:T(8,128)S(1)}, f32[4,56,256]{2,1,0:T(8,128)S(1)}, u32[]{:S(2)}, u32[]{:S(2)}) collective-permute-start(f32[4,56,256]{2,1,0:T(8,128)S(1)} %get-tuple-element.10), channel_id=1, source_target_pairs={{0,0},{9,1},{18,2},{27,3},{4,4},{13,5},{22,6},{31,7},{8,8},{17,9},... | collective-permute-start | bytes 688136 | tf_op jit(solution)/shard_map/ppermute | solution.py:44
  12.4 26.4 %collective-permute-start.2 = (f32[4,56,256]{2,1,0:T(8,128)S(1)}, f32[4,56,256]{2,1,0:T(8,128)S(1)}, u32[]{:S(2)}, u32[]{:S(2)}) collective-permute-start(f32[4,56,256]{2,1,0:T(8,128)S(1)} %get-tuple-element.11.s0), channel_id=1, source_target_pairs={{192,0},{193,1},{194,2},{195,3},{196,4},{197,5},{198,6},{199,7},{2... | collective-permute-start | bytes 688136 | tf_op jit(solution)/shard_map/ppermute | solution.py:44
  14.0 24.8 %collective-permute-start.1 = (f32[4,56,256]{2,1,0:T(8,128)S(1)}, f32[4,56,256]{2,1,0:T(8,128)S(1)}, u32[]{:S(2)}, u32[]{:S(2)}) collective-permute-start(f32[4,56,256]{2,1,0:T(8,128)S(1)} %get-tuple-element.11.s0), channel_id=1, source_target_pairs={{128,0},{129,1},{130,2},{131,3},{132,4},{133,5},{134,6},{135,7},{1... | collective-permute-start | bytes 688136 | tf_op jit(solution)/shard_map/ppermute | solution.py:44
  16.9 21.9 %collective-permute-start = (f32[4,56,256]{2,1,0:T(8,128)S(1)}, f32[4,56,256]{2,1,0:T(8,128)S(1)}, u32[]{:S(2)}, u32[]{:S(2)}) collective-permute-start(f32[4,56,256]{2,1,0:T(8,128)S(1)} %get-tuple-element.11.s0), channel_id=1, source_target_pairs={{64,0},{65,1},{66,2},{67,3},{68,4},{69,5},{70,6},{71,7},{72,8},{73... | collective-permute-start | bytes 688136 | tf_op jit(solution)/shard_map/ppermute | solution.py:44
  18.3 20.5 %collective-permute-start.6 = (f32[4,56,256]{2,1,0:T(8,128)S(1)}, f32[4,56,256]{2,1,0:T(8,128)S(1)}, u32[]{:S(2)}, u32[]{:S(2)}) collective-permute-start(f32[4,56,256]{2,1,0:T(8,128)S(1)} %collective-permute-done.5.t2), channel_id=1, source_target_pairs={{4,0},{5,1},{6,2},{7,3},{0,4},{1,5},{2,6},{3,7},{12,8},{13,9},{14,... | collective-permute-start | bytes 688136 | tf_op jit(solution)/shard_map/ppermute | solution.py:44
  26.2 12.6 %collective-permute-start.4 = (f32[4,56,256]{2,1,0:T(8,128)S(1)}, f32[4,56,256]{2,1,0:T(8,128)S(1)}, u32[]{:S(2)}, u32[]{:S(2)}) collective-permute-start(f32[4,56,256]{2,1,0:T(8,128)S(1)} %collective-permute-done.3.t0), channel_id=1, source_target_pairs={{4,0},{5,1},{6,2},{7,3},{0,4},{1,5},{2,6},{3,7},{12,8},{13,9},{14,... | collective-permute-start | bytes 688136 | tf_op jit(solution)/shard_map/ppermute | solution.py:44
  79.6 8.6 %copy-start.1 = (f32[4,256]{1,0:T(4,128)S(1)}, f32[4,256]{1,0:T(4,128)}, u32[]{:S(2)}) copy-start(f32[4,256]{1,0:T(4,128)} %param.10) | copy-start | bytes 12292
  79.7 8.5 %collective-permute-start.7 = (f32[4,256]{1,0:T(4,128)S(1)}, f32[4,256]{1,0:T(4,128)S(1)}, u32[]{:S(2)}, u32[]{:S(2)}) collective-permute-start(f32[4,256]{1,0:T(4,128)S(1)} %multiply_add_fusion), channel_id=1, source_target_pairs={{0,0},{57,1},{50,2},{43,3},{4,4},{61,5},{54,6},{47,7},{8,8},{1,9},... | collective-permute-start | bytes 12296 | tf_op jit(solution)/shard_map/ppermute | solution.py:44

commit v4 on v3

v4 whole, which is shorter than its diff:
```python
import math

import jax
import jax.numpy as jnp
from jax import lax
from jax.experimental import pallas as pl
from jax.experimental.pallas import tpu as pltpu
from jax.sharding import PartitionSpec as P


EPSILON = 0.5
NEGATIVE = -1e30
LN2 = math.log(2.0)
SCALE = 1.0 / (EPSILON * LN2)

CL = 4
CELLS = 256
NY, NZ, NC, NX = 4, 8, 2, 4
AXES = ("own", "split")

FAR = NZ // 2

BLOCK = 64
DEPTH = 2 * BLOCK
SLOTS = 64
DEEP = 4
LIST = SLOTS + 16

f32, bf16 = jnp.float32, jnp.bfloat16


def device(x, y, z, c):
    return (((y % NY) * NZ + z % NZ) * NC + c % NC) * NX + x % NX


def fetched(value, source):
    pairs = [
        (device(*source(x, y, z, c)), device(x, y, z, c))
        for y in range(NY)
        for z in range(NZ)
        for c in range(NC)
        for x in range(NX)
    ]
    return lax.ppermute(value, AXES, pairs)


def from_x(value, k):
    return fetched(value, lambda x, y, z, c: (x + k, y, z, c))


def from_y(value, k):
    return fetched(value, lambda x, y, z, c: (x, y + k, z, c))


PLANES = [[device(x, y, z, c) for x in range(NX) for y in range(NY)] for z in range(NZ) for c in range(NC)]
MEMBERS = 16


def exchanged(value, groups):
    return lax.all_to_all(value, AXES, 0, 0, axis_index_groups=groups, tiled=True)


def from_core(value):
    return fetched(value, lambda x, y, z, c: (x, y, z, c + 1))


def three_parts(v):
    high = v.astype(bf16).astype(f32)
    rest = v - high
    middle = rest.astype(bf16).astype(f32)
    return high, middle, rest - middle


def place():
    own, x = lax.axis_index("own"), lax.axis_index("split")
    return x, own // (NZ * NC), (own // NC) % NZ, own % NC


def target_owners():
    x, y, z, c = place()
    row = y * (NZ * NC)
    near = row + ((z + x) % NZ) * NC
    far = row + ((z + x + NZ // 2) % NZ) * NC
    return near + c, near + 1 - c, far + c, far + 1 - c


def centre(ref):
    middle = jnp.mean(ref[0], axis=1, keepdims=True)
    return jnp.broadcast_to(middle, (56, CELLS))


def load_cluster(ref, a, middle):
    top = ref[a, 0:48, :] - middle[0:48]
    tail = ref[a, 48:56, :]
    row = lax.broadcasted_iota(jnp.int32, (8, CELLS), 0)
    extra = tail[2:3, :]
    tail = jnp.where(row < 2, tail - middle[48:56], 0.0)
    square = jnp.sum(top * top, axis=0, keepdims=True) + jnp.sum(tail * tail, axis=0, keepdims=True)
    return top, tail, extra, square


def with_rows(tail, first, second):
    row = lax.broadcasted_iota(jnp.int32, (8, CELLS), 0)
    for k in range(3):
        tail = jnp.where(row == 2 + k, first[k], tail)
        tail = jnp.where(row == 5 + k, second[k], tail)
    return tail


def store_operand(ref, n, top, tail, first, second):
    zeros = jnp.zeros((8, CELLS), f32)
    for part, (head, end) in enumerate(zip(three_parts(top)[:2], three_parts(tail)[:2])):
        end = with_rows(end, first, second) if part == 0 else end
        at = part * BLOCK
        ref[n, at : at + 48, :] = head.astype(bf16)
        ref[n, at + 48 : at + BLOCK, :] = jnp.concatenate([end, zeros], axis=0).astype(bf16)


def logsum(top, total):
    return jnp.where(total > 0.0, top + jnp.log2(total), NEGATIVE)


def merged(parts):
    top = parts[0]
    for part in parts[1:]:
        top = jnp.maximum(top, part)
    total = sum(jnp.exp2(part - top) for part in parts)
    return top + jnp.log2(total)


def over_pairs(count, list_ref, left_ref, right_ref, pick, top_ref, sum_ref, scores, tops):
    def multiply(n, k):
        pair = list_ref[n]
        left, right, _ = pick(pair >> 8, pair & 255)
        cells = left_ref[left]
        high, low = right_ref[right, 0:BLOCK, :], right_ref[right, BLOCK:DEPTH, :]
        e = jnp.dot(
            jnp.concatenate([cells, cells], axis=1),
            jnp.concatenate([high, high, low, low], axis=0),
            preferred_element_type=f32,
        )
        scores[k][...] = e
        tops[k][...] = jnp.max(e.reshape(CELLS // 8, 8, CELLS), axis=0)

    def absorb(n, k):
        pair = list_ref[n]
        _, _, place = pick(pair >> 8, pair & 255)
        top = tops[k][...]
        e = scores[k][...].reshape(CELLS // 8, 8, CELLS)
        total = jnp.sum(jnp.exp2(e - top[None]), axis=0)
        old = top_ref[place]
        new = jnp.maximum(old, top)
        sum_ref[place] = sum_ref[place] * jnp.exp2(old - new) + total * jnp.exp2(top - new)
        top_ref[place] = new

    def step(q, carry):
        absorb(4 * q + 0, 0)
        multiply(4 * q + 4, 0)
        absorb(4 * q + 1, 1)
        multiply(4 * q + 5, 1)
        absorb(4 * q + 2, 2)
        multiply(4 * q + 6, 2)
        absorb(4 * q + 3, 3)
        multiply(4 * q + 7, 3)
        return carry

    multiply(0, 0)
    multiply(1, 1)
    multiply(2, 2)
    multiply(3, 3)
    lax.fori_loop(0, (count + 3) // 4, step, 0)


def finish(top_ref, sum_ref):
    tops, sums = top_ref[0 : 4 * CL], sum_ref[0 : 4 * CL]
    top = jnp.max(tops, axis=1, keepdims=True)
    total = jnp.sum(sums * jnp.exp2(tops - top), axis=1)
    return logsum(top[:, 0, :], total)


def row_kernel(codes_in, s0, s1, s2, s3, t0, t1, t2, t3, out, list_out, xn, yn, mass, square_out, codes, list_ref, yt, top, tot, *rest):
    scores, tops, sem = rest[:DEEP], rest[DEEP : 2 * DEEP], rest[2 * DEEP]
    arriving = pltpu.make_async_copy(codes_in, codes, sem.at[0])
    arriving.start()
    one = jnp.ones((1, CELLS), f32)
    ones = (one, one, one)
    middle = centre(s0)
    for k, ref in enumerate((s0, s1, s2, s3)):
        for a in range(CL):
            head, tail, extra, square = load_cluster(ref, a, middle)
            mass[k * CL + a : k * CL + a + 1, :] = extra
            square_out[k * CL + a : k * CL + a + 1, :] = square
            weight = three_parts(-square * SCALE)
            store_operand(xn, k * CL + a, head * (2.0 * SCALE), tail * (2.0 * SCALE), weight, ones)
    top[...] = jnp.full(top.shape, NEGATIVE, f32)
    tot[...] = jnp.zeros(tot.shape, f32)
    arriving.wait()
    owners = target_owners()
    count = jnp.int32(0)
    y = place()[1]
    for k in range(4):
        for d in range(NX):
            for t in range(4):
                code = codes[d * NY + (y + k) % NY, owners[t]]
                source = k * CL + (code >> 2)
                list_ref[count] = source * 256 + t * CL + (code & 3)
                count = count + (code >= 0).astype(jnp.int32)
    for k in range(2 * DEEP):
        list_ref[count + k] = 4 * CL * 256
    list_ref[LIST - 1] = count
    leaving = pltpu.make_async_copy(list_ref, list_out, sem.at[1])
    leaving.start()
    xn[4 * CL] = jnp.zeros((DEPTH, CELLS), bf16)
    for k, ref in enumerate((t0, t1, t2, t3)):
        for a in range(CL):
            head, tail, prior, square = load_cluster(ref, a, middle)
            weight = three_parts((prior - square) * SCALE)
            store_operand(yn, k * CL + a, head, tail, ones, weight)
            yt[k * CL + a] = yn[k * CL + a].T
    over_pairs(count, list_ref, yt, xn, lambda s, t: (t, s, s), top, tot, scores, tops)
    rows = finish(top, tot).reshape(4, CL, CELLS)
    for k in range(4):
        for m in range(MEMBERS):
            out[m, (y + k) % NY] = rows[k]
    leaving.wait()


def column_kernel(list_in, came, mass, square, x_in, yn, kept, given, potential, list_ref, xn, xt, four, top, tot, *rest):
    scores, tops, sem = rest[:DEEP], rest[DEEP : 2 * DEEP], rest[2 * DEEP]
    arriving = pltpu.make_async_copy(list_in, list_ref, sem.at[0])
    arriving.start()
    y = place()[1]
    four[...] = merged([came[m] for m in range(MEMBERS)])
    row = lax.broadcasted_iota(jnp.int32, (16, CELLS), 0)
    for k in range(4):
        rows = four[(y + k) % NY]
        for a in range(CL):
            n = k * CL + a
            p = EPSILON * mass[n : n + 1, :] - (EPSILON * LN2) * rows[a : a + 1]
            if k == 0:
                potential[a : a + 1, :] = p
            weight = three_parts((p - square[n : n + 1, :]) * SCALE)
            xn[...] = x_in[n]
            end = xn[48:64, :].astype(f32)
            for part in range(3):
                end = jnp.where(row == 2 + part, weight[part], end)
            xn[48:64, :] = end.astype(bf16)
            xt[n] = xn[...].T
    xt[4 * CL] = jnp.zeros((CELLS, DEPTH), bf16)
    top[...] = jnp.full(top.shape, NEGATIVE, f32)
    tot[...] = jnp.zeros(tot.shape, f32)
    arriving.wait()

    def pick(s, t):
        return s, t, jnp.where(s == 4 * CL, 4 * CL, t)

    over_pairs(list_ref[LIST - 1], list_ref, xt, yn, pick, top, tot, scores, tops)
    columns = finish(top, tot)
    for k in range(2):
        kept[k * CL : (k + 1) * CL, :] = columns[2 * k * CL : (2 * k + 1) * CL]
        given[k * CL : (k + 1) * CL, :] = columns[(2 * k + 1) * CL : (2 * k + 2) * CL]


VMEM = pl.BlockSpec(memory_space=pltpu.VMEM)
ANY = pl.BlockSpec(memory_space=pl.ANY)


def work(source_coords, target_coords, source_logmass, target_logmass, target_prior, pair_source, pair_target):
    codes = pair_source * 4 + pair_target
    codes = jnp.where(pair_target >= 0, codes, -1).reshape(1, -1)
    codes = exchanged(jnp.broadcast_to(codes, (MEMBERS, codes.shape[1])), PLANES)

    def packed(coords, extra):
        zeros = jnp.zeros((CL, 5, CELLS), f32)
        return jnp.concatenate([coords, extra[:, None, :], zeros], axis=1)

    s0 = packed(source_coords, source_logmass)
    t = packed(target_coords, target_prior)
    t2 = fetched(t, lambda x, y, z, c: (x, y, z + x + FAR, c))
    t0 = fetched(t, lambda x, y, z, c: (x, y, z + x, c))
    s1, s2, s3 = (from_y(s0, k) for k in (1, 2, 3))
    t1, t3 = from_core(t0), from_core(t2)
    shards = (s0, s1, s2, s3, t0, t1, t2, t3)

    shared = (
        [pltpu.VMEM((4 * CL + 1, 8, CELLS), f32)] * 2
        + [pltpu.VMEM((CELLS, CELLS), f32)] * DEEP
        + [pltpu.VMEM((8, CELLS), f32)] * DEEP
        + [pltpu.SemaphoreType.DMA((2,))]
    )
    params = pltpu.CompilerParams(vmem_limit_bytes=16 * 2**20)
    rows, pairs, xn, yn, mass, square = pl.pallas_call(
        row_kernel,
        out_shape=(
            jax.ShapeDtypeStruct((MEMBERS, 4, CL, CELLS), f32),
            jax.ShapeDtypeStruct((LIST,), jnp.int32),
            jax.ShapeDtypeStruct((4 * CL + 1, DEPTH, CELLS), bf16),
            jax.ShapeDtypeStruct((4 * CL, DEPTH, CELLS), bf16),
            jax.ShapeDtypeStruct((4 * CL, CELLS), f32),
            jax.ShapeDtypeStruct((4 * CL, CELLS), f32),
        ),
        in_specs=[ANY] + [VMEM] * 8,
        out_specs=(VMEM, ANY, VMEM, VMEM, VMEM, VMEM),
        scratch_shapes=[
            pltpu.SMEM((MEMBERS, SLOTS), jnp.int32),
            pltpu.SMEM((LIST,), jnp.int32),
            pltpu.VMEM((4 * CL, CELLS, DEPTH), bf16),
        ]
        + shared,
        compiler_params=params,
        name="rows",
    )(codes, *shards)

    rows = exchanged(rows, PLANES)

    kept, given, source_potential = pl.pallas_call(
        column_kernel,
        out_shape=(
            jax.ShapeDtypeStruct((2 * CL, CELLS), f32),
            jax.ShapeDtypeStruct((2 * CL, CELLS), f32),
            jax.ShapeDtypeStruct((CL, CELLS), f32),
        ),
        in_specs=[ANY] + [VMEM] * 5,
        out_specs=(VMEM, VMEM, VMEM),
        scratch_shapes=[
            pltpu.SMEM((LIST,), jnp.int32),
            pltpu.VMEM((DEPTH, CELLS), bf16),
            pltpu.VMEM((4 * CL + 1, CELLS, DEPTH), bf16),
            pltpu.VMEM((4, CL, CELLS), f32),
        ]
        + shared,
        compiler_params=params,
        name="columns",
    )(pairs, rows, mass, square, xn, yn)

    kept = merged([kept, from_core(given)])
    first = fetched(kept[:CL], lambda x, y, z, c: (x, y, z - x, c))
    second = fetched(kept[CL:], lambda x, y, z, c: (x, y, z - x - FAR, c))
    part = merged([first, second])
    part = merged([part] + [from_x(part, k) for k in (1, 2, 3)])
    target_potential = EPSILON * target_logmass + target_prior - (EPSILON * LN2) * part
    return source_potential, target_potential


def solution(mesh):
    return jax.shard_map(
        work,
        mesh=mesh,
        in_specs=(
            P("own", None, None),
            P("own", None, None),
            P("own", None),
            P("own", None),
            P("own", None),
            P("own", "split", None, None),
            P("own", "split", None, None),
        ),
        out_specs=(P("own", None), P("own", None)),
        check_vma=False,
    )
```

time: 89.1 us -> 80.3 us (0.901)
  the two profiles are of different devices: /device:TPU:6 before, /device:TPU:64 now
where the time goes in v4:
time: 80.3 us; the launch traced here: 80 us
  blocking collectives  31.9 us (40%)
  starting transfers between devices  27.1 us (34%)
  waiting for transfers between devices  9.45 us (12%)
  Pallas kernels  6.53 us (8%)
  local copies, waits for them, and re-layouts  3.44 us (4%)
    all_to_all x2, blocking collectives, exchanged(): lax.all_to_all(value, AXES, 0, 0, axis_index_groups=groups, tiled=True)  31.9 us
    ppermute x13, starting transfers between devices, fetched(): return lax.ppermute(value, AXES, pairs)  27.1 us
    ppermute x13, waiting for transfers between devices, fetched(): return lax.ppermute(value, AXES, pairs)  9.45 us
    pallas_call x1, Pallas kernels, work(): pl.pallas_call(row_kernel, out_shape=(jax.ShapeDtypeStruct((MEMBERS, 4, C...  3.32 us
    pallas_call x1, Pallas kernels, work(): pl.pallas_call(column_kernel, out_shape=(jax.ShapeDtypeStruct((2 * CL, CE...  3.2 us
    unnamed x10, local copies, waits for them, and re-layouts  1.96 us
  transfers between devices with their start and end apart: 13, of which 4 were waited for; matrix products, arithmetic and copies ran while one was open for 0% of the time, Pallas kernels for 0%

profile of v4, /device:TPU:64, one launch (start us, length us, event | category | flops | bytes accessed | tf_op | source)
XLA Modules:
  0.0 80.0 jit_solution(3499842406230870854)
XLA Ops:
  0.7 0.7 broadcast_in_dim.20
  1.4 0.7 broadcast_in_dim.21
  2.0 1.0 %copy.11 = f32[4,50,256]{2,1,0:T(8,128)S(1)} copy(f32[4,50,256]{2,0,1:T(4,128)} %param.7) | data formatting | bytes 409600 | tf_op args[0]
  3.0 1.0 %copy.12 = f32[4,50,256]{2,1,0:T(8,128)S(1)} copy(f32[4,50,256]{2,0,1:T(4,128)} %param.8) | data formatting | bytes 409600 | tf_op args[1]
  4.2 5.5 %collective-permute-start.5 = (f32[4,56,256]{2,1,0:T(8,128)S(1)}, f32[4,56,256]{2,1,0:T(8,128)S(1)}, u32[]{:S(2)}, u32[]{:S(2)}) collective-permute-start(f32[4,56,256]{2,1,0:T(8,128)S(1)} %get-tuple-element.22), channel_id=1, source_target_pairs={{32,0},{41,1},{50,2},{59,3},{36,4},{45,5},{54,6},{63,7},{40,8},{49... | collective-permute-start | bytes 688136 | tf_op jit(solution)/shard_map/ppermute | solution.py:44
  9.7 0.7 collective-permute-start.3
  10.3 1.7 %collective-permute-start.2 = (f32[4,56,256]{2,1,0:T(8,128)S(1)}, f32[4,56,256]{2,1,0:T(8,128)S(1)}, u32[]{:S(2)}, u32[]{:S(2)}) collective-permute-start(f32[4,56,256]{2,1,0:T(8,128)S(1)} %get-tuple-element.23.s0), channel_id=1, source_target_pairs={{192,0},{193,1},{194,2},{195,3},{196,4},{197,5},{198,6},{199,7},{2... | collective-permute-start | bytes 688136 | tf_op jit(solution)/shard_map/ppermute | solution.py:44
  12.0 2.9 %collective-permute-start.1 = (f32[4,56,256]{2,1,0:T(8,128)S(1)}, f32[4,56,256]{2,1,0:T(8,128)S(1)}, u32[]{:S(2)}, u32[]{:S(2)}) collective-permute-start(f32[4,56,256]{2,1,0:T(8,128)S(1)} %get-tuple-element.23.s0), channel_id=1, source_target_pairs={{128,0},{129,1},{130,2},{131,3},{132,4},{133,5},{134,6},{135,7},{1... | collective-permute-start | bytes 688136 | tf_op jit(solution)/shard_map/ppermute | solution.py:44
  14.9 1.3 %collective-permute-start = (f32[4,56,256]{2,1,0:T(8,128)S(1)}, f32[4,56,256]{2,1,0:T(8,128)S(1)}, u32[]{:S(2)}, u32[]{:S(2)}) collective-permute-start(f32[4,56,256]{2,1,0:T(8,128)S(1)} %get-tuple-element.23.s0), channel_id=1, source_target_pairs={{64,0},{65,1},{66,2},{67,3},{68,4},{69,5},{70,6},{71,7},{72,8},{73... | collective-permute-start | bytes 688136 | tf_op jit(solution)/shard_map/ppermute | solution.py:44
  16.2 4.3 %collective-permute-done.5.t2 = f32[4,56,256]{2,1,0:T(8,128)S(1)} collective-permute-done((f32[4,56,256]{2,1,0:T(8,128)S(1)}, f32[4,56,256]{2,1,0:T(8,128)S(1)}, u32[]{:S(2)}, u32[]{:S(2)}) %collective-permute-start.5) | collective-permute-done | bytes 229408 | tf_op jit(solution)/shard_map/ppermute | solution.py:44
  20.6 0.5 collective-permute-start.4
  21.1 20.3 %all_to_all.13 = s32[16,1,64]{2,1,0:T(1,128)S(1)} all-to-all(s32[16,1,64]{2,1,0:T(1,128)S(1)} %broadcast_in_dim.19), channel_id=1, replica_groups={{0,64,128,192,1,65,129,193,2,66,130,194,3,67,131,195},{4,68,132,196,5,6..., dimensions={0} | all-to-all | bytes 8192 | tf_op jit(solution)/shard_map/all_to_all | solution.py:60
  41.4 3.3 %rows.1 = (f32[16,4,4,256]{3,2,1,0:T(4,128)S(1)}, s32[80]{0:T(128)S(1)}, bf16[17,128,256]{2,1,0:T(8,128)(2,1)S(1)}, bf16[16,128,256]{2,1,0:T(8,128)(2,1)S(1)}, f...) custom-call(s32[16,64]{1,0:T(8,128)S(1)} %bitcast.3, f32[4,56,256]{2,1,0:T(8,128)S(1)} %get-tuple-element.23.s0, ...), custom_call_target="tpu_custom_call" | custom-call | tf_op jit(solution)/shard_map/rows/pallas_call | solution.py:292
  44.8 11.6 %all_to_all.14.came = f32[16,4,4,256]{3,2,1,0:T(4,128)S(1)} all-to-all(f32[16,4,4,256]{3,2,1,0:T(4,128)S(1)} %get-tuple-element.12), channel_id=1, replica_groups={{0,64,128,192,1,65,129,193,2,66,130,194,3,67,131,195},{4,68,132,196,5,6..., dimensions={0} | all-to-all | bytes 524288 | tf_op jit(solution)/shard_map/all_to_all | solution.py:60
  56.4 3.2 %columns.1 = (f32[8,256]{1,0:T(8,128)S(1)}, f32[8,256]{1,0:T(8,128)S(1)}, f32[4,256]{1,0:T(4,128)}) custom-call(s32[80]{0:T(128)S(1)} %get-tuple-element.11.list_in, f32[16,4,4,256]{3,2,1,0:T(4,128)S(1)} %all_to_all.14.came, f32[16,256]{1,0:T(8,128)S(1)} %get-tuple-element.13.mass, f32[16,256]{1,0:T(8,128)S(1)} %get-tuple-element.14.square, ...), custom_call_target="tpu_custom_call" | custom-call | tf_op jit(solution)/shard_map/columns/pallas_call | solution.py:316
  59.7 1.2 %collective-permute-done.7 = f32[8,256]{1,0:T(8,128)S(1)} collective-permute-done((f32[8,256]{1,0:T(8,128)S(1)}, f32[8,256]{1,0:T(8,128)S(1)}, u32[]{:S(2)}, u32[]{:S(2)}) %collective-permute-start.7) | collective-permute-done | bytes 8224 | tf_op jit(solution)/shard_map/ppermute | solution.py:44
  60.9 0.7 collective-permute-start.8
  61.6 6.2 %collective-permute-start.9 = (f32[4,256]{1,0:T(4,128)S(1)}, f32[4,256]{1,0:T(4,128)S(1)}, u32[]{:S(2)}, u32[]{:S(2)}) collective-permute-start(f32[4,256]{1,0:T(4,128)S(1)} %get-tuple-element.21), channel_id=1, source_target_pairs={{32,0},{25,1},{18,2},{11,3},{36,4},{29,5},{22,6},{15,7},{40,8},{33... | collective-permute-start | bytes 12296 | tf_op jit(solution)/shard_map/ppermute | solution.py:44
  67.8 1.6 %collective-permute-done.9 = f32[4,256]{1,0:T(4,128)S(1)} collective-permute-done((f32[4,256]{1,0:T(4,128)S(1)}, f32[4,256]{1,0:T(4,128)S(1)}, u32[]{:S(2)}, u32[]{:S(2)}) %collective-permute-start.9) | collective-permute-done | bytes 4128 | tf_op jit(solution)/shard_map/ppermute | solution.py:44
  69.4 4.8 %collective-permute-start.12 = (f32[4,256]{1,0:T(4,128)S(1)}, f32[4,256]{1,0:T(4,128)S(1)}, u32[]{:S(2)}, u32[]{:S(2)}) collective-permute-start(f32[4,256]{1,0:T(4,128)S(1)} %multiply_add_fusion.1), channel_id=1, source_target_pairs={{3,0},{0,1},{1,2},{2,3},{7,4},{4,5},{5,6},{6,7},{11,8},{8,9},{9,10... | collective-permute-start | bytes 12296 | tf_op jit(solution)/shard_map/ppermute | solution.py:44
  74.2 0.2 collective-permute-start.11
  74.4 2.6 %collective-permute-start.10 = (f32[4,256]{1,0:T(4,128)S(1)}, f32[4,256]{1,0:T(4,128)S(1)}, u32[]{:S(2)}, u32[]{:S(2)}) collective-permute-start(f32[4,256]{1,0:T(4,128)S(1)} %multiply_add_fusion.1), channel_id=1, source_target_pairs={{1,0},{2,1},{3,2},{0,3},{5,4},{6,5},{7,6},{4,7},{9,8},{10,9},{11,1... | collective-permute-start | bytes 12296 | tf_op jit(solution)/shard_map/ppermute | solution.py:44
  77.0 2.3 %collective-permute-done.11 = f32[4,256]{1,0:T(4,128)S(1)} collective-permute-done((f32[4,256]{1,0:T(4,128)S(1)}, f32[4,256]{1,0:T(4,128)S(1)}, u32[]{:S(2)}, u32[]{:S(2)}) %collective-permute-start.11) | collective-permute-done | bytes 4128 | tf_op jit(solution)/shard_map/ppermute | solution.py:44
  79.4 0.6 multiply_subtract_fusion
  (27 shorter events, 0.4 us)
Async XLA Ops:
  0.6 20.5 %copy-start.2 = (s32[1,1,64,1]{2,3,1,0:T(1,128)S(1)}, s32[1,1,64,1]{2,3,1,0:T(1,128)}, u32[]{:S(2)}) copy-start(s32[1,1,64,1]{2,3,1,0:T(1,128)} %param.13) | copy-start | bytes 772
  0.6 20.5 %copy-start.3 = (s32[1,1,64,1]{2,3,1,0:T(1,128)S(1)}, s32[1,1,64,1]{2,3,1,0:T(1,128)}, u32[]{:S(2)}) copy-start(s32[1,1,64,1]{2,3,1,0:T(1,128)} %param.12) | copy-start | bytes 772
  4.2 16.4 %collective-permute-start.5 = (f32[4,56,256]{2,1,0:T(8,128)S(1)}, f32[4,56,256]{2,1,0:T(8,128)S(1)}, u32[]{:S(2)}, u32[]{:S(2)}) collective-permute-start(f32[4,56,256]{2,1,0:T(8,128)S(1)} %get-tuple-element.22), channel_id=1, source_target_pairs={{32,0},{41,1},{50,2},{59,3},{36,4},{45,5},{54,6},{63,7},{40,8},{49... | collective-permute-start | bytes 688136 | tf_op jit(solution)/shard_map/ppermute | solution.py:44
  9.7 10.9 %collective-permute-start.3 = (f32[4,56,256]{2,1,0:T(8,128)S(1)}, f32[4,56,256]{2,1,0:T(8,128)S(1)}, u32[]{:S(2)}, u32[]{:S(2)}) collective-permute-start(f32[4,56,256]{2,1,0:T(8,128)S(1)} %get-tuple-element.22), channel_id=1, source_target_pairs={{0,0},{9,1},{18,2},{27,3},{4,4},{13,5},{22,6},{31,7},{8,8},{17,9},... | collective-permute-start | bytes 688136 | tf_op jit(solution)/shard_map/ppermute | solution.py:44
  10.3 31.1 %collective-permute-start.2 = (f32[4,56,256]{2,1,0:T(8,128)S(1)}, f32[4,56,256]{2,1,0:T(8,128)S(1)}, u32[]{:S(2)}, u32[]{:S(2)}) collective-permute-start(f32[4,56,256]{2,1,0:T(8,128)S(1)} %get-tuple-element.23.s0), channel_id=1, source_target_pairs={{192,0},{193,1},{194,2},{195,3},{196,4},{197,5},{198,6},{199,7},{2... | collective-permute-start | bytes 688136 | tf_op jit(solution)/shard_map/ppermute | solution.py:44
  12.0 29.4 %collective-permute-start.1 = (f32[4,56,256]{2,1,0:T(8,128)S(1)}, f32[4,56,256]{2,1,0:T(8,128)S(1)}, u32[]{:S(2)}, u32[]{:S(2)}) collective-permute-start(f32[4,56,256]{2,1,0:T(8,128)S(1)} %get-tuple-element.23.s0), channel_id=1, source_target_pairs={{128,0},{129,1},{130,2},{131,3},{132,4},{133,5},{134,6},{135,7},{1... | collective-permute-start | bytes 688136 | tf_op jit(solution)/shard_map/ppermute | solution.py:44
  14.9 26.5 %collective-permute-start = (f32[4,56,256]{2,1,0:T(8,128)S(1)}, f32[4,56,256]{2,1,0:T(8,128)S(1)}, u32[]{:S(2)}, u32[]{:S(2)}) collective-permute-start(f32[4,56,256]{2,1,0:T(8,128)S(1)} %get-tuple-element.23.s0), channel_id=1, source_target_pairs={{64,0},{65,1},{66,2},{67,3},{68,4},{69,5},{70,6},{71,7},{72,8},{73... | collective-permute-start | bytes 688136 | tf_op jit(solution)/shard_map/ppermute | solution.py:44
  20.6 20.8 %collective-permute-start.6 = (f32[4,56,256]{2,1,0:T(8,128)S(1)}, f32[4,56,256]{2,1,0:T(8,128)S(1)}, u32[]{:S(2)}, u32[]{:S(2)}) collective-permute-start(f32[4,56,256]{2,1,0:T(8,128)S(1)} %collective-permute-done.5.t2), channel_id=1, source_target_pairs={{4,0},{5,1},{6,2},{7,3},{0,4},{1,5},{2,6},{3,7},{12,8},{13,9},{14,... | collective-permute-start | bytes 688136 | tf_op jit(solution)/shard_map/ppermute | solution.py:44
  20.6 20.8 %collective-permute-start.4 = (f32[4,56,256]{2,1,0:T(8,128)S(1)}, f32[4,56,256]{2,1,0:T(8,128)S(1)}, u32[]{:S(2)}, u32[]{:S(2)}) collective-permute-start(f32[4,56,256]{2,1,0:T(8,128)S(1)} %collective-permute-done.3.t0), channel_id=1, source_target_pairs={{4,0},{5,1},{6,2},{7,3},{0,4},{1,5},{2,6},{3,7},{12,8},{13,9},{14,... | collective-permute-start | bytes 688136 | tf_op jit(solution)/shard_map/ppermute | solution.py:44
  56.4 22.9 %copy-start = (f32[4,256]{1,0:T(4,128)S(1)}, f32[4,256]{1,0:T(4,128)}, u32[]{:S(2)}) copy-start(f32[4,256]{1,0:T(4,128)} %param.11) | copy-start | bytes 12292
  56.4 22.9 %copy-start.1 = (f32[4,256]{1,0:T(4,128)S(1)}, f32[4,256]{1,0:T(4,128)}, u32[]{:S(2)}) copy-start(f32[4,256]{1,0:T(4,128)} %param.10) | copy-start | bytes 12292
  59.6 1.3 %collective-permute-start.7 = (f32[8,256]{1,0:T(8,128)S(1)}, f32[8,256]{1,0:T(8,128)S(1)}, u32[]{:S(2)}, u32[]{:S(2)}) collective-permute-start(f32[8,256]{1,0:T(8,128)S(1)} %get-tuple-element.19), channel_id=1, source_target_pairs={{4,0},{5,1},{6,2},{7,3},{0,4},{1,5},{2,6},{3,7},{12,8},{13,9},{14,... | collective-permute-start | bytes 24584 | tf_op jit(solution)/shard_map/ppermute | solution.py:44
  60.9 6.9 %collective-permute-start.8 = (f32[4,256]{1,0:T(4,128)S(1)}, f32[4,256]{1,0:T(4,128)S(1)}, u32[]{:S(2)}, u32[]{:S(2)}) collective-permute-start(f32[4,256]{1,0:T(4,128)S(1)} %get-tuple-element.20), channel_id=1, source_target_pairs={{0,0},{57,1},{50,2},{43,3},{4,4},{61,5},{54,6},{47,7},{8,8},{1,9},... | collective-permute-start | bytes 12296 | tf_op jit(solution)/shard_map/ppermute | solution.py:44
  61.6 7.8 %collective-permute-start.9 = (f32[4,256]{1,0:T(4,128)S(1)}, f32[4,256]{1,0:T(4,128)S(1)}, u32[]{:S(2)}, u32[]{:S(2)}) collective-permute-start(f32[4,256]{1,0:T(4,128)S(1)} %get-tuple-element.21), channel_id=1, source_target_pairs={{32,0},{25,1},{18,2},{11,3},{36,4},{29,5},{22,6},{15,7},{40,8},{33... | collective-permute-start | bytes 12296 | tf_op jit(solution)/shard_map/ppermute | solution.py:44
  69.4 7.6 %collective-permute-start.12 = (f32[4,256]{1,0:T(4,128)S(1)}, f32[4,256]{1,0:T(4,128)S(1)}, u32[]{:S(2)}, u32[]{:S(2)}) collective-permute-start(f32[4,256]{1,0:T(4,128)S(1)} %multiply_add_fusion.1), channel_id=1, source_target_pairs={{3,0},{0,1},{1,2},{2,3},{7,4},{4,5},{5,6},{6,7},{11,8},{8,9},{9,10... | collective-permute-start | bytes 12296 | tf_op jit(solution)/shard_map/ppermute | solution.py:44
  74.2 5.1 %collective-permute-start.11 = (f32[4,256]{1,0:T(4,128)S(1)}, f32[4,256]{1,0:T(4,128)S(1)}, u32[]{:S(2)}, u32[]{:S(2)}) collective-permute-start(f32[4,256]{1,0:T(4,128)S(1)} %multiply_add_fusion.1), channel_id=1, source_target_pairs={{2,0},{3,1},{0,2},{1,3},{6,4},{7,5},{4,6},{5,7},{10,8},{11,9},{8,1... | collective-permute-start | bytes 12296 | tf_op jit(solution)/shard_map/ppermute | solution.py:44
  74.4 4.9 %collective-permute-start.10 = (f32[4,256]{1,0:T(4,128)S(1)}, f32[4,256]{1,0:T(4,128)S(1)}, u32[]{:S(2)}, u32[]{:S(2)}) collective-permute-start(f32[4,256]{1,0:T(4,128)S(1)} %multiply_add_fusion.1), channel_id=1, source_target_pairs={{1,0},{2,1},{3,2},{0,3},{5,4},{6,5},{7,6},{4,7},{9,8},{10,9},{11,1... | collective-permute-start | bytes 12296 | tf_op jit(solution)/shard_map/ppermute | solution.py:44

commit v5 on v4

--- a/solution.py
+++ b/solution.py
@@ -13,8 +13,10 @@
 LN2 = math.log(2.0)
 SCALE = 1.0 / (EPSILON * LN2)
 
+COMP = 50
 CL = 4
 CELLS = 256
+PACKED = 56
 NY, NZ, NC, NX = 4, 8, 2, 4
 AXES = ("own", "split")
 
@@ -86,12 +88,12 @@
 
 def centre(ref):
     middle = jnp.mean(ref[0], axis=1, keepdims=True)
-    return jnp.broadcast_to(middle, (56, CELLS))
+    return jnp.broadcast_to(middle, (PACKED, CELLS))
 
 
 def load_cluster(ref, a, middle):
     top = ref[a, 0:48, :] - middle[0:48]
-    tail = ref[a, 48:56, :]
+    tail = ref[a, 48:PACKED, :]
     row = lax.broadcasted_iota(jnp.int32, (8, CELLS), 0)
     extra = tail[2:3, :]
     tail = jnp.where(row < 2, tail - middle[48:56], 0.0)
@@ -176,6 +178,29 @@
     top = jnp.max(tops, axis=1, keepdims=True)
     total = jnp.sum(sums * jnp.exp2(tops - top), axis=1)
     return logsum(top[:, 0, :], total)
+
+
+def pack_kernel(cells_in, extra_in, more_cells_in, more_extra_in, out, more_out, cells, more_cells, extra, more_extra, sem):
+    copies = [
+        pltpu.make_async_copy(a, b, sem.at[k])
+        for k, (a, b) in enumerate(
+            (
+                (cells_in, cells),
+                (extra_in, extra),
+                (more_cells_in, more_cells),
+                (more_extra_in, more_extra),
+            )
+        )
+    ]
+    for copy in copies:
+        copy.start()
+    for k, (a, b, o) in enumerate(((cells, extra, out), (more_cells, more_extra, more_out))):
+        copies[2 * k].wait()
+        copies[2 * k + 1].wait()
+        for n in range(CL):
+            o[n, 0:COMP, :] = a[:, n, :]
+            o[n, COMP : COMP + 1, :] = b[n : n + 1, :]
+            o[n, COMP + 1 : PACKED, :] = jnp.zeros((PACKED - COMP - 1, CELLS), f32)
 
 
 def row_kernel(codes_in, s0, s1, s2, s3, t0, t1, t2, t3, out, list_out, xn, yn, mass, square_out, codes, list_ref, yt, top, tot, *rest):
@@ -263,6 +288,7 @@
 
 VMEM = pl.BlockSpec(memory_space=pltpu.VMEM)
 ANY = pl.BlockSpec(memory_space=pl.ANY)
+HBM = pl.BlockSpec(memory_space=pltpu.HBM)
 
 
 def work(source_coords, target_coords, source_logmass, target_logmass, target_prior, pair_source, pair_target):
@@ -270,12 +296,27 @@
     codes = jnp.where(pair_target >= 0, codes, -1).reshape(1, -1)
     codes = exchanged(jnp.broadcast_to(codes, (MEMBERS, codes.shape[1])), PLANES)
 
-    def packed(coords, extra):
-        zeros = jnp.zeros((CL, 5, CELLS), f32)
-        return jnp.concatenate([coords, extra[:, None, :], zeros], axis=1)
-
-    s0 = packed(source_coords, source_logmass)
-    t = packed(target_coords, target_prior)
+    cells = jax.ShapeDtypeStruct((CL, PACKED, CELLS), f32)
+    loose = pltpu.VMEM((COMP, CL, CELLS), f32)
+    t, s0 = pl.pallas_call(
+        pack_kernel,
+        out_shape=(cells, cells),
+        in_specs=[HBM] * 4,
+        out_specs=(VMEM, VMEM),
+        scratch_shapes=[loose, loose] + [pltpu.VMEM((CL, CELLS), f32)] * 2 + [pltpu.SemaphoreType.DMA((4,))],
+        compiler_params=pltpu.CompilerParams(vmem_limit_bytes=4 * 2**20),
+        name="pack",
+    )(
+        *(
+            pltpu.with_memory_space_constraint(value, pltpu.HBM)
+            for value in (
+                jnp.transpose(target_coords, (1, 0, 2)),
+                target_prior,
+                jnp.transpose(source_coords, (1, 0, 2)),
+                source_logmass,
+            )
+        )
+    )
     t2 = fetched(t, lambda x, y, z, c: (x, y, z + x + FAR, c))
     t0 = fetched(t, lambda x, y, z, c: (x, y, z + x, c))
     s1, s2, s3 = (from_y(s0, k) for k in (1, 2, 3))

time: 80.3 us -> 78.5 us (0.978)
  local copies, waits for them, and re-layouts: 3.44 us -> 0.02 us
  Pallas kernels: 6.53 us -> 7.67 us
    unnamed x10 -> x4, local copies, waits for them, and re-layouts: 1.96 us -> 0.01 us
    broadcast_in_dim x2 -> x0, local copies, waits for them, and re-layouts: 1.39 us -> none  [packed(): return jnp.concatenate([coords, extra[:, None, :], zeros], axis=1)]
    pallas_call x0 -> x1, Pallas kernels: none -> 1.15 us  [work(): pl.pallas_call(pack_kernel, out_shape=(cells, cells), in_specs=[HBM] * 4,...]
  transfers between devices with their start and end apart: 13 -> 13, of which waited for: 4 -> 4; matrix products, arithmetic and copies ran while one was open for 0% -> 1% of each run, Pallas kernels for 0% -> 0%
where the time goes in v5:
time: 78.5 us; the launch traced here: 78.2 us
  blocking collectives  31.9 us (41%)
  starting transfers between devices  27.1 us (35%)
  waiting for transfers between devices  9.45 us (12%)
  Pallas kernels  7.67 us (10%)
  other arithmetic  1.33 us (2%)
    all_to_all x2, blocking collectives, exchanged(): lax.all_to_all(value, AXES, 0, 0, axis_index_groups=groups, tiled=True)  31.9 us
    ppermute x13, starting transfers between devices, fetched(): return lax.ppermute(value, AXES, pairs)  27.1 us
    ppermute x13, waiting for transfers between devices, fetched(): return lax.ppermute(value, AXES, pairs)  9.45 us
    pallas_call x1, Pallas kernels, work(): pl.pallas_call(row_kernel, out_shape=(jax.ShapeDtypeStruct((MEMBERS, 4, C...  3.32 us
    pallas_call x1, Pallas kernels, work(): pl.pallas_call(column_kernel, out_shape=(jax.ShapeDtypeStruct((2 * CL, CE...  3.2 us
  transfers between devices with their start and end apart: 13, of which 4 were waited for; matrix products, arithmetic and copies ran while one was open for 1% of the time, Pallas kernels for 0%

profile of v5, /device:TPU:64, one launch (start us, length us, event | category | flops | bytes accessed | tf_op | source)
XLA Modules:
  0.0 78.2 jit_solution(10134452574199979790)
XLA Ops:
  0.6 1.2 %pack.1 = (f32[4,56,256]{2,1,0:T(8,128)S(1)}, f32[4,56,256]{2,1,0:T(8,128)S(1)}) custom-call(f32[50,4,256]{2,1,0:T(4,128)} %bitcast.6, f32[4,256]{1,0:T(4,128)} %extra_in.1, f32[50,4,256]{2,1,0:T(4,128)} %bitcast.7, f32[4,256]{1,0:T(4,128)} %more_extra_in.1), custom_call_target="tpu_custom_call" | custom-call | tf_op jit(solution)/shard_map/pack/pallas_call | solution.py:301
  1.8 5.5 %collective-permute-start.5 = (f32[4,56,256]{2,1,0:T(8,128)S(1)}, f32[4,56,256]{2,1,0:T(8,128)S(1)}, u32[]{:S(2)}, u32[]{:S(2)}) collective-permute-start(f32[4,56,256]{2,1,0:T(8,128)S(1)} %get-tuple-element.14), channel_id=1, source_target_pairs={{32,0},{41,1},{50,2},{59,3},{36,4},{45,5},{54,6},{63,7},{40,8},{49... | collective-permute-start | bytes 688136 | tf_op jit(solution)/shard_map/ppermute | solution.py:46
  7.3 0.7 collective-permute-start.3
  7.9 1.7 %collective-permute-start.2 = (f32[4,56,256]{2,1,0:T(8,128)S(1)}, f32[4,56,256]{2,1,0:T(8,128)S(1)}, u32[]{:S(2)}, u32[]{:S(2)}) collective-permute-start(f32[4,56,256]{2,1,0:T(8,128)S(1)} %get-tuple-element.13.s0), channel_id=1, source_target_pairs={{192,0},{193,1},{194,2},{195,3},{196,4},{197,5},{198,6},{199,7},{2... | collective-permute-start | bytes 688136 | tf_op jit(solution)/shard_map/ppermute | solution.py:46
  9.6 2.9 %collective-permute-start.1 = (f32[4,56,256]{2,1,0:T(8,128)S(1)}, f32[4,56,256]{2,1,0:T(8,128)S(1)}, u32[]{:S(2)}, u32[]{:S(2)}) collective-permute-start(f32[4,56,256]{2,1,0:T(8,128)S(1)} %get-tuple-element.13.s0), channel_id=1, source_target_pairs={{128,0},{129,1},{130,2},{131,3},{132,4},{133,5},{134,6},{135,7},{1... | collective-permute-start | bytes 688136 | tf_op jit(solution)/shard_map/ppermute | solution.py:46
  12.5 1.3 %collective-permute-start = (f32[4,56,256]{2,1,0:T(8,128)S(1)}, f32[4,56,256]{2,1,0:T(8,128)S(1)}, u32[]{:S(2)}, u32[]{:S(2)}) collective-permute-start(f32[4,56,256]{2,1,0:T(8,128)S(1)} %get-tuple-element.13.s0), channel_id=1, source_target_pairs={{64,0},{65,1},{66,2},{67,3},{68,4},{69,5},{70,6},{71,7},{72,8},{73... | collective-permute-start | bytes 688136 | tf_op jit(solution)/shard_map/ppermute | solution.py:46
  13.8 4.3 %collective-permute-done.5.t2 = f32[4,56,256]{2,1,0:T(8,128)S(1)} collective-permute-done((f32[4,56,256]{2,1,0:T(8,128)S(1)}, f32[4,56,256]{2,1,0:T(8,128)S(1)}, u32[]{:S(2)}, u32[]{:S(2)}) %collective-permute-start.5) | collective-permute-done | bytes 229408 | tf_op jit(solution)/shard_map/ppermute | solution.py:46
  18.2 0.0 collective-permute-done.3.t0
  18.2 0.5 collective-permute-start.4
  18.7 0.7 fusion.4
  19.4 20.3 %all_to_all.13 = s32[16,1,64]{2,1,0:T(1,128)S(1)} all-to-all(s32[16,1,64]{2,1,0:T(1,128)S(1)} %broadcast_in_dim.13), channel_id=1, replica_groups={{0,64,128,192,1,65,129,193,2,66,130,194,3,67,131,195},{4,68,132,196,5,6..., dimensions={0} | all-to-all | bytes 8192 | tf_op jit(solution)/shard_map/all_to_all | solution.py:62
  39.7 3.3 %rows.1 = (f32[16,4,4,256]{3,2,1,0:T(4,128)S(1)}, s32[80]{0:T(128)S(1)}, bf16[17,128,256]{2,1,0:T(8,128)(2,1)S(1)}, bf16[16,128,256]{2,1,0:T(8,128)(2,1)S(1)}, f...) custom-call(s32[16,64]{1,0:T(8,128)S(1)} %bitcast.5, f32[4,56,256]{2,1,0:T(8,128)S(1)} %get-tuple-element.13.s0, ...), custom_call_target="tpu_custom_call" | custom-call | tf_op jit(solution)/shard_map/rows/pallas_call | solution.py:333
  43.0 11.7 %all_to_all.14.came = f32[16,4,4,256]{3,2,1,0:T(4,128)S(1)} all-to-all(f32[16,4,4,256]{3,2,1,0:T(4,128)S(1)} %get-tuple-element.16), channel_id=1, replica_groups={{0,64,128,192,1,65,129,193,2,66,130,194,3,67,131,195},{4,68,132,196,5,6..., dimensions={0} | all-to-all | bytes 524288 | tf_op jit(solution)/shard_map/all_to_all | solution.py:62
  54.7 3.2 %columns.1 = (f32[8,256]{1,0:T(8,128)S(1)}, f32[8,256]{1,0:T(8,128)S(1)}, f32[4,256]{1,0:T(4,128)}) custom-call(s32[80]{0:T(128)S(1)} %get-tuple-element.15.list_in, f32[16,4,4,256]{3,2,1,0:T(4,128)S(1)} %all_to_all.14.came, f32[16,256]{1,0:T(8,128)S(1)} %get-tuple-element.17.mass, f32[16,256]{1,0:T(8,128)S(1)} %get-tuple-element.18.square, ...), custom_call_target="tpu_custom_call" | custom-call | tf_op jit(solution)/shard_map/columns/pallas_call | solution.py:357
  57.9 0.1 collective-permute-start.7
  58.0 1.2 %collective-permute-done.7 = f32[8,256]{1,0:T(8,128)S(1)} collective-permute-done((f32[8,256]{1,0:T(8,128)S(1)}, f32[8,256]{1,0:T(8,128)S(1)}, u32[]{:S(2)}, u32[]{:S(2)}) %collective-permute-start.7) | collective-permute-done | bytes 8224 | tf_op jit(solution)/shard_map/ppermute | solution.py:46
  59.2 0.7 collective-permute-start.8
  59.8 6.2 %collective-permute-start.9 = (f32[4,256]{1,0:T(4,128)S(1)}, f32[4,256]{1,0:T(4,128)S(1)}, u32[]{:S(2)}, u32[]{:S(2)}) collective-permute-start(f32[4,256]{1,0:T(4,128)S(1)} %get-tuple-element.25), channel_id=1, source_target_pairs={{32,0},{25,1},{18,2},{11,3},{36,4},{29,5},{22,6},{15,7},{40,8},{33... | collective-permute-start | bytes 12296 | tf_op jit(solution)/shard_map/ppermute | solution.py:46
  66.1 1.6 %collective-permute-done.9 = f32[4,256]{1,0:T(4,128)S(1)} collective-permute-done((f32[4,256]{1,0:T(4,128)S(1)}, f32[4,256]{1,0:T(4,128)S(1)}, u32[]{:S(2)}, u32[]{:S(2)}) %collective-permute-start.9) | collective-permute-done | bytes 4128 | tf_op jit(solution)/shard_map/ppermute | solution.py:46
  67.7 4.8 %collective-permute-start.12 = (f32[4,256]{1,0:T(4,128)S(1)}, f32[4,256]{1,0:T(4,128)S(1)}, u32[]{:S(2)}, u32[]{:S(2)}) collective-permute-start(f32[4,256]{1,0:T(4,128)S(1)} %multiply_add_fusion.1), channel_id=1, source_target_pairs={{3,0},{0,1},{1,2},{2,3},{7,4},{4,5},{5,6},{6,7},{11,8},{8,9},{9,10... | collective-permute-start | bytes 12296 | tf_op jit(solution)/shard_map/ppermute | solution.py:46
  72.5 0.2 collective-permute-start.11
  72.7 2.6 %collective-permute-start.10 = (f32[4,256]{1,0:T(4,128)S(1)}, f32[4,256]{1,0:T(4,128)S(1)}, u32[]{:S(2)}, u32[]{:S(2)}) collective-permute-start(f32[4,256]{1,0:T(4,128)S(1)} %multiply_add_fusion.1), channel_id=1, source_target_pairs={{1,0},{2,1},{3,2},{0,3},{5,4},{6,5},{7,6},{4,7},{9,8},{10,9},{11,1... | collective-permute-start | bytes 12296 | tf_op jit(solution)/shard_map/ppermute | solution.py:46
  75.3 2.3 %collective-permute-done.11 = f32[4,256]{1,0:T(4,128)S(1)} collective-permute-done((f32[4,256]{1,0:T(4,128)S(1)}, f32[4,256]{1,0:T(4,128)S(1)}, u32[]{:S(2)}, u32[]{:S(2)}) %collective-permute-start.11) | collective-permute-done | bytes 4128 | tf_op jit(solution)/shard_map/ppermute | solution.py:46
  77.6 0.6 multiply_subtract_fusion
  (17 shorter events, 0.1 us)
Async XLA Ops:
  1.8 16.4 %collective-permute-start.5 = (f32[4,56,256]{2,1,0:T(8,128)S(1)}, f32[4,56,256]{2,1,0:T(8,128)S(1)}, u32[]{:S(2)}, u32[]{:S(2)}) collective-permute-start(f32[4,56,256]{2,1,0:T(8,128)S(1)} %get-tuple-element.14), channel_id=1, source_target_pairs={{32,0},{41,1},{50,2},{59,3},{36,4},{45,5},{54,6},{63,7},{40,8},{49... | collective-permute-start | bytes 688136 | tf_op jit(solution)/shard_map/ppermute | solution.py:46
  7.3 10.9 %collective-permute-start.3 = (f32[4,56,256]{2,1,0:T(8,128)S(1)}, f32[4,56,256]{2,1,0:T(8,128)S(1)}, u32[]{:S(2)}, u32[]{:S(2)}) collective-permute-start(f32[4,56,256]{2,1,0:T(8,128)S(1)} %get-tuple-element.14), channel_id=1, source_target_pairs={{0,0},{9,1},{18,2},{27,3},{4,4},{13,5},{22,6},{31,7},{8,8},{17,9},... | collective-permute-start | bytes 688136 | tf_op jit(solution)/shard_map/ppermute | solution.py:46
  7.9 31.7 %collective-permute-start.2 = (f32[4,56,256]{2,1,0:T(8,128)S(1)}, f32[4,56,256]{2,1,0:T(8,128)S(1)}, u32[]{:S(2)}, u32[]{:S(2)}) collective-permute-start(f32[4,56,256]{2,1,0:T(8,128)S(1)} %get-tuple-element.13.s0), channel_id=1, source_target_pairs={{192,0},{193,1},{194,2},{195,3},{196,4},{197,5},{198,6},{199,7},{2... | collective-permute-start | bytes 688136 | tf_op jit(solution)/shard_map/ppermute | solution.py:46
  9.6 30.1 %collective-permute-start.1 = (f32[4,56,256]{2,1,0:T(8,128)S(1)}, f32[4,56,256]{2,1,0:T(8,128)S(1)}, u32[]{:S(2)}, u32[]{:S(2)}) collective-permute-start(f32[4,56,256]{2,1,0:T(8,128)S(1)} %get-tuple-element.13.s0), channel_id=1, source_target_pairs={{128,0},{129,1},{130,2},{131,3},{132,4},{133,5},{134,6},{135,7},{1... | collective-permute-start | bytes 688136 | tf_op jit(solution)/shard_map/ppermute | solution.py:46
  12.5 27.2 %collective-permute-start = (f32[4,56,256]{2,1,0:T(8,128)S(1)}, f32[4,56,256]{2,1,0:T(8,128)S(1)}, u32[]{:S(2)}, u32[]{:S(2)}) collective-permute-start(f32[4,56,256]{2,1,0:T(8,128)S(1)} %get-tuple-element.13.s0), channel_id=1, source_target_pairs={{64,0},{65,1},{66,2},{67,3},{68,4},{69,5},{70,6},{71,7},{72,8},{73... | collective-permute-start | bytes 688136 | tf_op jit(solution)/shard_map/ppermute | solution.py:46
  18.2 21.5 %collective-permute-start.6 = (f32[4,56,256]{2,1,0:T(8,128)S(1)}, f32[4,56,256]{2,1,0:T(8,128)S(1)}, u32[]{:S(2)}, u32[]{:S(2)}) collective-permute-start(f32[4,56,256]{2,1,0:T(8,128)S(1)} %collective-permute-done.5.t2), channel_id=1, source_target_pairs={{4,0},{5,1},{6,2},{7,3},{0,4},{1,5},{2,6},{3,7},{12,8},{13,9},{14,... | collective-permute-start | bytes 688136 | tf_op jit(solution)/shard_map/ppermute | solution.py:46
  18.2 21.5 %collective-permute-start.4 = (f32[4,56,256]{2,1,0:T(8,128)S(1)}, f32[4,56,256]{2,1,0:T(8,128)S(1)}, u32[]{:S(2)}, u32[]{:S(2)}) collective-permute-start(f32[4,56,256]{2,1,0:T(8,128)S(1)} %collective-permute-done.3.t0), channel_id=1, source_target_pairs={{4,0},{5,1},{6,2},{7,3},{0,4},{1,5},{2,6},{3,7},{12,8},{13,9},{14,... | collective-permute-start | bytes 688136 | tf_op jit(solution)/shard_map/ppermute | solution.py:46
  54.7 22.9 %copy-start = (f32[4,256]{1,0:T(4,128)S(1)}, f32[4,256]{1,0:T(4,128)}, u32[]{:S(2)}) copy-start(f32[4,256]{1,0:T(4,128)} %extra_in.1) | copy-start | bytes 12292
  54.7 22.9 %copy-start.1 = (f32[4,256]{1,0:T(4,128)S(1)}, f32[4,256]{1,0:T(4,128)}, u32[]{:S(2)}) copy-start(f32[4,256]{1,0:T(4,128)} %param.10) | copy-start | bytes 12292
  57.9 1.3 %collective-permute-start.7 = (f32[8,256]{1,0:T(8,128)S(1)}, f32[8,256]{1,0:T(8,128)S(1)}, u32[]{:S(2)}, u32[]{:S(2)}) collective-permute-start(f32[8,256]{1,0:T(8,128)S(1)} %get-tuple-element.23), channel_id=1, source_target_pairs={{4,0},{5,1},{6,2},{7,3},{0,4},{1,5},{2,6},{3,7},{12,8},{13,9},{14,... | collective-permute-start | bytes 24584 | tf_op jit(solution)/shard_map/ppermute | solution.py:46
  59.2 6.9 %collective-permute-start.8 = (f32[4,256]{1,0:T(4,128)S(1)}, f32[4,256]{1,0:T(4,128)S(1)}, u32[]{:S(2)}, u32[]{:S(2)}) collective-permute-start(f32[4,256]{1,0:T(4,128)S(1)} %get-tuple-element.24), channel_id=1, source_target_pairs={{0,0},{57,1},{50,2},{43,3},{4,4},{61,5},{54,6},{47,7},{8,8},{1,9},... | collective-permute-start | bytes 12296 | tf_op jit(solution)/shard_map/ppermute | solution.py:46
  59.8 7.8 %collective-permute-start.9 = (f32[4,256]{1,0:T(4,128)S(1)}, f32[4,256]{1,0:T(4,128)S(1)}, u32[]{:S(2)}, u32[]{:S(2)}) collective-permute-start(f32[4,256]{1,0:T(4,128)S(1)} %get-tuple-element.25), channel_id=1, source_target_pairs={{32,0},{25,1},{18,2},{11,3},{36,4},{29,5},{22,6},{15,7},{40,8},{33... | collective-permute-start | bytes 12296 | tf_op jit(solution)/shard_map/ppermute | solution.py:46
  67.7 7.6 %collective-permute-start.12 = (f32[4,256]{1,0:T(4,128)S(1)}, f32[4,256]{1,0:T(4,128)S(1)}, u32[]{:S(2)}, u32[]{:S(2)}) collective-permute-start(f32[4,256]{1,0:T(4,128)S(1)} %multiply_add_fusion.1), channel_id=1, source_target_pairs={{3,0},{0,1},{1,2},{2,3},{7,4},{4,5},{5,6},{6,7},{11,8},{8,9},{9,10... | collective-permute-start | bytes 12296 | tf_op jit(solution)/shard_map/ppermute | solution.py:46
  72.5 5.1 %collective-permute-start.11 = (f32[4,256]{1,0:T(4,128)S(1)}, f32[4,256]{1,0:T(4,128)S(1)}, u32[]{:S(2)}, u32[]{:S(2)}) collective-permute-start(f32[4,256]{1,0:T(4,128)S(1)} %multiply_add_fusion.1), channel_id=1, source_target_pairs={{2,0},{3,1},{0,2},{1,3},{6,4},{7,5},{4,6},{5,7},{10,8},{11,9},{8,1... | collective-permute-start | bytes 12296 | tf_op jit(solution)/shard_map/ppermute | solution.py:46
  72.7 4.9 %collective-permute-start.10 = (f32[4,256]{1,0:T(4,128)S(1)}, f32[4,256]{1,0:T(4,128)S(1)}, u32[]{:S(2)}, u32[]{:S(2)}) collective-permute-start(f32[4,256]{1,0:T(4,128)S(1)} %multiply_add_fusion.1), channel_id=1, source_target_pairs={{1,0},{2,1},{3,2},{0,3},{5,4},{6,5},{7,6},{4,7},{9,8},{10,9},{11,1... | collective-permute-start | bytes 12296 | tf_op jit(solution)/shard_map/ppermute | solution.py:46

commit v6 on v5

--- a/solution.py
+++ b/solution.py
@@ -16,7 +16,7 @@
 COMP = 50
 CL = 4
 CELLS = 256
-PACKED = 56
+PACKED = 52
 NY, NZ, NC, NX = 4, 8, 2, 4
 AXES = ("own", "split")
 
@@ -87,13 +87,14 @@
 
 
 def centre(ref):
-    middle = jnp.mean(ref[0], axis=1, keepdims=True)
-    return jnp.broadcast_to(middle, (PACKED, CELLS))
+    middle = jnp.mean(ref[0:56, :], axis=1, keepdims=True)
+    return jnp.broadcast_to(middle, (56, CELLS))
 
 
 def load_cluster(ref, a, middle):
-    top = ref[a, 0:48, :] - middle[0:48]
-    tail = ref[a, 48:PACKED, :]
+    at = PACKED * a
+    top = ref[at : at + 48, :] - middle[0:48]
+    tail = jnp.concatenate([ref[at + 48 : at + PACKED, :], jnp.zeros((4, CELLS), f32)], axis=0)
     row = lax.broadcasted_iota(jnp.int32, (8, CELLS), 0)
     extra = tail[2:3, :]
     tail = jnp.where(row < 2, tail - middle[48:56], 0.0)
@@ -180,7 +181,7 @@
     return logsum(top[:, 0, :], total)
 
 
-def pack_kernel(cells_in, extra_in, more_cells_in, more_extra_in, out, more_out, cells, more_cells, extra, more_extra, sem):
+def pack_kernel(cells_in, extra_in, more_cells_in, more_extra_in, source_in, target_in, out, more_out, codes_out, cells, more_cells, extra, more_extra, source, target, sem):
     copies = [
         pltpu.make_async_copy(a, b, sem.at[k])
         for k, (a, b) in enumerate(
@@ -189,6 +190,8 @@
                 (extra_in, extra),
                 (more_cells_in, more_cells),
                 (more_extra_in, more_extra),
+                (source_in, source),
+                (target_in, target),
             )
         )
     ]
@@ -197,10 +200,16 @@
     for k, (a, b, o) in enumerate(((cells, extra, out), (more_cells, more_extra, more_out))):
         copies[2 * k].wait()
         copies[2 * k + 1].wait()
+        if k == 1:
+            copies[4].wait()
+            copies[5].wait()
+            codes = jnp.where(target[...] >= 0, source[...] * CL + target[...], -1)
+            codes_out[...] = jnp.broadcast_to(codes[None], codes_out.shape)
         for n in range(CL):
-            o[n, 0:COMP, :] = a[:, n, :]
-            o[n, COMP : COMP + 1, :] = b[n : n + 1, :]
-            o[n, COMP + 1 : PACKED, :] = jnp.zeros((PACKED - COMP - 1, CELLS), f32)
+            at = PACKED * n
+            o[at : at + COMP, :] = a[:, n, :]
+            o[at + COMP : at + COMP + 1, :] = b[n : n + 1, :]
+            o[at + COMP + 1 : at + PACKED, :] = jnp.zeros((PACKED - COMP - 1, CELLS), f32)
 
 
 def row_kernel(codes_in, s0, s1, s2, s3, t0, t1, t2, t3, out, list_out, xn, yn, mass, square_out, codes, list_ref, yt, top, tot, *rest):
@@ -243,22 +252,18 @@
             store_operand(yn, k * CL + a, head, tail, ones, weight)
             yt[k * CL + a] = yn[k * CL + a].T
     over_pairs(count, list_ref, yt, xn, lambda s, t: (t, s, s), top, tot, scores, tops)
-    rows = finish(top, tot).reshape(4, CL, CELLS)
-    for k in range(4):
-        for m in range(MEMBERS):
-            out[m, (y + k) % NY] = rows[k]
+    out[...] = finish(top, tot)
     leaving.wait()
 
 
-def column_kernel(list_in, came, mass, square, x_in, yn, kept, given, potential, list_ref, xn, xt, four, top, tot, *rest):
+def column_kernel(list_in, m0, m1, m2, m3, mass, square, x_in, yn, kept, given, potential, list_ref, xn, xt, top, tot, *rest):
     scores, tops, sem = rest[:DEEP], rest[DEEP : 2 * DEEP], rest[2 * DEEP]
     arriving = pltpu.make_async_copy(list_in, list_ref, sem.at[0])
     arriving.start()
-    y = place()[1]
-    four[...] = merged([came[m] for m in range(MEMBERS)])
+    came = [m[...].reshape(4, CL, CELLS) for m in (m0, m1, m2, m3)]
     row = lax.broadcasted_iota(jnp.int32, (16, CELLS), 0)
     for k in range(4):
-        rows = four[(y + k) % NY]
+        rows = merged([came[d][(k - d) % NY] for d in range(NY)])
         for a in range(CL):
             n = k * CL + a
             p = EPSILON * mass[n : n + 1, :] - (EPSILON * LN2) * rows[a : a + 1]
@@ -292,18 +297,17 @@
 
 
 def work(source_coords, target_coords, source_logmass, target_logmass, target_prior, pair_source, pair_target):
-    codes = pair_source * 4 + pair_target
-    codes = jnp.where(pair_target >= 0, codes, -1).reshape(1, -1)
-    codes = exchanged(jnp.broadcast_to(codes, (MEMBERS, codes.shape[1])), PLANES)
-
-    cells = jax.ShapeDtypeStruct((CL, PACKED, CELLS), f32)
+    cells = jax.ShapeDtypeStruct((CL * PACKED, CELLS), f32)
     loose = pltpu.VMEM((COMP, CL, CELLS), f32)
-    t, s0 = pl.pallas_call(
+    t, s0, codes = pl.pallas_call(
         pack_kernel,
-        out_shape=(cells, cells),
-        in_specs=[HBM] * 4,
-        out_specs=(VMEM, VMEM),
-        scratch_shapes=[loose, loose] + [pltpu.VMEM((CL, CELLS), f32)] * 2 + [pltpu.SemaphoreType.DMA((4,))],
+        out_shape=(cells, cells, jax.ShapeDtypeStruct((MEMBERS, 1, SLOTS), jnp.int32)),
+        in_specs=[HBM] * 6,
+        out_specs=(VMEM, VMEM, VMEM),
+        scratch_shapes=[loose, loose]
+        + [pltpu.VMEM((CL, CELLS), f32)] * 2
+        + [pltpu.VMEM((1, SLOTS), jnp.int32)] * 2
+        + [pltpu.SemaphoreType.DMA((6,))],
         compiler_params=pltpu.CompilerParams(vmem_limit_bytes=4 * 2**20),
         name="pack",
     )(
@@ -314,12 +318,15 @@
                 target_prior,
                 jnp.transpose(source_coords, (1, 0, 2)),
                 source_logmass,
+                pair_source.reshape(1, SLOTS),
+                pair_target.reshape(1, SLOTS),
             )
         )
     )
     t2 = fetched(t, lambda x, y, z, c: (x, y, z + x + FAR, c))
     t0 = fetched(t, lambda x, y, z, c: (x, y, z + x, c))
     s1, s2, s3 = (from_y(s0, k) for k in (1, 2, 3))
+    codes = exchanged(codes, PLANES).reshape(MEMBERS, SLOTS)
     t1, t3 = from_core(t0), from_core(t2)
     shards = (s0, s1, s2, s3, t0, t1, t2, t3)
 
@@ -333,7 +340,7 @@
     rows, pairs, xn, yn, mass, square = pl.pallas_call(
         row_kernel,
         out_shape=(
-            jax.ShapeDtypeStruct((MEMBERS, 4, CL, CELLS), f32),
+            jax.ShapeDtypeStruct((4 * CL, CELLS), f32),
             jax.ShapeDtypeStruct((LIST,), jnp.int32),
             jax.ShapeDtypeStruct((4 * CL + 1, DEPTH, CELLS), bf16),
             jax.ShapeDtypeStruct((4 * CL, DEPTH, CELLS), bf16),
@@ -352,7 +359,8 @@
         name="rows",
     )(codes, *shards)
 
-    rows = exchanged(rows, PLANES)
+    rows = merged([rows] + [from_x(rows, k) for k in (1, 2, 3)])
+    others = [from_y(rows, k) for k in (1, 2, 3)]
 
     kept, given, source_potential = pl.pallas_call(
         column_kernel,
@@ -361,18 +369,17 @@
             jax.ShapeDtypeStruct((2 * CL, CELLS), f32),
             jax.ShapeDtypeStruct((CL, CELLS), f32),
         ),
-        in_specs=[ANY] + [VMEM] * 5,
+        in_specs=[ANY] + [VMEM] * 8,
         out_specs=(VMEM, VMEM, VMEM),
         scratch_shapes=[
             pltpu.SMEM((LIST,), jnp.int32),
             pltpu.VMEM((DEPTH, CELLS), bf16),
             pltpu.VMEM((4 * CL + 1, CELLS, DEPTH), bf16),
-            pltpu.VMEM((4, CL, CELLS), f32),
         ]
         + shared,
         compiler_params=params,
         name="columns",
-    )(pairs, rows, mass, square, xn, yn)
+    )(pairs, rows, *others, mass, square, xn, yn)
 
     kept = merged([kept, from_core(given)])
     first = fetched(kept[:CL], lambda x, y, z, c: (x, y, z - x, c))

time: 78.5 us -> 79 us (level); the launches traced: 78.2 us -> 77.9 us
  blocking collectives: 31.9 us -> 20.5 us
  starting transfers between devices: 27.1 us -> 34.4 us
  waiting for transfers between devices: 9.45 us -> 13.8 us
    all_to_all x2 -> x1, blocking collectives: 31.9 us -> 20.5 us  [exchanged(): lax.all_to_all(value, AXES, 0, 0, axis_index_groups=groups, tiled=True)]
    ppermute x13 -> x19, starting transfers between devices: 27.1 us -> 34.4 us  [fetched(): return lax.ppermute(value, AXES, pairs)]
    ppermute x13 -> x19, waiting for transfers between devices: 9.45 us -> 13.8 us  [fetched(): return lax.ppermute(value, AXES, pairs)]
  transfers between devices with their start and end apart: 13 -> 19, of which waited for: 4 -> 11; matrix products, arithmetic and copies ran while one was open for 1% -> 0% of each run, Pallas kernels for 0% -> 0%
where the time goes in v6:
time: 79 us; the launch traced here: 77.9 us
  starting transfers between devices  34.4 us (44%)
  blocking collectives  20.5 us (26%)
  waiting for transfers between devices  13.8 us (17%)
  Pallas kernels  7.7 us (10%)
    ppermute x19, starting transfers between devices, fetched(): return lax.ppermute(value, AXES, pairs)  34.4 us
    all_to_all x1, blocking collectives, exchanged(): lax.all_to_all(value, AXES, 0, 0, axis_index_groups=groups, tiled=True)  20.5 us
    ppermute x19, waiting for transfers between devices, fetched(): return lax.ppermute(value, AXES, pairs)  13.8 us
    pallas_call x1, Pallas kernels, work(): pl.pallas_call(row_kernel, out_shape=(jax.ShapeDtypeStruct((4 * CL, CELLS...  3.42 us
    pallas_call x1, Pallas kernels, work(): pl.pallas_call(column_kernel, out_shape=(jax.ShapeDtypeStruct((2 * CL, CE...  3.1 us
  transfers between devices with their start and end apart: 19, of which 11 were waited for; matrix products, arithmetic and copies ran while one was open for 0% of the time, Pallas kernels for 0%

profile of v6, /device:TPU:64, one launch (start us, length us, event | category | flops | bytes accessed | tf_op | source)
XLA Modules:
  0.0 77.9 jit_solution(1009041194572789635)
XLA Ops:
  0.6 1.2 %pack.1 = (f32[208,256]{1,0:T(8,128)S(1)}, f32[208,256]{1,0:T(8,128)S(1)}, s32[16,1,64]{2,1,0:T(1,128)S(1)}) custom-call(f32[50,4,256]{2,1,0:T(4,128)} %bitcast.6, f32[4,256]{1,0:T(4,128)} %extra_in.1, f32[50,4,256]{2,1,0:T(4,128)} %bitcast.7, f32[4,256]{1,0:T(4,128)} %more_extra_in.1, s32[1,64]{1,0:T(1,128)} %bitcast.8, s32[1,64]{1,0:T(1,128)} %bitcast.9), custom_call_target="tpu_custom_call" | custom-call | tf_op jit(solution)/shard_map/pack/pallas_call | solution.py:302
  1.8 5.5 %collective-permute-start.5 = (f32[208,256]{1,0:T(8,128)S(1)}, f32[208,256]{1,0:T(8,128)S(1)}, u32[]{:S(2)}, u32[]{:S(2)}) collective-permute-start(f32[208,256]{1,0:T(8,128)S(1)} %get-tuple-element.16), channel_id=1, source_target_pairs={{32,0},{41,1},{50,2},{59,3},{36,4},{45,5},{54,6},{63,7},{40,8},{49... | collective-permute-start | bytes 638984 | tf_op jit(solution)/shard_map/ppermute | solution.py:46
  7.3 0.7 collective-permute-start.3
  8.0 1.7 %collective-permute-start.2 = (f32[208,256]{1,0:T(8,128)S(1)}, f32[208,256]{1,0:T(8,128)S(1)}, u32[]{:S(2)}, u32[]{:S(2)}) collective-permute-start(f32[208,256]{1,0:T(8,128)S(1)} %get-tuple-element.15.s0), channel_id=1, source_target_pairs={{192,0},{193,1},{194,2},{195,3},{196,4},{197,5},{198,6},{199,7},{2... | collective-permute-start | bytes 638984 | tf_op jit(solution)/shard_map/ppermute | solution.py:46
  9.6 2.9 %collective-permute-start.1 = (f32[208,256]{1,0:T(8,128)S(1)}, f32[208,256]{1,0:T(8,128)S(1)}, u32[]{:S(2)}, u32[]{:S(2)}) collective-permute-start(f32[208,256]{1,0:T(8,128)S(1)} %get-tuple-element.15.s0), channel_id=1, source_target_pairs={{128,0},{129,1},{130,2},{131,3},{132,4},{133,5},{134,6},{135,7},{1... | collective-permute-start | bytes 638984 | tf_op jit(solution)/shard_map/ppermute | solution.py:46
  12.5 1.3 %collective-permute-start = (f32[208,256]{1,0:T(8,128)S(1)}, f32[208,256]{1,0:T(8,128)S(1)}, u32[]{:S(2)}, u32[]{:S(2)}) collective-permute-start(f32[208,256]{1,0:T(8,128)S(1)} %get-tuple-element.15.s0), channel_id=1, source_target_pairs={{64,0},{65,1},{66,2},{67,3},{68,4},{69,5},{70,6},{71,7},{72,8},{73... | collective-permute-start | bytes 638984 | tf_op jit(solution)/shard_map/ppermute | solution.py:46
  13.9 3.5 %collective-permute-done.5.t2 = f32[208,256]{1,0:T(8,128)S(1)} collective-permute-done((f32[208,256]{1,0:T(8,128)S(1)}, f32[208,256]{1,0:T(8,128)S(1)}, u32[]{:S(2)}, u32[]{:S(2)}) %collective-permute-start.5) | collective-permute-done | bytes 213024 | tf_op jit(solution)/shard_map/ppermute | solution.py:46
  17.9 20.5 %all_to_all.5 = s32[16,1,64]{2,1,0:T(1,128)S(1)} all-to-all(s32[16,1,64]{2,1,0:T(1,128)S(1)} %get-tuple-element.14), channel_id=1, replica_groups={{0,64,128,192,1,65,129,193,2,66,130,194,3,67,131,195},{4,68,132,196,5,6..., dimensions={0} | all-to-all | bytes 8192 | tf_op jit(solution)/shard_map/all_to_all | solution.py:62
  38.4 3.4 %rows.1 = (f32[16,256]{1,0:T(8,128)S(1)}, s32[80]{0:T(128)S(1)}, bf16[17,128,256]{2,1,0:T(8,128)(2,1)S(1)}, bf16[16,128,256]{2,1,0:T(8,128)(2,1)S(1)}, f32[16,256]{1,0:T(8,128)S(1)}, /*index=5*/f32[16,256]{1,0:T(8,128)S(1)}) custom-call(s32[16,64]{1,0:T(8,128)S(1)} %bitcast.5, f32[208,256]{1,0:T(8,128)S(1)} %get-tuple-element.15.s0, ...), custom_call_target="tpu_custom_call" | custom-call | tf_op jit(solution)/shard_map/rows/pallas_call | solution.py:340
  41.9 2.6 %collective-permute-start.8 = (f32[16,256]{1,0:T(8,128)S(1)}, f32[16,256]{1,0:T(8,128)S(1)}, u32[]{:S(2)}, u32[]{:S(2)}) collective-permute-start(f32[16,256]{1,0:T(8,128)S(1)} %get-tuple-element.18), channel_id=1, source_target_pairs={{2,0},{3,1},{0,2},{1,3},{6,4},{7,5},{4,6},{5,7},{10,8},{11,9},{8,1... | collective-permute-start | bytes 49160 | tf_op jit(solution)/shard_map/ppermute | solution.py:46
  45.2 1.8 %collective-permute-done.9 = f32[16,256]{1,0:T(8,128)S(1)} collective-permute-done((f32[16,256]{1,0:T(8,128)S(1)}, f32[16,256]{1,0:T(8,128)S(1)}, u32[]{:S(2)}, u32[]{:S(2)}) %collective-permute-start.9) | collective-permute-done | bytes 16416 | tf_op jit(solution)/shard_map/ppermute | solution.py:46
  47.3 1.0 %collective-permute-done.7 = f32[16,256]{1,0:T(8,128)S(1)} collective-permute-done((f32[16,256]{1,0:T(8,128)S(1)}, f32[16,256]{1,0:T(8,128)S(1)}, u32[]{:S(2)}, u32[]{:S(2)}) %collective-permute-start.7) | collective-permute-done | bytes 16416 | tf_op jit(solution)/shard_map/ppermute | solution.py:46
  48.7 2.3 %collective-permute-start.11 = (f32[16,256]{1,0:T(8,128)S(1)}, f32[16,256]{1,0:T(8,128)S(1)}, u32[]{:S(2)}, u32[]{:S(2)}) collective-permute-start(f32[16,256]{1,0:T(8,128)S(1)} %multiply_add_fusion.m0), channel_id=1, source_target_pairs={{128,0},{129,1},{130,2},{131,3},{132,4},{133,5},{134,6},{135,7},{1... | collective-permute-start | bytes 49160 | tf_op jit(solution)/shard_map/ppermute | solution.py:46
  51.0 0.7 collective-permute-start.10
  51.6 1.7 %collective-permute-done.12.m3 = f32[16,256]{1,0:T(8,128)S(1)} collective-permute-done((f32[16,256]{1,0:T(8,128)S(1)}, f32[16,256]{1,0:T(8,128)S(1)}, u32[]{:S(2)}, u32[]{:S(2)}) %collective-permute-start.12) | collective-permute-done | bytes 16416 | tf_op jit(solution)/shard_map/ppermute | solution.py:46
  53.9 0.8 %collective-permute-done.10.m1 = f32[16,256]{1,0:T(8,128)S(1)} collective-permute-done((f32[16,256]{1,0:T(8,128)S(1)}, f32[16,256]{1,0:T(8,128)S(1)}, u32[]{:S(2)}, u32[]{:S(2)}) %collective-permute-start.10) | collective-permute-done | bytes 16416 | tf_op jit(solution)/shard_map/ppermute | solution.py:46
  54.7 3.1 %columns.1 = (f32[8,256]{1,0:T(8,128)S(1)}, f32[8,256]{1,0:T(8,128)S(1)}, f32[4,256]{1,0:T(4,128)}) custom-call(s32[80]{0:T(128)S(1)} %get-tuple-element.17.list_in, f32[16,256]{1,0:T(8,128)S(1)} %multiply_add_fusion.m0, f32[16,256]{1,0:T(8,128)S(1)} %collective-permute-done.10.m1, f32[16,256]{1,0:T(8,128)S(1)} %collective-permute-done.11.m2, ...), custom_call_target="tpu_custom_call" | custom-call | tf_op jit(solution)/shard_map/columns/pallas_call | solution.py:365
  58.1 1.2 %collective-permute-done.13 = f32[8,256]{1,0:T(8,128)S(1)} collective-permute-done((f32[8,256]{1,0:T(8,128)S(1)}, f32[8,256]{1,0:T(8,128)S(1)}, u32[]{:S(2)}, u32[]{:S(2)}) %collective-permute-start.13) | collective-permute-done | bytes 8224 | tf_op jit(solution)/shard_map/ppermute | solution.py:46
  60.0 6.0 %collective-permute-start.15 = (f32[4,256]{1,0:T(4,128)S(1)}, f32[4,256]{1,0:T(4,128)S(1)}, u32[]{:S(2)}, u32[]{:S(2)}) collective-permute-start(f32[4,256]{1,0:T(4,128)S(1)} %get-tuple-element.27), channel_id=1, source_target_pairs={{32,0},{25,1},{18,2},{11,3},{36,4},{29,5},{22,6},{15,7},{40,8},{33... | collective-permute-start | bytes 12296 | tf_op jit(solution)/shard_map/ppermute | solution.py:46
  66.0 1.6 %collective-permute-done.15 = f32[4,256]{1,0:T(4,128)S(1)} collective-permute-done((f32[4,256]{1,0:T(4,128)S(1)}, f32[4,256]{1,0:T(4,128)S(1)}, u32[]{:S(2)}, u32[]{:S(2)}) %collective-permute-start.15) | collective-permute-done | bytes 4128 | tf_op jit(solution)/shard_map/ppermute | solution.py:46
  67.6 3.9 %collective-permute-start.18 = (f32[4,256]{1,0:T(4,128)S(1)}, f32[4,256]{1,0:T(4,128)S(1)}, u32[]{:S(2)}, u32[]{:S(2)}) collective-permute-start(f32[4,256]{1,0:T(4,128)S(1)} %multiply_add_fusion.2), channel_id=1, source_target_pairs={{3,0},{0,1},{1,2},{2,3},{7,4},{4,5},{5,6},{6,7},{11,8},{8,9},{9,10... | collective-permute-start | bytes 12296 | tf_op jit(solution)/shard_map/ppermute | solution.py:46
  71.5 2.1 %collective-permute-start.17 = (f32[4,256]{1,0:T(4,128)S(1)}, f32[4,256]{1,0:T(4,128)S(1)}, u32[]{:S(2)}, u32[]{:S(2)}) collective-permute-start(f32[4,256]{1,0:T(4,128)S(1)} %multiply_add_fusion.2), channel_id=1, source_target_pairs={{2,0},{3,1},{0,2},{1,3},{6,4},{7,5},{4,6},{5,7},{10,8},{11,9},{8,1... | collective-permute-start | bytes 12296 | tf_op jit(solution)/shard_map/ppermute | solution.py:46
  73.6 2.3 %collective-permute-start.16 = (f32[4,256]{1,0:T(4,128)S(1)}, f32[4,256]{1,0:T(4,128)S(1)}, u32[]{:S(2)}, u32[]{:S(2)}) collective-permute-start(f32[4,256]{1,0:T(4,128)S(1)} %multiply_add_fusion.2), channel_id=1, source_target_pairs={{1,0},{2,1},{3,2},{0,3},{5,4},{6,5},{7,6},{4,7},{9,8},{10,9},{11,1... | collective-permute-start | bytes 12296 | tf_op jit(solution)/shard_map/ppermute | solution.py:46
  75.9 0.7 collective-permute-done.17
  (27 shorter events, 4.7 us)
Async XLA Ops:
  1.8 15.6 %collective-permute-start.5 = (f32[208,256]{1,0:T(8,128)S(1)}, f32[208,256]{1,0:T(8,128)S(1)}, u32[]{:S(2)}, u32[]{:S(2)}) collective-permute-start(f32[208,256]{1,0:T(8,128)S(1)} %get-tuple-element.16), channel_id=1, source_target_pairs={{32,0},{41,1},{50,2},{59,3},{36,4},{45,5},{54,6},{63,7},{40,8},{49... | collective-permute-start | bytes 638984 | tf_op jit(solution)/shard_map/ppermute | solution.py:46
  7.3 10.1 %collective-permute-start.3 = (f32[208,256]{1,0:T(8,128)S(1)}, f32[208,256]{1,0:T(8,128)S(1)}, u32[]{:S(2)}, u32[]{:S(2)}) collective-permute-start(f32[208,256]{1,0:T(8,128)S(1)} %get-tuple-element.16), channel_id=1, source_target_pairs={{0,0},{9,1},{18,2},{27,3},{4,4},{13,5},{22,6},{31,7},{8,8},{17,9},... | collective-permute-start | bytes 638984 | tf_op jit(solution)/shard_map/ppermute | solution.py:46
  8.0 30.4 %collective-permute-start.2 = (f32[208,256]{1,0:T(8,128)S(1)}, f32[208,256]{1,0:T(8,128)S(1)}, u32[]{:S(2)}, u32[]{:S(2)}) collective-permute-start(f32[208,256]{1,0:T(8,128)S(1)} %get-tuple-element.15.s0), channel_id=1, source_target_pairs={{192,0},{193,1},{194,2},{195,3},{196,4},{197,5},{198,6},{199,7},{2... | collective-permute-start | bytes 638984 | tf_op jit(solution)/shard_map/ppermute | solution.py:46
  9.6 28.8 %collective-permute-start.1 = (f32[208,256]{1,0:T(8,128)S(1)}, f32[208,256]{1,0:T(8,128)S(1)}, u32[]{:S(2)}, u32[]{:S(2)}) collective-permute-start(f32[208,256]{1,0:T(8,128)S(1)} %get-tuple-element.15.s0), channel_id=1, source_target_pairs={{128,0},{129,1},{130,2},{131,3},{132,4},{133,5},{134,6},{135,7},{1... | collective-permute-start | bytes 638984 | tf_op jit(solution)/shard_map/ppermute | solution.py:46
  12.5 25.9 %collective-permute-start = (f32[208,256]{1,0:T(8,128)S(1)}, f32[208,256]{1,0:T(8,128)S(1)}, u32[]{:S(2)}, u32[]{:S(2)}) collective-permute-start(f32[208,256]{1,0:T(8,128)S(1)} %get-tuple-element.15.s0), channel_id=1, source_target_pairs={{64,0},{65,1},{66,2},{67,3},{68,4},{69,5},{70,6},{71,7},{72,8},{73... | collective-permute-start | bytes 638984 | tf_op jit(solution)/shard_map/ppermute | solution.py:46
  17.4 21.0 %collective-permute-start.6 = (f32[208,256]{1,0:T(8,128)S(1)}, f32[208,256]{1,0:T(8,128)S(1)}, u32[]{:S(2)}, u32[]{:S(2)}) collective-permute-start(f32[208,256]{1,0:T(8,128)S(1)} %collective-permute-done.5.t2), channel_id=1, source_target_pairs={{4,0},{5,1},{6,2},{7,3},{0,4},{1,5},{2,6},{3,7},{12,8},{13,9},{14,... | collective-permute-start | bytes 638984 | tf_op jit(solution)/shard_map/ppermute | solution.py:46
  17.4 21.0 %collective-permute-start.4 = (f32[208,256]{1,0:T(8,128)S(1)}, f32[208,256]{1,0:T(8,128)S(1)}, u32[]{:S(2)}, u32[]{:S(2)}) collective-permute-start(f32[208,256]{1,0:T(8,128)S(1)} %collective-permute-done.3.t0), channel_id=1, source_target_pairs={{4,0},{5,1},{6,2},{7,3},{0,4},{1,5},{2,6},{3,7},{12,8},{13,9},{14,... | collective-permute-start | bytes 638984 | tf_op jit(solution)/shard_map/ppermute | solution.py:46
  41.9 5.1 %collective-permute-start.9 = (f32[16,256]{1,0:T(8,128)S(1)}, f32[16,256]{1,0:T(8,128)S(1)}, u32[]{:S(2)}, u32[]{:S(2)}) collective-permute-start(f32[16,256]{1,0:T(8,128)S(1)} %get-tuple-element.18), channel_id=1, source_target_pairs={{3,0},{0,1},{1,2},{2,3},{7,4},{4,5},{5,6},{6,7},{11,8},{8,9},{9,10... | collective-permute-start | bytes 49160 | tf_op jit(solution)/shard_map/ppermute | solution.py:46
  41.9 5.3 %collective-permute-start.8 = (f32[16,256]{1,0:T(8,128)S(1)}, f32[16,256]{1,0:T(8,128)S(1)}, u32[]{:S(2)}, u32[]{:S(2)}) collective-permute-start(f32[16,256]{1,0:T(8,128)S(1)} %get-tuple-element.18), channel_id=1, source_target_pairs={{2,0},{3,1},{0,2},{1,3},{6,4},{7,5},{4,6},{5,7},{10,8},{11,9},{8,1... | collective-permute-start | bytes 49160 | tf_op jit(solution)/shard_map/ppermute | solution.py:46
  44.6 3.7 %collective-permute-start.7 = (f32[16,256]{1,0:T(8,128)S(1)}, f32[16,256]{1,0:T(8,128)S(1)}, u32[]{:S(2)}, u32[]{:S(2)}) collective-permute-start(f32[16,256]{1,0:T(8,128)S(1)} %get-tuple-element.18), channel_id=1, source_target_pairs={{1,0},{2,1},{3,2},{0,3},{5,4},{6,5},{7,6},{4,7},{9,8},{10,9},{11,1... | collective-permute-start | bytes 49160 | tf_op jit(solution)/shard_map/ppermute | solution.py:46
  48.3 5.0 %collective-permute-start.12 = (f32[16,256]{1,0:T(8,128)S(1)}, f32[16,256]{1,0:T(8,128)S(1)}, u32[]{:S(2)}, u32[]{:S(2)}) collective-permute-start(f32[16,256]{1,0:T(8,128)S(1)} %multiply_add_fusion.m0), channel_id=1, source_target_pairs={{192,0},{193,1},{194,2},{195,3},{196,4},{197,5},{198,6},{199,7},{2... | collective-permute-start | bytes 49160 | tf_op jit(solution)/shard_map/ppermute | solution.py:46
  48.7 5.2 %collective-permute-start.11 = (f32[16,256]{1,0:T(8,128)S(1)}, f32[16,256]{1,0:T(8,128)S(1)}, u32[]{:S(2)}, u32[]{:S(2)}) collective-permute-start(f32[16,256]{1,0:T(8,128)S(1)} %multiply_add_fusion.m0), channel_id=1, source_target_pairs={{128,0},{129,1},{130,2},{131,3},{132,4},{133,5},{134,6},{135,7},{1... | collective-permute-start | bytes 49160 | tf_op jit(solution)/shard_map/ppermute | solution.py:46
  51.0 3.7 %collective-permute-start.10 = (f32[16,256]{1,0:T(8,128)S(1)}, f32[16,256]{1,0:T(8,128)S(1)}, u32[]{:S(2)}, u32[]{:S(2)}) collective-permute-start(f32[16,256]{1,0:T(8,128)S(1)} %multiply_add_fusion.m0), channel_id=1, source_target_pairs={{64,0},{65,1},{66,2},{67,3},{68,4},{69,5},{70,6},{71,7},{72,8},{73... | collective-permute-start | bytes 49160 | tf_op jit(solution)/shard_map/ppermute | solution.py:46
  54.7 22.5 %copy-start = (f32[4,256]{1,0:T(4,128)S(1)}, f32[4,256]{1,0:T(4,128)}, u32[]{:S(2)}) copy-start(f32[4,256]{1,0:T(4,128)} %extra_in.1) | copy-start | bytes 12292
  54.7 22.5 %copy-start.1 = (f32[4,256]{1,0:T(4,128)S(1)}, f32[4,256]{1,0:T(4,128)}, u32[]{:S(2)}) copy-start(f32[4,256]{1,0:T(4,128)} %param.10) | copy-start | bytes 12292
  57.8 1.4 %collective-permute-start.13 = (f32[8,256]{1,0:T(8,128)S(1)}, f32[8,256]{1,0:T(8,128)S(1)}, u32[]{:S(2)}, u32[]{:S(2)}) collective-permute-start(f32[8,256]{1,0:T(8,128)S(1)} %get-tuple-element.25), channel_id=1, source_target_pairs={{4,0},{5,1},{6,2},{7,3},{0,4},{1,5},{2,6},{3,7},{12,8},{13,9},{14,... | collective-permute-start | bytes 24584 | tf_op jit(solution)/shard_map/ppermute | solution.py:46
  59.3 6.7 %collective-permute-start.14 = (f32[4,256]{1,0:T(4,128)S(1)}, f32[4,256]{1,0:T(4,128)S(1)}, u32[]{:S(2)}, u32[]{:S(2)}) collective-permute-start(f32[4,256]{1,0:T(4,128)S(1)} %get-tuple-element.26), channel_id=1, source_target_pairs={{0,0},{57,1},{50,2},{43,3},{4,4},{61,5},{54,6},{47,7},{8,8},{1,9},... | collective-permute-start | bytes 12296 | tf_op jit(solution)/shard_map/ppermute | solution.py:46
  60.0 7.6 %collective-permute-start.15 = (f32[4,256]{1,0:T(4,128)S(1)}, f32[4,256]{1,0:T(4,128)S(1)}, u32[]{:S(2)}, u32[]{:S(2)}) collective-permute-start(f32[4,256]{1,0:T(4,128)S(1)} %get-tuple-element.27), channel_id=1, source_target_pairs={{32,0},{25,1},{18,2},{11,3},{36,4},{29,5},{22,6},{15,7},{40,8},{33... | collective-permute-start | bytes 12296 | tf_op jit(solution)/shard_map/ppermute | solution.py:46
  67.6 8.3 %collective-permute-start.18 = (f32[4,256]{1,0:T(4,128)S(1)}, f32[4,256]{1,0:T(4,128)S(1)}, u32[]{:S(2)}, u32[]{:S(2)}) collective-permute-start(f32[4,256]{1,0:T(4,128)S(1)} %multiply_add_fusion.2), channel_id=1, source_target_pairs={{3,0},{0,1},{1,2},{2,3},{7,4},{4,5},{5,6},{6,7},{11,8},{8,9},{9,10... | collective-permute-start | bytes 12296 | tf_op jit(solution)/shard_map/ppermute | solution.py:46
  71.5 5.1 %collective-permute-start.17 = (f32[4,256]{1,0:T(4,128)S(1)}, f32[4,256]{1,0:T(4,128)S(1)}, u32[]{:S(2)}, u32[]{:S(2)}) collective-permute-start(f32[4,256]{1,0:T(4,128)S(1)} %multiply_add_fusion.2), channel_id=1, source_target_pairs={{2,0},{3,1},{0,2},{1,3},{6,4},{7,5},{4,6},{5,7},{10,8},{11,9},{8,1... | collective-permute-start | bytes 12296 | tf_op jit(solution)/shard_map/ppermute | solution.py:46
  73.6 3.6 %collective-permute-start.16 = (f32[4,256]{1,0:T(4,128)S(1)}, f32[4,256]{1,0:T(4,128)S(1)}, u32[]{:S(2)}, u32[]{:S(2)}) collective-permute-start(f32[4,256]{1,0:T(4,128)S(1)} %multiply_add_fusion.2), channel_id=1, source_target_pairs={{1,0},{2,1},{3,2},{0,3},{5,4},{6,5},{7,6},{4,7},{9,8},{10,9},{11,1... | collective-permute-start | bytes 12296 | tf_op jit(solution)/shard_map/ppermute | solution.py:46

commit v7 on v6

--- a/solution.py
+++ b/solution.py
@@ -195,21 +195,20 @@
             )
         )
     ]
-    for copy in copies:
+    for copy in (*copies[4:], *copies[:4]):
         copy.start()
     for k, (a, b, o) in enumerate(((cells, extra, out), (more_cells, more_extra, more_out))):
         copies[2 * k].wait()
         copies[2 * k + 1].wait()
-        if k == 1:
-            copies[4].wait()
-            copies[5].wait()
-            codes = jnp.where(target[...] >= 0, source[...] * CL + target[...], -1)
-            codes_out[...] = jnp.broadcast_to(codes[None], codes_out.shape)
         for n in range(CL):
             at = PACKED * n
             o[at : at + COMP, :] = a[:, n, :]
             o[at + COMP : at + COMP + 1, :] = b[n : n + 1, :]
             o[at + COMP + 1 : at + PACKED, :] = jnp.zeros((PACKED - COMP - 1, CELLS), f32)
+    copies[4].wait()
+    copies[5].wait()
+    codes = jnp.where(target[...] >= 0, source[...] * CL + target[...], -1)
+    codes_out[...] = jnp.broadcast_to(codes[None], codes_out.shape)
 
 
 def row_kernel(codes_in, s0, s1, s2, s3, t0, t1, t2, t3, out, list_out, xn, yn, mass, square_out, codes, list_ref, yt, top, tot, *rest):
@@ -252,18 +251,22 @@
             store_operand(yn, k * CL + a, head, tail, ones, weight)
             yt[k * CL + a] = yn[k * CL + a].T
     over_pairs(count, list_ref, yt, xn, lambda s, t: (t, s, s), top, tot, scores, tops)
-    out[...] = finish(top, tot)
+    rows = finish(top, tot).reshape(4, CL, CELLS)
+    for k in range(4):
+        for m in range(MEMBERS):
+            out[m, (y + k) % NY] = rows[k]
     leaving.wait()
 
 
-def column_kernel(list_in, m0, m1, m2, m3, mass, square, x_in, yn, kept, given, potential, list_ref, xn, xt, top, tot, *rest):
+def column_kernel(list_in, came, mass, square, x_in, yn, kept, given, potential, list_ref, xn, xt, four, top, tot, *rest):
     scores, tops, sem = rest[:DEEP], rest[DEEP : 2 * DEEP], rest[2 * DEEP]
     arriving = pltpu.make_async_copy(list_in, list_ref, sem.at[0])
     arriving.start()
-    came = [m[...].reshape(4, CL, CELLS) for m in (m0, m1, m2, m3)]
+    y = place()[1]
+    four[...] = merged([came[m] for m in range(MEMBERS)])
     row = lax.broadcasted_iota(jnp.int32, (16, CELLS), 0)
     for k in range(4):
-        rows = merged([came[d][(k - d) % NY] for d in range(NY)])
+        rows = four[(y + k) % NY]
         for a in range(CL):
             n = k * CL + a
             p = EPSILON * mass[n : n + 1, :] - (EPSILON * LN2) * rows[a : a + 1]
@@ -340,7 +343,7 @@
     rows, pairs, xn, yn, mass, square = pl.pallas_call(
         row_kernel,
         out_shape=(
-            jax.ShapeDtypeStruct((4 * CL, CELLS), f32),
+            jax.ShapeDtypeStruct((MEMBERS, 4, CL, CELLS), f32),
             jax.ShapeDtypeStruct((LIST,), jnp.int32),
             jax.ShapeDtypeStruct((4 * CL + 1, DEPTH, CELLS), bf16),
             jax.ShapeDtypeStruct((4 * CL, DEPTH, CELLS), bf16),
@@ -359,8 +362,7 @@
         name="rows",
     )(codes, *shards)
 
-    rows = merged([rows] + [from_x(rows, k) for k in (1, 2, 3)])
-    others = [from_y(rows, k) for k in (1, 2, 3)]
+    rows = exchanged(rows, PLANES)
 
     kept, given, source_potential = pl.pallas_call(
         column_kernel,
@@ -369,23 +371,25 @@
             jax.ShapeDtypeStruct((2 * CL, CELLS), f32),
             jax.ShapeDtypeStruct((CL, CELLS), f32),
         ),
-        in_specs=[ANY] + [VMEM] * 8,
+        in_specs=[ANY] + [VMEM] * 5,
         out_specs=(VMEM, VMEM, VMEM),
         scratch_shapes=[
             pltpu.SMEM((LIST,), jnp.int32),
             pltpu.VMEM((DEPTH, CELLS), bf16),
             pltpu.VMEM((4 * CL + 1, CELLS, DEPTH), bf16),
+            pltpu.VMEM((4, CL, CELLS), f32),
         ]
         + shared,
         compiler_params=params,
         name="columns",
-    )(pairs, rows, *others, mass, square, xn, yn)
+    )(pairs, rows, mass, square, xn, yn)
 
     kept = merged([kept, from_core(given)])
     first = fetched(kept[:CL], lambda x, y, z, c: (x, y, z - x, c))
     second = fetched(kept[CL:], lambda x, y, z, c: (x, y, z - x - FAR, c))
     part = merged([first, second])
-    part = merged([part] + [from_x(part, k) for k in (1, 2, 3)])
+    opposite = from_x(part, 2)
+    part = merged([part, opposite] + [from_x(part, k) for k in (1, 3)])
     target_potential = EPSILON * target_logmass + target_prior - (EPSILON * LN2) * part
     return source_potential, target_potential
 

time: 79 us -> 76.5 us (0.968)
  blocking collectives: 20.5 us -> 32.1 us
  starting transfers between devices: 34.4 us -> 26.2 us
  waiting for transfers between devices: 13.8 us -> 8.22 us
    all_to_all x1 -> x2, blocking collectives: 20.5 us -> 32.1 us  [exchanged(): lax.all_to_all(value, AXES, 0, 0, axis_index_groups=groups, tiled=True)]
    ppermute x19 -> x13, starting transfers between devices: 34.4 us -> 26.2 us  [fetched(): return lax.ppermute(value, AXES, pairs)]
    ppermute x19 -> x13, waiting for transfers between devices: 13.8 us -> 8.22 us  [fetched(): return lax.ppermute(value, AXES, pairs)]
  transfers between devices with their start and end apart: 19 -> 13, of which waited for: 11 -> 4; matrix products, arithmetic and copies ran while one was open for 0% -> 0% of each run, Pallas kernels for 0% -> 0%
where the time goes in v7:
time: 76.5 us; the launch traced here: 75.7 us
  blocking collectives  32.1 us (42%)
  starting transfers between devices  26.2 us (34%)
  waiting for transfers between devices  8.22 us (11%)
  Pallas kernels  7.83 us (10%)
    all_to_all x2, blocking collectives, exchanged(): lax.all_to_all(value, AXES, 0, 0, axis_index_groups=groups, tiled=True)  32.1 us
    ppermute x13, starting transfers between devices, fetched(): return lax.ppermute(value, AXES, pairs)  26.2 us
    ppermute x13, waiting for transfers between devices, fetched(): return lax.ppermute(value, AXES, pairs)  8.22 us
    pallas_call x1, Pallas kernels, work(): pl.pallas_call(row_kernel, out_shape=(jax.ShapeDtypeStruct((MEMBERS, 4, C...  3.42 us
    pallas_call x1, Pallas kernels, work(): pl.pallas_call(column_kernel, out_shape=(jax.ShapeDtypeStruct((2 * CL, CE...  3.2 us
  transfers between devices with their start and end apart: 13, of which 4 were waited for; matrix products, arithmetic and copies ran while one was open for 0% of the time, Pallas kernels for 0%

profile of v7, /device:TPU:64, one launch (start us, length us, event | category | flops | bytes accessed | tf_op | source)
XLA Modules:
  0.0 75.7 jit_solution(3236342263634402805)
XLA Ops:
  0.6 1.2 %pack.1 = (f32[208,256]{1,0:T(8,128)S(1)}, f32[208,256]{1,0:T(8,128)S(1)}, s32[16,1,64]{2,1,0:T(1,128)S(1)}) custom-call(f32[50,4,256]{2,1,0:T(4,128)} %bitcast.6, f32[4,256]{1,0:T(4,128)} %extra_in.1, f32[50,4,256]{2,1,0:T(4,128)} %bitcast.7, f32[4,256]{1,0:T(4,128)} %more_extra_in.1, s32[1,64]{1,0:T(1,128)} %bitcast.8, s32[1,64]{1,0:T(1,128)} %bitcast.9), custom_call_target="tpu_custom_call" | custom-call | tf_op jit(solution)/shard_map/pack/pallas_call | solution.py:305
  1.9 5.5 %collective-permute-start.5 = (f32[208,256]{1,0:T(8,128)S(1)}, f32[208,256]{1,0:T(8,128)S(1)}, u32[]{:S(2)}, u32[]{:S(2)}) collective-permute-start(f32[208,256]{1,0:T(8,128)S(1)} %get-tuple-element.16), channel_id=1, source_target_pairs={{32,0},{41,1},{50,2},{59,3},{36,4},{45,5},{54,6},{63,7},{40,8},{49... | collective-permute-start | bytes 638984 | tf_op jit(solution)/shard_map/ppermute | solution.py:46
  7.3 0.7 collective-permute-start.3
  8.0 1.7 %collective-permute-start.2 = (f32[208,256]{1,0:T(8,128)S(1)}, f32[208,256]{1,0:T(8,128)S(1)}, u32[]{:S(2)}, u32[]{:S(2)}) collective-permute-start(f32[208,256]{1,0:T(8,128)S(1)} %get-tuple-element.15.s0), channel_id=1, source_target_pairs={{192,0},{193,1},{194,2},{195,3},{196,4},{197,5},{198,6},{199,7},{2... | collective-permute-start | bytes 638984 | tf_op jit(solution)/shard_map/ppermute | solution.py:46
  9.6 2.9 %collective-permute-start.1 = (f32[208,256]{1,0:T(8,128)S(1)}, f32[208,256]{1,0:T(8,128)S(1)}, u32[]{:S(2)}, u32[]{:S(2)}) collective-permute-start(f32[208,256]{1,0:T(8,128)S(1)} %get-tuple-element.15.s0), channel_id=1, source_target_pairs={{128,0},{129,1},{130,2},{131,3},{132,4},{133,5},{134,6},{135,7},{1... | collective-permute-start | bytes 638984 | tf_op jit(solution)/shard_map/ppermute | solution.py:46
  12.5 1.3 %collective-permute-start = (f32[208,256]{1,0:T(8,128)S(1)}, f32[208,256]{1,0:T(8,128)S(1)}, u32[]{:S(2)}, u32[]{:S(2)}) collective-permute-start(f32[208,256]{1,0:T(8,128)S(1)} %get-tuple-element.15.s0), channel_id=1, source_target_pairs={{64,0},{65,1},{66,2},{67,3},{68,4},{69,5},{70,6},{71,7},{72,8},{73... | collective-permute-start | bytes 638984 | tf_op jit(solution)/shard_map/ppermute | solution.py:46
  13.9 3.5 %collective-permute-done.5.t2 = f32[208,256]{1,0:T(8,128)S(1)} collective-permute-done((f32[208,256]{1,0:T(8,128)S(1)}, f32[208,256]{1,0:T(8,128)S(1)}, u32[]{:S(2)}, u32[]{:S(2)}) %collective-permute-start.5) | collective-permute-done | bytes 213024 | tf_op jit(solution)/shard_map/ppermute | solution.py:46
  17.4 0.0 collective-permute-start.6
  17.4 0.0 collective-permute-done.3.t0
  17.4 0.5 collective-permute-start.4
  18.0 20.5 %all_to_all.10 = s32[16,1,64]{2,1,0:T(1,128)S(1)} all-to-all(s32[16,1,64]{2,1,0:T(1,128)S(1)} %get-tuple-element.14), channel_id=1, replica_groups={{0,64,128,192,1,65,129,193,2,66,130,194,3,67,131,195},{4,68,132,196,5,6..., dimensions={0} | all-to-all | bytes 8192 | tf_op jit(solution)/shard_map/all_to_all | solution.py:62
  38.5 3.4 %rows.1 = (f32[16,4,4,256]{3,2,1,0:T(4,128)S(1)}, s32[80]{0:T(128)S(1)}, bf16[17,128,256]{2,1,0:T(8,128)(2,1)S(1)}, bf16[16,128,256]{2,1,0:T(8,128)(2,1)S(1)}, f...) custom-call(s32[16,64]{1,0:T(8,128)S(1)} %bitcast.5, f32[208,256]{1,0:T(8,128)S(1)} %get-tuple-element.15.s0, ...), custom_call_target="tpu_custom_call" | custom-call | tf_op jit(solution)/shard_map/rows/pallas_call | solution.py:343
  41.9 11.7 %all_to_all.11.came = f32[16,4,4,256]{3,2,1,0:T(4,128)S(1)} all-to-all(f32[16,4,4,256]{3,2,1,0:T(4,128)S(1)} %get-tuple-element.18), channel_id=1, replica_groups={{0,64,128,192,1,65,129,193,2,66,130,194,3,67,131,195},{4,68,132,196,5,6..., dimensions={0} | all-to-all | bytes 524288 | tf_op jit(solution)/shard_map/all_to_all | solution.py:62
  53.6 3.2 %columns.1 = (f32[8,256]{1,0:T(8,128)S(1)}, f32[8,256]{1,0:T(8,128)S(1)}, f32[4,256]{1,0:T(4,128)}) custom-call(s32[80]{0:T(128)S(1)} %get-tuple-element.17.list_in, f32[16,4,4,256]{3,2,1,0:T(4,128)S(1)} %all_to_all.11.came, f32[16,256]{1,0:T(8,128)S(1)} %get-tuple-element.19.mass, f32[16,256]{1,0:T(8,128)S(1)} %get-tuple-element.20.square, ...), custom_call_target="tpu_custom_call" | custom-call | tf_op jit(solution)/shard_map/columns/pallas_call | solution.py:367
  56.8 0.1 collective-permute-start.7
  56.9 1.2 %collective-permute-done.7 = f32[8,256]{1,0:T(8,128)S(1)} collective-permute-done((f32[8,256]{1,0:T(8,128)S(1)}, f32[8,256]{1,0:T(8,128)S(1)}, u32[]{:S(2)}, u32[]{:S(2)}) %collective-permute-start.7) | collective-permute-done | bytes 8224 | tf_op jit(solution)/shard_map/ppermute | solution.py:46
  58.1 0.7 collective-permute-start.8
  58.7 5.7 %collective-permute-start.9 = (f32[4,256]{1,0:T(4,128)S(1)}, f32[4,256]{1,0:T(4,128)S(1)}, u32[]{:S(2)}, u32[]{:S(2)}) collective-permute-start(f32[4,256]{1,0:T(4,128)S(1)} %get-tuple-element.27), channel_id=1, source_target_pairs={{32,0},{25,1},{18,2},{11,3},{36,4},{29,5},{22,6},{15,7},{40,8},{33... | collective-permute-start | bytes 12296 | tf_op jit(solution)/shard_map/ppermute | solution.py:46
  64.4 1.9 %collective-permute-done.9 = f32[4,256]{1,0:T(4,128)S(1)} collective-permute-done((f32[4,256]{1,0:T(4,128)S(1)}, f32[4,256]{1,0:T(4,128)S(1)}, u32[]{:S(2)}, u32[]{:S(2)}) %collective-permute-start.9) | collective-permute-done | bytes 4128 | tf_op jit(solution)/shard_map/ppermute | solution.py:46
  66.3 2.4 %collective-permute-start.12 = (f32[4,256]{1,0:T(4,128)S(1)}, f32[4,256]{1,0:T(4,128)S(1)}, u32[]{:S(2)}, u32[]{:S(2)}) collective-permute-start(f32[4,256]{1,0:T(4,128)S(1)} %multiply_add_fusion.1), channel_id=1, source_target_pairs={{3,0},{0,1},{1,2},{2,3},{7,4},{4,5},{5,6},{6,7},{11,8},{8,9},{9,10... | collective-permute-start | bytes 12296 | tf_op jit(solution)/shard_map/ppermute | solution.py:46
  68.7 1.0 %collective-permute-start.11 = (f32[4,256]{1,0:T(4,128)S(1)}, f32[4,256]{1,0:T(4,128)S(1)}, u32[]{:S(2)}, u32[]{:S(2)}) collective-permute-start(f32[4,256]{1,0:T(4,128)S(1)} %multiply_add_fusion.1), channel_id=1, source_target_pairs={{1,0},{2,1},{3,2},{0,3},{5,4},{6,5},{7,6},{4,7},{9,8},{10,9},{11,1... | collective-permute-start | bytes 12296 | tf_op jit(solution)/shard_map/ppermute | solution.py:46
  69.7 3.8 %collective-permute-start.10 = (f32[4,256]{1,0:T(4,128)S(1)}, f32[4,256]{1,0:T(4,128)S(1)}, u32[]{:S(2)}, u32[]{:S(2)}) collective-permute-start(f32[4,256]{1,0:T(4,128)S(1)} %multiply_add_fusion.1), channel_id=1, source_target_pairs={{2,0},{3,1},{0,2},{1,3},{6,4},{7,5},{4,6},{5,7},{10,8},{11,9},{8,1... | collective-permute-start | bytes 12296 | tf_op jit(solution)/shard_map/ppermute | solution.py:46
  73.5 1.6 %collective-permute-done.10 = f32[4,256]{1,0:T(4,128)S(1)} collective-permute-done((f32[4,256]{1,0:T(4,128)S(1)}, f32[4,256]{1,0:T(4,128)S(1)}, u32[]{:S(2)}, u32[]{:S(2)}) %collective-permute-start.10) | collective-permute-done | bytes 4128 | tf_op jit(solution)/shard_map/ppermute | solution.py:46
  75.1 0.6 multiply_subtract_fusion
  (15 shorter events, 0.1 us)
Async XLA Ops:
  1.9 15.6 %collective-permute-start.5 = (f32[208,256]{1,0:T(8,128)S(1)}, f32[208,256]{1,0:T(8,128)S(1)}, u32[]{:S(2)}, u32[]{:S(2)}) collective-permute-start(f32[208,256]{1,0:T(8,128)S(1)} %get-tuple-element.16), channel_id=1, source_target_pairs={{32,0},{41,1},{50,2},{59,3},{36,4},{45,5},{54,6},{63,7},{40,8},{49... | collective-permute-start | bytes 638984 | tf_op jit(solution)/shard_map/ppermute | solution.py:46
  7.3 10.1 %collective-permute-start.3 = (f32[208,256]{1,0:T(8,128)S(1)}, f32[208,256]{1,0:T(8,128)S(1)}, u32[]{:S(2)}, u32[]{:S(2)}) collective-permute-start(f32[208,256]{1,0:T(8,128)S(1)} %get-tuple-element.16), channel_id=1, source_target_pairs={{0,0},{9,1},{18,2},{27,3},{4,4},{13,5},{22,6},{31,7},{8,8},{17,9},... | collective-permute-start | bytes 638984 | tf_op jit(solution)/shard_map/ppermute | solution.py:46
  8.0 30.4 %collective-permute-start.2 = (f32[208,256]{1,0:T(8,128)S(1)}, f32[208,256]{1,0:T(8,128)S(1)}, u32[]{:S(2)}, u32[]{:S(2)}) collective-permute-start(f32[208,256]{1,0:T(8,128)S(1)} %get-tuple-element.15.s0), channel_id=1, source_target_pairs={{192,0},{193,1},{194,2},{195,3},{196,4},{197,5},{198,6},{199,7},{2... | collective-permute-start | bytes 638984 | tf_op jit(solution)/shard_map/ppermute | solution.py:46
  9.6 28.8 %collective-permute-start.1 = (f32[208,256]{1,0:T(8,128)S(1)}, f32[208,256]{1,0:T(8,128)S(1)}, u32[]{:S(2)}, u32[]{:S(2)}) collective-permute-start(f32[208,256]{1,0:T(8,128)S(1)} %get-tuple-element.15.s0), channel_id=1, source_target_pairs={{128,0},{129,1},{130,2},{131,3},{132,4},{133,5},{134,6},{135,7},{1... | collective-permute-start | bytes 638984 | tf_op jit(solution)/shard_map/ppermute | solution.py:46
  12.5 25.9 %collective-permute-start = (f32[208,256]{1,0:T(8,128)S(1)}, f32[208,256]{1,0:T(8,128)S(1)}, u32[]{:S(2)}, u32[]{:S(2)}) collective-permute-start(f32[208,256]{1,0:T(8,128)S(1)} %get-tuple-element.15.s0), channel_id=1, source_target_pairs={{64,0},{65,1},{66,2},{67,3},{68,4},{69,5},{70,6},{71,7},{72,8},{73... | collective-permute-start | bytes 638984 | tf_op jit(solution)/shard_map/ppermute | solution.py:46
  17.4 21.0 %collective-permute-start.6 = (f32[208,256]{1,0:T(8,128)S(1)}, f32[208,256]{1,0:T(8,128)S(1)}, u32[]{:S(2)}, u32[]{:S(2)}) collective-permute-start(f32[208,256]{1,0:T(8,128)S(1)} %collective-permute-done.5.t2), channel_id=1, source_target_pairs={{4,0},{5,1},{6,2},{7,3},{0,4},{1,5},{2,6},{3,7},{12,8},{13,9},{14,... | collective-permute-start | bytes 638984 | tf_op jit(solution)/shard_map/ppermute | solution.py:46
  17.4 21.0 %collective-permute-start.4 = (f32[208,256]{1,0:T(8,128)S(1)}, f32[208,256]{1,0:T(8,128)S(1)}, u32[]{:S(2)}, u32[]{:S(2)}) collective-permute-start(f32[208,256]{1,0:T(8,128)S(1)} %collective-permute-done.3.t0), channel_id=1, source_target_pairs={{4,0},{5,1},{6,2},{7,3},{0,4},{1,5},{2,6},{3,7},{12,8},{13,9},{14,... | collective-permute-start | bytes 638984 | tf_op jit(solution)/shard_map/ppermute | solution.py:46
  53.5 21.6 %copy-start = (f32[4,256]{1,0:T(4,128)S(1)}, f32[4,256]{1,0:T(4,128)}, u32[]{:S(2)}) copy-start(f32[4,256]{1,0:T(4,128)} %extra_in.1) | copy-start | bytes 12292
  53.5 21.6 %copy-start.1 = (f32[4,256]{1,0:T(4,128)S(1)}, f32[4,256]{1,0:T(4,128)}, u32[]{:S(2)}) copy-start(f32[4,256]{1,0:T(4,128)} %param.10) | copy-start | bytes 12292
  56.8 1.3 %collective-permute-start.7 = (f32[8,256]{1,0:T(8,128)S(1)}, f32[8,256]{1,0:T(8,128)S(1)}, u32[]{:S(2)}, u32[]{:S(2)}) collective-permute-start(f32[8,256]{1,0:T(8,128)S(1)} %get-tuple-element.25), channel_id=1, source_target_pairs={{4,0},{5,1},{6,2},{7,3},{0,4},{1,5},{2,6},{3,7},{12,8},{13,9},{14,... | collective-permute-start | bytes 24584 | tf_op jit(solution)/shard_map/ppermute | solution.py:46
  58.1 6.4 %collective-permute-start.8 = (f32[4,256]{1,0:T(4,128)S(1)}, f32[4,256]{1,0:T(4,128)S(1)}, u32[]{:S(2)}, u32[]{:S(2)}) collective-permute-start(f32[4,256]{1,0:T(4,128)S(1)} %get-tuple-element.26), channel_id=1, source_target_pairs={{0,0},{57,1},{50,2},{43,3},{4,4},{61,5},{54,6},{47,7},{8,8},{1,9},... | collective-permute-start | bytes 12296 | tf_op jit(solution)/shard_map/ppermute | solution.py:46
  58.7 7.6 %collective-permute-start.9 = (f32[4,256]{1,0:T(4,128)S(1)}, f32[4,256]{1,0:T(4,128)S(1)}, u32[]{:S(2)}, u32[]{:S(2)}) collective-permute-start(f32[4,256]{1,0:T(4,128)S(1)} %get-tuple-element.27), channel_id=1, source_target_pairs={{32,0},{25,1},{18,2},{11,3},{36,4},{29,5},{22,6},{15,7},{40,8},{33... | collective-permute-start | bytes 12296 | tf_op jit(solution)/shard_map/ppermute | solution.py:46
  66.3 7.2 %collective-permute-start.12 = (f32[4,256]{1,0:T(4,128)S(1)}, f32[4,256]{1,0:T(4,128)S(1)}, u32[]{:S(2)}, u32[]{:S(2)}) collective-permute-start(f32[4,256]{1,0:T(4,128)S(1)} %multiply_add_fusion.1), channel_id=1, source_target_pairs={{3,0},{0,1},{1,2},{2,3},{7,4},{4,5},{5,6},{6,7},{11,8},{8,9},{9,10... | collective-permute-start | bytes 12296 | tf_op jit(solution)/shard_map/ppermute | solution.py:46
  68.7 4.8 %collective-permute-start.11 = (f32[4,256]{1,0:T(4,128)S(1)}, f32[4,256]{1,0:T(4,128)S(1)}, u32[]{:S(2)}, u32[]{:S(2)}) collective-permute-start(f32[4,256]{1,0:T(4,128)S(1)} %multiply_add_fusion.1), channel_id=1, source_target_pairs={{1,0},{2,1},{3,2},{0,3},{5,4},{6,5},{7,6},{4,7},{9,8},{10,9},{11,1... | collective-permute-start | bytes 12296 | tf_op jit(solution)/shard_map/ppermute | solution.py:46
  69.7 5.4 %collective-permute-start.10 = (f32[4,256]{1,0:T(4,128)S(1)}, f32[4,256]{1,0:T(4,128)S(1)}, u32[]{:S(2)}, u32[]{:S(2)}) collective-permute-start(f32[4,256]{1,0:T(4,128)S(1)} %multiply_add_fusion.1), channel_id=1, source_target_pairs={{2,0},{3,1},{0,2},{1,3},{6,4},{7,5},{4,6},{5,7},{10,8},{11,9},{8,1... | collective-permute-start | bytes 12296 | tf_op jit(solution)/shard_map/ppermute | solution.py:46

commit v8 on v7

--- a/solution.py
+++ b/solution.py
@@ -16,7 +16,7 @@
 COMP = 50
 CL = 4
 CELLS = 256
-PACKED = 52
+PACKED = 56
 NY, NZ, NC, NX = 4, 8, 2, 4
 AXES = ("own", "split")
 
@@ -94,7 +94,7 @@
 def load_cluster(ref, a, middle):
     at = PACKED * a
     top = ref[at : at + 48, :] - middle[0:48]
-    tail = jnp.concatenate([ref[at + 48 : at + PACKED, :], jnp.zeros((4, CELLS), f32)], axis=0)
+    tail = ref[at + 48 : at + PACKED, :]
     row = lax.broadcasted_iota(jnp.int32, (8, CELLS), 0)
     extra = tail[2:3, :]
     tail = jnp.where(row < 2, tail - middle[48:56], 0.0)
@@ -258,7 +258,7 @@
     leaving.wait()
 
 
-def column_kernel(list_in, came, mass, square, x_in, yn, kept, given, potential, list_ref, xn, xt, four, top, tot, *rest):
+def column_kernel(list_in, came, mass, square, x_in, yn, kept, given, own, list_ref, xn, xt, four, top, tot, *rest):
     scores, tops, sem = rest[:DEEP], rest[DEEP : 2 * DEEP], rest[2 * DEEP]
     arriving = pltpu.make_async_copy(list_in, list_ref, sem.at[0])
     arriving.start()
@@ -267,11 +267,11 @@
     row = lax.broadcasted_iota(jnp.int32, (16, CELLS), 0)
     for k in range(4):
         rows = four[(y + k) % NY]
+        if k == 0:
+            own[...] = rows
         for a in range(CL):
             n = k * CL + a
             p = EPSILON * mass[n : n + 1, :] - (EPSILON * LN2) * rows[a : a + 1]
-            if k == 0:
-                potential[a : a + 1, :] = p
             weight = three_parts((p - square[n : n + 1, :]) * SCALE)
             xn[...] = x_in[n]
             end = xn[48:64, :].astype(f32)
@@ -364,7 +364,7 @@
 
     rows = exchanged(rows, PLANES)
 
-    kept, given, source_potential = pl.pallas_call(
+    kept, given, own = pl.pallas_call(
         column_kernel,
         out_shape=(
             jax.ShapeDtypeStruct((2 * CL, CELLS), f32),
@@ -391,6 +391,7 @@
     opposite = from_x(part, 2)
     part = merged([part, opposite] + [from_x(part, k) for k in (1, 3)])
     target_potential = EPSILON * target_logmass + target_prior - (EPSILON * LN2) * part
+    source_potential = EPSILON * source_logmass - (EPSILON * LN2) * own
     return source_potential, target_potential
 
 

time: 76.5 us -> 78.2 us (1.022)
  waiting for transfers between devices: 8.22 us -> 9.46 us
    ppermute x13, waiting for transfers between devices: 8.22 us -> 9.46 us  [fetched(): return lax.ppermute(value, AXES, pairs)]
  transfers between devices with their start and end apart: 13 -> 13, of which waited for: 4 -> 5; matrix products, arithmetic and copies ran while one was open for 0% -> 1% of each run, Pallas kernels for 0% -> 0%
where the time goes in v8:
time: 78.2 us; the launch traced here: 77 us
  blocking collectives  31.9 us (41%)
  starting transfers between devices  26.5 us (34%)
  waiting for transfers between devices  9.46 us (12%)
  Pallas kernels  7.1 us (9%)
  other arithmetic  1.25 us (2%)
    all_to_all x2, blocking collectives, exchanged(): lax.all_to_all(value, AXES, 0, 0, axis_index_groups=groups, tiled=True)  31.9 us
    ppermute x13, starting transfers between devices, fetched(): return lax.ppermute(value, AXES, pairs)  26.5 us
    ppermute x13, waiting for transfers between devices, fetched(): return lax.ppermute(value, AXES, pairs)  9.46 us
    pallas_call x1, Pallas kernels, work(): pl.pallas_call(row_kernel, out_shape=(jax.ShapeDtypeStruct((MEMBERS, 4, C...  3.31 us
    pallas_call x1, Pallas kernels, work(): pl.pallas_call(column_kernel, out_shape=(jax.ShapeDtypeStruct((2 * CL, CE...  2.58 us
  transfers between devices with their start and end apart: 13, of which 5 were waited for; matrix products, arithmetic and copies ran while one was open for 1% of the time, Pallas kernels for 0%

profile of v8, /device:TPU:64, one launch (start us, length us, event | category | flops | bytes accessed | tf_op | source)
XLA Modules:
  0.0 77.0 jit_solution(5267448456946172645)
XLA Ops:
  0.6 1.2 %pack.1 = (f32[224,256]{1,0:T(8,128)S(1)}, f32[224,256]{1,0:T(8,128)S(1)}, s32[16,1,64]{2,1,0:T(1,128)S(1)}) custom-call(f32[50,4,256]{2,1,0:T(4,128)} %bitcast.6, f32[4,256]{1,0:T(4,128)} %extra_in.1, f32[50,4,256]{2,1,0:T(4,128)} %bitcast.7, f32[4,256]{1,0:T(4,128)} %more_extra_in.1, s32[1,64]{1,0:T(1,128)} %bitcast.8, s32[1,64]{1,0:T(1,128)} %bitcast.9), custom_call_target="tpu_custom_call" | custom-call | tf_op jit(solution)/shard_map/pack/pallas_call | solution.py:305
  1.9 5.5 %collective-permute-start.5 = (f32[224,256]{1,0:T(8,128)S(1)}, f32[224,256]{1,0:T(8,128)S(1)}, u32[]{:S(2)}, u32[]{:S(2)}) collective-permute-start(f32[224,256]{1,0:T(8,128)S(1)} %get-tuple-element.16), channel_id=1, source_target_pairs={{32,0},{41,1},{50,2},{59,3},{36,4},{45,5},{54,6},{63,7},{40,8},{49... | collective-permute-start | bytes 688136 | tf_op jit(solution)/shard_map/ppermute | solution.py:46
  7.3 0.7 collective-permute-start.3
  8.0 1.7 %collective-permute-start.2 = (f32[224,256]{1,0:T(8,128)S(1)}, f32[224,256]{1,0:T(8,128)S(1)}, u32[]{:S(2)}, u32[]{:S(2)}) collective-permute-start(f32[224,256]{1,0:T(8,128)S(1)} %get-tuple-element.15.s0), channel_id=1, source_target_pairs={{192,0},{193,1},{194,2},{195,3},{196,4},{197,5},{198,6},{199,7},{2... | collective-permute-start | bytes 688136 | tf_op jit(solution)/shard_map/ppermute | solution.py:46
  9.6 2.9 %collective-permute-start.1 = (f32[224,256]{1,0:T(8,128)S(1)}, f32[224,256]{1,0:T(8,128)S(1)}, u32[]{:S(2)}, u32[]{:S(2)}) collective-permute-start(f32[224,256]{1,0:T(8,128)S(1)} %get-tuple-element.15.s0), channel_id=1, source_target_pairs={{128,0},{129,1},{130,2},{131,3},{132,4},{133,5},{134,6},{135,7},{1... | collective-permute-start | bytes 688136 | tf_op jit(solution)/shard_map/ppermute | solution.py:46
  12.5 1.3 %collective-permute-start = (f32[224,256]{1,0:T(8,128)S(1)}, f32[224,256]{1,0:T(8,128)S(1)}, u32[]{:S(2)}, u32[]{:S(2)}) collective-permute-start(f32[224,256]{1,0:T(8,128)S(1)} %get-tuple-element.15.s0), channel_id=1, source_target_pairs={{64,0},{65,1},{66,2},{67,3},{68,4},{69,5},{70,6},{71,7},{72,8},{73... | collective-permute-start | bytes 688136 | tf_op jit(solution)/shard_map/ppermute | solution.py:46
  13.9 4.3 %collective-permute-done.5.t2 = f32[224,256]{1,0:T(8,128)S(1)} collective-permute-done((f32[224,256]{1,0:T(8,128)S(1)}, f32[224,256]{1,0:T(8,128)S(1)}, u32[]{:S(2)}, u32[]{:S(2)}) %collective-permute-start.5) | collective-permute-done | bytes 229408 | tf_op jit(solution)/shard_map/ppermute | solution.py:46
  18.2 0.0 collective-permute-done.3.t0
  18.2 0.5 collective-permute-start.4
  18.8 20.3 %all_to_all.10 = s32[16,1,64]{2,1,0:T(1,128)S(1)} all-to-all(s32[16,1,64]{2,1,0:T(1,128)S(1)} %get-tuple-element.14), channel_id=1, replica_groups={{0,64,128,192,1,65,129,193,2,66,130,194,3,67,131,195},{4,68,132,196,5,6..., dimensions={0} | all-to-all | bytes 8192 | tf_op jit(solution)/shard_map/all_to_all | solution.py:62
  39.1 3.3 %rows.1 = (f32[16,4,4,256]{3,2,1,0:T(4,128)S(1)}, s32[80]{0:T(128)S(1)}, bf16[17,128,256]{2,1,0:T(8,128)(2,1)S(1)}, bf16[16,128,256]{2,1,0:T(8,128)(2,1)S(1)}, f...) custom-call(s32[16,64]{1,0:T(8,128)S(1)} %bitcast.5, f32[224,256]{1,0:T(8,128)S(1)} %get-tuple-element.15.s0, ...), custom_call_target="tpu_custom_call" | custom-call | tf_op jit(solution)/shard_map/rows/pallas_call | solution.py:343
  42.4 11.7 %all_to_all.11.came = f32[16,4,4,256]{3,2,1,0:T(4,128)S(1)} all-to-all(f32[16,4,4,256]{3,2,1,0:T(4,128)S(1)} %get-tuple-element.18), channel_id=1, replica_groups={{0,64,128,192,1,65,129,193,2,66,130,194,3,67,131,195},{4,68,132,196,5,6..., dimensions={0} | all-to-all | bytes 524288 | tf_op jit(solution)/shard_map/all_to_all | solution.py:62
  54.0 2.6 %columns.1 = (f32[8,256]{1,0:T(8,128)S(1)}, f32[8,256]{1,0:T(8,128)S(1)}, f32[4,256]{1,0:T(4,128)S(1)}) custom-call(s32[80]{0:T(128)S(1)} %get-tuple-element.17.list_in, f32[16,4,4,256]{3,2,1,0:T(4,128)S(1)} %all_to_all.11.came, f32[16,256]{1,0:T(8,128)S(1)} %get-tuple-element.19.mass, f32[16,256]{1,0:T(8,128)S(1)} %get-tuple-element.20.square, ...), custom_call_target="tpu_custom_call" | custom-call | tf_op jit(solution)/shard_map/columns/pallas_call | solution.py:367
  56.6 0.1 collective-permute-start.7
  56.7 1.2 %collective-permute-done.7 = f32[8,256]{1,0:T(8,128)S(1)} collective-permute-done((f32[8,256]{1,0:T(8,128)S(1)}, f32[8,256]{1,0:T(8,128)S(1)}, u32[]{:S(2)}, u32[]{:S(2)}) %collective-permute-start.7) | collective-permute-done | bytes 8224 | tf_op jit(solution)/shard_map/ppermute | solution.py:46
  57.9 0.7 collective-permute-start.8
  58.6 6.2 %collective-permute-start.9 = (f32[4,256]{1,0:T(4,128)S(1)}, f32[4,256]{1,0:T(4,128)S(1)}, u32[]{:S(2)}, u32[]{:S(2)}) collective-permute-start(f32[4,256]{1,0:T(4,128)S(1)} %get-tuple-element.27), channel_id=1, source_target_pairs={{32,0},{25,1},{18,2},{11,3},{36,4},{29,5},{22,6},{15,7},{40,8},{33... | collective-permute-start | bytes 12296 | tf_op jit(solution)/shard_map/ppermute | solution.py:46
  64.8 1.6 %collective-permute-done.9 = f32[4,256]{1,0:T(4,128)S(1)} collective-permute-done((f32[4,256]{1,0:T(4,128)S(1)}, f32[4,256]{1,0:T(4,128)S(1)}, u32[]{:S(2)}, u32[]{:S(2)}) %collective-permute-start.9) | collective-permute-done | bytes 4128 | tf_op jit(solution)/shard_map/ppermute | solution.py:46
  66.4 4.8 %collective-permute-start.12 = (f32[4,256]{1,0:T(4,128)S(1)}, f32[4,256]{1,0:T(4,128)S(1)}, u32[]{:S(2)}, u32[]{:S(2)}) collective-permute-start(f32[4,256]{1,0:T(4,128)S(1)} %multiply_add_fusion.1), channel_id=1, source_target_pairs={{3,0},{0,1},{1,2},{2,3},{7,4},{4,5},{5,6},{6,7},{11,8},{8,9},{9,10... | collective-permute-start | bytes 12296 | tf_op jit(solution)/shard_map/ppermute | solution.py:46
  71.3 2.2 %collective-permute-start.10 = (f32[4,256]{1,0:T(4,128)S(1)}, f32[4,256]{1,0:T(4,128)S(1)}, u32[]{:S(2)}, u32[]{:S(2)}) collective-permute-start(f32[4,256]{1,0:T(4,128)S(1)} %multiply_add_fusion.1), channel_id=1, source_target_pairs={{2,0},{3,1},{0,2},{1,3},{6,4},{7,5},{4,6},{5,7},{10,8},{11,9},{8,1... | collective-permute-start | bytes 12296 | tf_op jit(solution)/shard_map/ppermute | solution.py:46
  73.4 0.6 multiply_subtract_fusion.1
  74.0 0.8 %collective-permute-done.11 = f32[4,256]{1,0:T(4,128)S(1)} collective-permute-done((f32[4,256]{1,0:T(4,128)S(1)}, f32[4,256]{1,0:T(4,128)S(1)}, u32[]{:S(2)}, u32[]{:S(2)}) %collective-permute-start.11) | collective-permute-done | bytes 4128 | tf_op jit(solution)/shard_map/ppermute | solution.py:46
  74.9 1.5 %collective-permute-done.10 = f32[4,256]{1,0:T(4,128)S(1)} collective-permute-done((f32[4,256]{1,0:T(4,128)S(1)}, f32[4,256]{1,0:T(4,128)S(1)}, u32[]{:S(2)}, u32[]{:S(2)}) %collective-permute-start.10) | collective-permute-done | bytes 4128 | tf_op jit(solution)/shard_map/ppermute | solution.py:46
  76.4 0.6 multiply_subtract_fusion
  (18 shorter events, 0.1 us)
Async XLA Ops:
  1.9 16.4 %collective-permute-start.5 = (f32[224,256]{1,0:T(8,128)S(1)}, f32[224,256]{1,0:T(8,128)S(1)}, u32[]{:S(2)}, u32[]{:S(2)}) collective-permute-start(f32[224,256]{1,0:T(8,128)S(1)} %get-tuple-element.16), channel_id=1, source_target_pairs={{32,0},{41,1},{50,2},{59,3},{36,4},{45,5},{54,6},{63,7},{40,8},{49... | collective-permute-start | bytes 688136 | tf_op jit(solution)/shard_map/ppermute | solution.py:46
  7.3 10.9 %collective-permute-start.3 = (f32[224,256]{1,0:T(8,128)S(1)}, f32[224,256]{1,0:T(8,128)S(1)}, u32[]{:S(2)}, u32[]{:S(2)}) collective-permute-start(f32[224,256]{1,0:T(8,128)S(1)} %get-tuple-element.16), channel_id=1, source_target_pairs={{0,0},{9,1},{18,2},{27,3},{4,4},{13,5},{22,6},{31,7},{8,8},{17,9},... | collective-permute-start | bytes 688136 | tf_op jit(solution)/shard_map/ppermute | solution.py:46
  8.0 31.0 %collective-permute-start.2 = (f32[224,256]{1,0:T(8,128)S(1)}, f32[224,256]{1,0:T(8,128)S(1)}, u32[]{:S(2)}, u32[]{:S(2)}) collective-permute-start(f32[224,256]{1,0:T(8,128)S(1)} %get-tuple-element.15.s0), channel_id=1, source_target_pairs={{192,0},{193,1},{194,2},{195,3},{196,4},{197,5},{198,6},{199,7},{2... | collective-permute-start | bytes 688136 | tf_op jit(solution)/shard_map/ppermute | solution.py:46
  9.6 29.4 %collective-permute-start.1 = (f32[224,256]{1,0:T(8,128)S(1)}, f32[224,256]{1,0:T(8,128)S(1)}, u32[]{:S(2)}, u32[]{:S(2)}) collective-permute-start(f32[224,256]{1,0:T(8,128)S(1)} %get-tuple-element.15.s0), channel_id=1, source_target_pairs={{128,0},{129,1},{130,2},{131,3},{132,4},{133,5},{134,6},{135,7},{1... | collective-permute-start | bytes 688136 | tf_op jit(solution)/shard_map/ppermute | solution.py:46
  12.5 26.5 %collective-permute-start = (f32[224,256]{1,0:T(8,128)S(1)}, f32[224,256]{1,0:T(8,128)S(1)}, u32[]{:S(2)}, u32[]{:S(2)}) collective-permute-start(f32[224,256]{1,0:T(8,128)S(1)} %get-tuple-element.15.s0), channel_id=1, source_target_pairs={{64,0},{65,1},{66,2},{67,3},{68,4},{69,5},{70,6},{71,7},{72,8},{73... | collective-permute-start | bytes 688136 | tf_op jit(solution)/shard_map/ppermute | solution.py:46
  18.2 20.8 %collective-permute-start.6 = (f32[224,256]{1,0:T(8,128)S(1)}, f32[224,256]{1,0:T(8,128)S(1)}, u32[]{:S(2)}, u32[]{:S(2)}) collective-permute-start(f32[224,256]{1,0:T(8,128)S(1)} %collective-permute-done.5.t2), channel_id=1, source_target_pairs={{4,0},{5,1},{6,2},{7,3},{0,4},{1,5},{2,6},{3,7},{12,8},{13,9},{14,... | collective-permute-start | bytes 688136 | tf_op jit(solution)/shard_map/ppermute | solution.py:46
  18.2 20.8 %collective-permute-start.4 = (f32[224,256]{1,0:T(8,128)S(1)}, f32[224,256]{1,0:T(8,128)S(1)}, u32[]{:S(2)}, u32[]{:S(2)}) collective-permute-start(f32[224,256]{1,0:T(8,128)S(1)} %collective-permute-done.3.t0), channel_id=1, source_target_pairs={{4,0},{5,1},{6,2},{7,3},{0,4},{1,5},{2,6},{3,7},{12,8},{13,9},{14,... | collective-permute-start | bytes 688136 | tf_op jit(solution)/shard_map/ppermute | solution.py:46
  54.0 19.4 %copy-start = (f32[4,256]{1,0:T(4,128)S(1)}, f32[4,256]{1,0:T(4,128)}, u32[]{:S(2)}) copy-start(f32[4,256]{1,0:T(4,128)} %more_extra_in.1) | copy-start | bytes 12292
  54.0 22.3 %copy-start.1 = (f32[4,256]{1,0:T(4,128)S(1)}, f32[4,256]{1,0:T(4,128)}, u32[]{:S(2)}) copy-start(f32[4,256]{1,0:T(4,128)} %extra_in.1) | copy-start | bytes 12292
  54.0 22.3 %copy-start.2 = (f32[4,256]{1,0:T(4,128)S(1)}, f32[4,256]{1,0:T(4,128)}, u32[]{:S(2)}) copy-start(f32[4,256]{1,0:T(4,128)} %param.10) | copy-start | bytes 12292
  56.6 1.3 %collective-permute-start.7 = (f32[8,256]{1,0:T(8,128)S(1)}, f32[8,256]{1,0:T(8,128)S(1)}, u32[]{:S(2)}, u32[]{:S(2)}) collective-permute-start(f32[8,256]{1,0:T(8,128)S(1)} %get-tuple-element.25), channel_id=1, source_target_pairs={{4,0},{5,1},{6,2},{7,3},{0,4},{1,5},{2,6},{3,7},{12,8},{13,9},{14,... | collective-permute-start | bytes 24584 | tf_op jit(solution)/shard_map/ppermute | solution.py:46
  57.9 6.9 %collective-permute-start.8 = (f32[4,256]{1,0:T(4,128)S(1)}, f32[4,256]{1,0:T(4,128)S(1)}, u32[]{:S(2)}, u32[]{:S(2)}) collective-permute-start(f32[4,256]{1,0:T(4,128)S(1)} %get-tuple-element.26), channel_id=1, source_target_pairs={{0,0},{57,1},{50,2},{43,3},{4,4},{61,5},{54,6},{47,7},{8,8},{1,9},... | collective-permute-start | bytes 12296 | tf_op jit(solution)/shard_map/ppermute | solution.py:46
  58.6 7.8 %collective-permute-start.9 = (f32[4,256]{1,0:T(4,128)S(1)}, f32[4,256]{1,0:T(4,128)S(1)}, u32[]{:S(2)}, u32[]{:S(2)}) collective-permute-start(f32[4,256]{1,0:T(4,128)S(1)} %get-tuple-element.27), channel_id=1, source_target_pairs={{32,0},{25,1},{18,2},{11,3},{36,4},{29,5},{22,6},{15,7},{40,8},{33... | collective-permute-start | bytes 12296 | tf_op jit(solution)/shard_map/ppermute | solution.py:46
  66.4 7.6 %collective-permute-start.12 = (f32[4,256]{1,0:T(4,128)S(1)}, f32[4,256]{1,0:T(4,128)S(1)}, u32[]{:S(2)}, u32[]{:S(2)}) collective-permute-start(f32[4,256]{1,0:T(4,128)S(1)} %multiply_add_fusion.1), channel_id=1, source_target_pairs={{3,0},{0,1},{1,2},{2,3},{7,4},{4,5},{5,6},{6,7},{11,8},{8,9},{9,10... | collective-permute-start | bytes 12296 | tf_op jit(solution)/shard_map/ppermute | solution.py:46
  71.3 3.6 %collective-permute-start.11 = (f32[4,256]{1,0:T(4,128)S(1)}, f32[4,256]{1,0:T(4,128)S(1)}, u32[]{:S(2)}, u32[]{:S(2)}) collective-permute-start(f32[4,256]{1,0:T(4,128)S(1)} %multiply_add_fusion.1), channel_id=1, source_target_pairs={{1,0},{2,1},{3,2},{0,3},{5,4},{6,5},{7,6},{4,7},{9,8},{10,9},{11,1... | collective-permute-start | bytes 12296 | tf_op jit(solution)/shard_map/ppermute | solution.py:46
  71.3 5.1 %collective-permute-start.10 = (f32[4,256]{1,0:T(4,128)S(1)}, f32[4,256]{1,0:T(4,128)S(1)}, u32[]{:S(2)}, u32[]{:S(2)}) collective-permute-start(f32[4,256]{1,0:T(4,128)S(1)} %multiply_add_fusion.1), channel_id=1, source_target_pairs={{2,0},{3,1},{0,2},{1,3},{6,4},{7,5},{4,6},{5,7},{10,8},{11,9},{8,1... | collective-permute-start | bytes 12296 | tf_op jit(solution)/shard_map/ppermute | solution.py:46

commit v9 on v5

--- a/solution.py
+++ b/solution.py
@@ -250,7 +250,7 @@
     leaving.wait()
 
 
-def column_kernel(list_in, came, mass, square, x_in, yn, kept, given, potential, list_ref, xn, xt, four, top, tot, *rest):
+def column_kernel(list_in, came, mass, square, x_in, yn, kept, given, own, list_ref, xn, xt, four, top, tot, *rest):
     scores, tops, sem = rest[:DEEP], rest[DEEP : 2 * DEEP], rest[2 * DEEP]
     arriving = pltpu.make_async_copy(list_in, list_ref, sem.at[0])
     arriving.start()
@@ -259,11 +259,11 @@
     row = lax.broadcasted_iota(jnp.int32, (16, CELLS), 0)
     for k in range(4):
         rows = four[(y + k) % NY]
+        if k == 0:
+            own[...] = rows
         for a in range(CL):
             n = k * CL + a
             p = EPSILON * mass[n : n + 1, :] - (EPSILON * LN2) * rows[a : a + 1]
-            if k == 0:
-                potential[a : a + 1, :] = p
             weight = three_parts((p - square[n : n + 1, :]) * SCALE)
             xn[...] = x_in[n]
             end = xn[48:64, :].astype(f32)
@@ -354,7 +354,7 @@
 
     rows = exchanged(rows, PLANES)
 
-    kept, given, source_potential = pl.pallas_call(
+    kept, given, own = pl.pallas_call(
         column_kernel,
         out_shape=(
             jax.ShapeDtypeStruct((2 * CL, CELLS), f32),
@@ -380,6 +380,7 @@
     part = merged([first, second])
     part = merged([part] + [from_x(part, k) for k in (1, 2, 3)])
     target_potential = EPSILON * target_logmass + target_prior - (EPSILON * LN2) * part
+    source_potential = EPSILON * source_logmass - (EPSILON * LN2) * own
     return source_potential, target_potential
 
 

time: 78.5 us -> 77.9 us (level)
  transfers between devices with their start and end apart: 13 -> 13, of which waited for: 4 -> 4; matrix products, arithmetic and copies ran while one was open for 1% -> 2% of each run, Pallas kernels for 0% -> 0%
where the time goes in v9:
time: 77.9 us; the launch traced here: 77.6 us
  blocking collectives  31.9 us (41%)
  starting transfers between devices  27.1 us (35%)
  waiting for transfers between devices  8.85 us (11%)
  Pallas kernels  7.06 us (9%)
  other arithmetic  1.93 us (2%)
    all_to_all x2, blocking collectives, exchanged(): lax.all_to_all(value, AXES, 0, 0, axis_index_groups=groups, tiled=True)  31.9 us
    ppermute x13, starting transfers between devices, fetched(): return lax.ppermute(value, AXES, pairs)  27.1 us
    ppermute x13, waiting for transfers between devices, fetched(): return lax.ppermute(value, AXES, pairs)  8.85 us
    pallas_call x1, Pallas kernels, work(): pl.pallas_call(row_kernel, out_shape=(jax.ShapeDtypeStruct((MEMBERS, 4, C...  3.32 us
    pallas_call x1, Pallas kernels, work(): pl.pallas_call(column_kernel, out_shape=(jax.ShapeDtypeStruct((2 * CL, CE...  2.59 us
  transfers between devices with their start and end apart: 13, of which 4 were waited for; matrix products, arithmetic and copies ran while one was open for 2% of the time, Pallas kernels for 0%

profile of v9, /device:TPU:64, one launch (start us, length us, event | category | flops | bytes accessed | tf_op | source)
XLA Modules:
  0.0 77.6 jit_solution(12135485852662620547)
XLA Ops:
  0.6 1.2 %pack.1 = (f32[4,56,256]{2,1,0:T(8,128)S(1)}, f32[4,56,256]{2,1,0:T(8,128)S(1)}) custom-call(f32[50,4,256]{2,1,0:T(4,128)} %bitcast.6, f32[4,256]{1,0:T(4,128)} %extra_in.1, f32[50,4,256]{2,1,0:T(4,128)} %bitcast.7, f32[4,256]{1,0:T(4,128)} %more_extra_in.1), custom_call_target="tpu_custom_call" | custom-call | tf_op jit(solution)/shard_map/pack/pallas_call | solution.py:301
  1.8 5.5 %collective-permute-start.5 = (f32[4,56,256]{2,1,0:T(8,128)S(1)}, f32[4,56,256]{2,1,0:T(8,128)S(1)}, u32[]{:S(2)}, u32[]{:S(2)}) collective-permute-start(f32[4,56,256]{2,1,0:T(8,128)S(1)} %get-tuple-element.14), channel_id=1, source_target_pairs={{32,0},{41,1},{50,2},{59,3},{36,4},{45,5},{54,6},{63,7},{40,8},{49... | collective-permute-start | bytes 688136 | tf_op jit(solution)/shard_map/ppermute | solution.py:46
  7.3 0.7 collective-permute-start.3
  7.9 1.7 %collective-permute-start.2 = (f32[4,56,256]{2,1,0:T(8,128)S(1)}, f32[4,56,256]{2,1,0:T(8,128)S(1)}, u32[]{:S(2)}, u32[]{:S(2)}) collective-permute-start(f32[4,56,256]{2,1,0:T(8,128)S(1)} %get-tuple-element.13.s0), channel_id=1, source_target_pairs={{192,0},{193,1},{194,2},{195,3},{196,4},{197,5},{198,6},{199,7},{2... | collective-permute-start | bytes 688136 | tf_op jit(solution)/shard_map/ppermute | solution.py:46
  9.6 2.9 %collective-permute-start.1 = (f32[4,56,256]{2,1,0:T(8,128)S(1)}, f32[4,56,256]{2,1,0:T(8,128)S(1)}, u32[]{:S(2)}, u32[]{:S(2)}) collective-permute-start(f32[4,56,256]{2,1,0:T(8,128)S(1)} %get-tuple-element.13.s0), channel_id=1, source_target_pairs={{128,0},{129,1},{130,2},{131,3},{132,4},{133,5},{134,6},{135,7},{1... | collective-permute-start | bytes 688136 | tf_op jit(solution)/shard_map/ppermute | solution.py:46
  12.5 1.3 %collective-permute-start = (f32[4,56,256]{2,1,0:T(8,128)S(1)}, f32[4,56,256]{2,1,0:T(8,128)S(1)}, u32[]{:S(2)}, u32[]{:S(2)}) collective-permute-start(f32[4,56,256]{2,1,0:T(8,128)S(1)} %get-tuple-element.13.s0), channel_id=1, source_target_pairs={{64,0},{65,1},{66,2},{67,3},{68,4},{69,5},{70,6},{71,7},{72,8},{73... | collective-permute-start | bytes 688136 | tf_op jit(solution)/shard_map/ppermute | solution.py:46
  13.8 4.3 %collective-permute-done.5.t2 = f32[4,56,256]{2,1,0:T(8,128)S(1)} collective-permute-done((f32[4,56,256]{2,1,0:T(8,128)S(1)}, f32[4,56,256]{2,1,0:T(8,128)S(1)}, u32[]{:S(2)}, u32[]{:S(2)}) %collective-permute-start.5) | collective-permute-done | bytes 229408 | tf_op jit(solution)/shard_map/ppermute | solution.py:46
  18.2 0.5 collective-permute-start.4
  18.7 0.7 fusion.4
  19.4 20.3 %all_to_all.13 = s32[16,1,64]{2,1,0:T(1,128)S(1)} all-to-all(s32[16,1,64]{2,1,0:T(1,128)S(1)} %broadcast_in_dim.13), channel_id=1, replica_groups={{0,64,128,192,1,65,129,193,2,66,130,194,3,67,131,195},{4,68,132,196,5,6..., dimensions={0} | all-to-all | bytes 8192 | tf_op jit(solution)/shard_map/all_to_all | solution.py:62
  39.7 3.3 %rows.1 = (f32[16,4,4,256]{3,2,1,0:T(4,128)S(1)}, s32[80]{0:T(128)S(1)}, bf16[17,128,256]{2,1,0:T(8,128)(2,1)S(1)}, bf16[16,128,256]{2,1,0:T(8,128)(2,1)S(1)}, f...) custom-call(s32[16,64]{1,0:T(8,128)S(1)} %bitcast.5, f32[4,56,256]{2,1,0:T(8,128)S(1)} %get-tuple-element.13.s0, ...), custom_call_target="tpu_custom_call" | custom-call | tf_op jit(solution)/shard_map/rows/pallas_call | solution.py:333
  43.0 11.7 %all_to_all.14.came = f32[16,4,4,256]{3,2,1,0:T(4,128)S(1)} all-to-all(f32[16,4,4,256]{3,2,1,0:T(4,128)S(1)} %get-tuple-element.16), channel_id=1, replica_groups={{0,64,128,192,1,65,129,193,2,66,130,194,3,67,131,195},{4,68,132,196,5,6..., dimensions={0} | all-to-all | bytes 524288 | tf_op jit(solution)/shard_map/all_to_all | solution.py:62
  54.7 2.6 %columns.1 = (f32[8,256]{1,0:T(8,128)S(1)}, f32[8,256]{1,0:T(8,128)S(1)}, f32[4,256]{1,0:T(4,128)S(1)}) custom-call(s32[80]{0:T(128)S(1)} %get-tuple-element.15.list_in, f32[16,4,4,256]{3,2,1,0:T(4,128)S(1)} %all_to_all.14.came, f32[16,256]{1,0:T(8,128)S(1)} %get-tuple-element.17.mass, f32[16,256]{1,0:T(8,128)S(1)} %get-tuple-element.18.square, ...), custom_call_target="tpu_custom_call" | custom-call | tf_op jit(solution)/shard_map/columns/pallas_call | solution.py:357
  57.3 0.1 collective-permute-start.7
  57.4 1.2 %collective-permute-done.7 = f32[8,256]{1,0:T(8,128)S(1)} collective-permute-done((f32[8,256]{1,0:T(8,128)S(1)}, f32[8,256]{1,0:T(8,128)S(1)}, u32[]{:S(2)}, u32[]{:S(2)}) %collective-permute-start.7) | collective-permute-done | bytes 8224 | tf_op jit(solution)/shard_map/ppermute | solution.py:46
  58.6 0.7 collective-permute-start.8
  59.2 6.3 %collective-permute-start.9 = (f32[4,256]{1,0:T(4,128)S(1)}, f32[4,256]{1,0:T(4,128)S(1)}, u32[]{:S(2)}, u32[]{:S(2)}) collective-permute-start(f32[4,256]{1,0:T(4,128)S(1)} %get-tuple-element.25), channel_id=1, source_target_pairs={{32,0},{25,1},{18,2},{11,3},{36,4},{29,5},{22,6},{15,7},{40,8},{33... | collective-permute-start | bytes 12296 | tf_op jit(solution)/shard_map/ppermute | solution.py:46
  65.5 1.6 %collective-permute-done.9 = f32[4,256]{1,0:T(4,128)S(1)} collective-permute-done((f32[4,256]{1,0:T(4,128)S(1)}, f32[4,256]{1,0:T(4,128)S(1)}, u32[]{:S(2)}, u32[]{:S(2)}) %collective-permute-start.9) | collective-permute-done | bytes 4128 | tf_op jit(solution)/shard_map/ppermute | solution.py:46
  67.1 4.8 %collective-permute-start.12 = (f32[4,256]{1,0:T(4,128)S(1)}, f32[4,256]{1,0:T(4,128)S(1)}, u32[]{:S(2)}, u32[]{:S(2)}) collective-permute-start(f32[4,256]{1,0:T(4,128)S(1)} %multiply_add_fusion.1), channel_id=1, source_target_pairs={{3,0},{0,1},{1,2},{2,3},{7,4},{4,5},{5,6},{6,7},{11,8},{8,9},{9,10... | collective-permute-start | bytes 12296 | tf_op jit(solution)/shard_map/ppermute | solution.py:46
  71.9 0.2 collective-permute-start.11
  72.1 2.6 %collective-permute-start.10 = (f32[4,256]{1,0:T(4,128)S(1)}, f32[4,256]{1,0:T(4,128)S(1)}, u32[]{:S(2)}, u32[]{:S(2)}) collective-permute-start(f32[4,256]{1,0:T(4,128)S(1)} %multiply_add_fusion.1), channel_id=1, source_target_pairs={{1,0},{2,1},{3,2},{0,3},{5,4},{6,5},{7,6},{4,7},{9,8},{10,9},{11,1... | collective-permute-start | bytes 12296 | tf_op jit(solution)/shard_map/ppermute | solution.py:46
  74.7 0.6 multiply_subtract_fusion.1
  75.3 1.7 %collective-permute-done.11 = f32[4,256]{1,0:T(4,128)S(1)} collective-permute-done((f32[4,256]{1,0:T(4,128)S(1)}, f32[4,256]{1,0:T(4,128)S(1)}, u32[]{:S(2)}, u32[]{:S(2)}) %collective-permute-start.11) | collective-permute-done | bytes 4128 | tf_op jit(solution)/shard_map/ppermute | solution.py:46
  77.0 0.6 multiply_subtract_fusion
  (20 shorter events, 0.1 us)
Async XLA Ops:
  1.8 16.4 %collective-permute-start.5 = (f32[4,56,256]{2,1,0:T(8,128)S(1)}, f32[4,56,256]{2,1,0:T(8,128)S(1)}, u32[]{:S(2)}, u32[]{:S(2)}) collective-permute-start(f32[4,56,256]{2,1,0:T(8,128)S(1)} %get-tuple-element.14), channel_id=1, source_target_pairs={{32,0},{41,1},{50,2},{59,3},{36,4},{45,5},{54,6},{63,7},{40,8},{49... | collective-permute-start | bytes 688136 | tf_op jit(solution)/shard_map/ppermute | solution.py:46
  7.3 10.9 %collective-permute-start.3 = (f32[4,56,256]{2,1,0:T(8,128)S(1)}, f32[4,56,256]{2,1,0:T(8,128)S(1)}, u32[]{:S(2)}, u32[]{:S(2)}) collective-permute-start(f32[4,56,256]{2,1,0:T(8,128)S(1)} %get-tuple-element.14), channel_id=1, source_target_pairs={{0,0},{9,1},{18,2},{27,3},{4,4},{13,5},{22,6},{31,7},{8,8},{17,9},... | collective-permute-start | bytes 688136 | tf_op jit(solution)/shard_map/ppermute | solution.py:46
  7.9 31.7 %collective-permute-start.2 = (f32[4,56,256]{2,1,0:T(8,128)S(1)}, f32[4,56,256]{2,1,0:T(8,128)S(1)}, u32[]{:S(2)}, u32[]{:S(2)}) collective-permute-start(f32[4,56,256]{2,1,0:T(8,128)S(1)} %get-tuple-element.13.s0), channel_id=1, source_target_pairs={{192,0},{193,1},{194,2},{195,3},{196,4},{197,5},{198,6},{199,7},{2... | collective-permute-start | bytes 688136 | tf_op jit(solution)/shard_map/ppermute | solution.py:46
  9.6 30.1 %collective-permute-start.1 = (f32[4,56,256]{2,1,0:T(8,128)S(1)}, f32[4,56,256]{2,1,0:T(8,128)S(1)}, u32[]{:S(2)}, u32[]{:S(2)}) collective-permute-start(f32[4,56,256]{2,1,0:T(8,128)S(1)} %get-tuple-element.13.s0), channel_id=1, source_target_pairs={{128,0},{129,1},{130,2},{131,3},{132,4},{133,5},{134,6},{135,7},{1... | collective-permute-start | bytes 688136 | tf_op jit(solution)/shard_map/ppermute | solution.py:46
  12.5 27.2 %collective-permute-start = (f32[4,56,256]{2,1,0:T(8,128)S(1)}, f32[4,56,256]{2,1,0:T(8,128)S(1)}, u32[]{:S(2)}, u32[]{:S(2)}) collective-permute-start(f32[4,56,256]{2,1,0:T(8,128)S(1)} %get-tuple-element.13.s0), channel_id=1, source_target_pairs={{64,0},{65,1},{66,2},{67,3},{68,4},{69,5},{70,6},{71,7},{72,8},{73... | collective-permute-start | bytes 688136 | tf_op jit(solution)/shard_map/ppermute | solution.py:46
  18.2 21.5 %collective-permute-start.6 = (f32[4,56,256]{2,1,0:T(8,128)S(1)}, f32[4,56,256]{2,1,0:T(8,128)S(1)}, u32[]{:S(2)}, u32[]{:S(2)}) collective-permute-start(f32[4,56,256]{2,1,0:T(8,128)S(1)} %collective-permute-done.5.t2), channel_id=1, source_target_pairs={{4,0},{5,1},{6,2},{7,3},{0,4},{1,5},{2,6},{3,7},{12,8},{13,9},{14,... | collective-permute-start | bytes 688136 | tf_op jit(solution)/shard_map/ppermute | solution.py:46
  18.2 21.5 %collective-permute-start.4 = (f32[4,56,256]{2,1,0:T(8,128)S(1)}, f32[4,56,256]{2,1,0:T(8,128)S(1)}, u32[]{:S(2)}, u32[]{:S(2)}) collective-permute-start(f32[4,56,256]{2,1,0:T(8,128)S(1)} %collective-permute-done.3.t0), channel_id=1, source_target_pairs={{4,0},{5,1},{6,2},{7,3},{0,4},{1,5},{2,6},{3,7},{12,8},{13,9},{14,... | collective-permute-start | bytes 688136 | tf_op jit(solution)/shard_map/ppermute | solution.py:46
  54.7 20.0 %copy-start = (f32[4,256]{1,0:T(4,128)S(1)}, f32[4,256]{1,0:T(4,128)}, u32[]{:S(2)}) copy-start(f32[4,256]{1,0:T(4,128)} %more_extra_in.1) | copy-start | bytes 12292
  54.7 22.3 %copy-start.1 = (f32[4,256]{1,0:T(4,128)S(1)}, f32[4,256]{1,0:T(4,128)}, u32[]{:S(2)}) copy-start(f32[4,256]{1,0:T(4,128)} %extra_in.1) | copy-start | bytes 12292
  54.7 22.3 %copy-start.2 = (f32[4,256]{1,0:T(4,128)S(1)}, f32[4,256]{1,0:T(4,128)}, u32[]{:S(2)}) copy-start(f32[4,256]{1,0:T(4,128)} %param.10) | copy-start | bytes 12292
  57.3 1.3 %collective-permute-start.7 = (f32[8,256]{1,0:T(8,128)S(1)}, f32[8,256]{1,0:T(8,128)S(1)}, u32[]{:S(2)}, u32[]{:S(2)}) collective-permute-start(f32[8,256]{1,0:T(8,128)S(1)} %get-tuple-element.23), channel_id=1, source_target_pairs={{4,0},{5,1},{6,2},{7,3},{0,4},{1,5},{2,6},{3,7},{12,8},{13,9},{14,... | collective-permute-start | bytes 24584 | tf_op jit(solution)/shard_map/ppermute | solution.py:46
  58.6 6.9 %collective-permute-start.8 = (f32[4,256]{1,0:T(4,128)S(1)}, f32[4,256]{1,0:T(4,128)S(1)}, u32[]{:S(2)}, u32[]{:S(2)}) collective-permute-start(f32[4,256]{1,0:T(4,128)S(1)} %get-tuple-element.24), channel_id=1, source_target_pairs={{0,0},{57,1},{50,2},{43,3},{4,4},{61,5},{54,6},{47,7},{8,8},{1,9},... | collective-permute-start | bytes 12296 | tf_op jit(solution)/shard_map/ppermute | solution.py:46
  59.2 7.8 %collective-permute-start.9 = (f32[4,256]{1,0:T(4,128)S(1)}, f32[4,256]{1,0:T(4,128)S(1)}, u32[]{:S(2)}, u32[]{:S(2)}) collective-permute-start(f32[4,256]{1,0:T(4,128)S(1)} %get-tuple-element.25), channel_id=1, source_target_pairs={{32,0},{25,1},{18,2},{11,3},{36,4},{29,5},{22,6},{15,7},{40,8},{33... | collective-permute-start | bytes 12296 | tf_op jit(solution)/shard_map/ppermute | solution.py:46
  67.1 8.2 %collective-permute-start.12 = (f32[4,256]{1,0:T(4,128)S(1)}, f32[4,256]{1,0:T(4,128)S(1)}, u32[]{:S(2)}, u32[]{:S(2)}) collective-permute-start(f32[4,256]{1,0:T(4,128)S(1)} %multiply_add_fusion.1), channel_id=1, source_target_pairs={{3,0},{0,1},{1,2},{2,3},{7,4},{4,5},{5,6},{6,7},{11,8},{8,9},{9,10... | collective-permute-start | bytes 12296 | tf_op jit(solution)/shard_map/ppermute | solution.py:46
  71.9 5.1 %collective-permute-start.11 = (f32[4,256]{1,0:T(4,128)S(1)}, f32[4,256]{1,0:T(4,128)S(1)}, u32[]{:S(2)}, u32[]{:S(2)}) collective-permute-start(f32[4,256]{1,0:T(4,128)S(1)} %multiply_add_fusion.1), channel_id=1, source_target_pairs={{2,0},{3,1},{0,2},{1,3},{6,4},{7,5},{4,6},{5,7},{10,8},{11,9},{8,1... | collective-permute-start | bytes 12296 | tf_op jit(solution)/shard_map/ppermute | solution.py:46
  72.1 4.9 %collective-permute-start.10 = (f32[4,256]{1,0:T(4,128)S(1)}, f32[4,256]{1,0:T(4,128)S(1)}, u32[]{:S(2)}, u32[]{:S(2)}) collective-permute-start(f32[4,256]{1,0:T(4,128)S(1)} %multiply_add_fusion.1), channel_id=1, source_target_pairs={{1,0},{2,1},{3,2},{0,3},{5,4},{6,5},{7,6},{4,7},{9,8},{10,9},{11,1... | collective-permute-start | bytes 12296 | tf_op jit(solution)/shard_map/ppermute | solution.py:46

commit v10 on v9

--- a/solution.py
+++ b/solution.py
@@ -180,7 +180,7 @@
     return logsum(top[:, 0, :], total)
 
 
-def pack_kernel(cells_in, extra_in, more_cells_in, more_extra_in, out, more_out, cells, more_cells, extra, more_extra, sem):
+def pack_kernel(cells_in, extra_in, more_cells_in, more_extra_in, source_in, target_in, out, more_out, codes_out, cells, more_cells, extra, more_extra, source, target, sem):
     copies = [
         pltpu.make_async_copy(a, b, sem.at[k])
         for k, (a, b) in enumerate(
@@ -189,6 +189,8 @@
                 (extra_in, extra),
                 (more_cells_in, more_cells),
                 (more_extra_in, more_extra),
+                (source_in, source),
+                (target_in, target),
             )
         )
     ]
@@ -201,6 +203,9 @@
             o[n, 0:COMP, :] = a[:, n, :]
             o[n, COMP : COMP + 1, :] = b[n : n + 1, :]
             o[n, COMP + 1 : PACKED, :] = jnp.zeros((PACKED - COMP - 1, CELLS), f32)
+    copies[4].wait()
+    copies[5].wait()
+    codes_out[...] = jnp.where(target[...] >= 0, source[...] * CL + target[...], -1)
 
 
 def row_kernel(codes_in, s0, s1, s2, s3, t0, t1, t2, t3, out, list_out, xn, yn, mass, square_out, codes, list_ref, yt, top, tot, *rest):
@@ -292,18 +297,16 @@
 
 
 def work(source_coords, target_coords, source_logmass, target_logmass, target_prior, pair_source, pair_target):
-    codes = pair_source * 4 + pair_target
-    codes = jnp.where(pair_target >= 0, codes, -1).reshape(1, -1)
-    codes = exchanged(jnp.broadcast_to(codes, (MEMBERS, codes.shape[1])), PLANES)
-
     cells = jax.ShapeDtypeStruct((CL, PACKED, CELLS), f32)
     loose = pltpu.VMEM((COMP, CL, CELLS), f32)
-    t, s0 = pl.pallas_call(
+    t, s0, codes = pl.pallas_call(
         pack_kernel,
-        out_shape=(cells, cells),
-        in_specs=[HBM] * 4,
-        out_specs=(VMEM, VMEM),
-        scratch_shapes=[loose, loose] + [pltpu.VMEM((CL, CELLS), f32)] * 2 + [pltpu.SemaphoreType.DMA((4,))],
+        out_shape=(cells, cells, jax.ShapeDtypeStruct((1, SLOTS), jnp.int32)),
+        in_specs=[HBM] * 6,
+        out_specs=(VMEM, VMEM, VMEM),
+        scratch_shapes=[loose, loose] + [pltpu.VMEM((CL, CELLS), f32)] * 2
+        + [pltpu.VMEM((1, SLOTS), jnp.int32)] * 2
+        + [pltpu.SemaphoreType.DMA((6,))],
         compiler_params=pltpu.CompilerParams(vmem_limit_bytes=4 * 2**20),
         name="pack",
     )(
@@ -314,12 +317,15 @@
                 target_prior,
                 jnp.transpose(source_coords, (1, 0, 2)),
                 source_logmass,
+                pair_source.reshape(1, SLOTS),
+                pair_target.reshape(1, SLOTS),
             )
         )
     )
     t2 = fetched(t, lambda x, y, z, c: (x, y, z + x + FAR, c))
     t0 = fetched(t, lambda x, y, z, c: (x, y, z + x, c))
     s1, s2, s3 = (from_y(s0, k) for k in (1, 2, 3))
+    codes = exchanged(jnp.broadcast_to(codes, (MEMBERS, SLOTS)), PLANES)
     t1, t3 = from_core(t0), from_core(t2)
     shards = (s0, s1, s2, s3, t0, t1, t2, t3)
 

time: 77.9 us -> 77.2 us (level)
  transfers between devices with their start and end apart: 13 -> 13, of which waited for: 4 -> 4; matrix products, arithmetic and copies ran while one was open for 2% -> 1% of each run, Pallas kernels for 0% -> 0%
where the time goes in v10:
time: 77.2 us; the launch traced here: 77 us
  blocking collectives  31.9 us (41%)
  starting transfers between devices  27.1 us (35%)
  waiting for transfers between devices  8.85 us (11%)
  Pallas kernels  7.1 us (9%)
  other arithmetic  1.26 us (2%)
    all_to_all x2, blocking collectives, exchanged(): lax.all_to_all(value, AXES, 0, 0, axis_index_groups=groups, tiled=True)  31.9 us
    ppermute x13, starting transfers between devices, fetched(): return lax.ppermute(value, AXES, pairs)  27.1 us
    ppermute x13, waiting for transfers between devices, fetched(): return lax.ppermute(value, AXES, pairs)  8.85 us
    pallas_call x1, Pallas kernels, work(): pl.pallas_call(row_kernel, out_shape=(jax.ShapeDtypeStruct((MEMBERS, 4, C...  3.32 us
    pallas_call x1, Pallas kernels, work(): pl.pallas_call(column_kernel, out_shape=(jax.ShapeDtypeStruct((2 * CL, CE...  2.6 us
  transfers between devices with their start and end apart: 13, of which 4 were waited for; matrix products, arithmetic and copies ran while one was open for 1% of the time, Pallas kernels for 0%

profile of v10, /device:TPU:64, one launch (start us, length us, event | category | flops | bytes accessed | tf_op | source)
XLA Modules:
  0.0 77.0 jit_solution(13660540792660196188)
XLA Ops:
  0.6 1.2 %pack.1 = (f32[4,56,256]{2,1,0:T(8,128)S(1)}, f32[4,56,256]{2,1,0:T(8,128)S(1)}, s32[1,64]{1,0:T(1,128)S(1)}) custom-call(f32[50,4,256]{2,1,0:T(4,128)} %bitcast.8, f32[4,256]{1,0:T(4,128)} %extra_in.1, f32[50,4,256]{2,1,0:T(4,128)} %bitcast.9, f32[4,256]{1,0:T(4,128)} %more_extra_in.1, s32[1,64]{1,0:T(1,128)} %bitcast.10, s32[1,64]{1,0:T(1,128)} %bitcast.11), custom_call_target="tpu_custom_call" | custom-call | tf_op jit(solution)/shard_map/pack/pallas_call | solution.py:302
  1.8 5.5 %collective-permute-start.5 = (f32[4,56,256]{2,1,0:T(8,128)S(1)}, f32[4,56,256]{2,1,0:T(8,128)S(1)}, u32[]{:S(2)}, u32[]{:S(2)}) collective-permute-start(f32[4,56,256]{2,1,0:T(8,128)S(1)} %get-tuple-element.16), channel_id=1, source_target_pairs={{32,0},{41,1},{50,2},{59,3},{36,4},{45,5},{54,6},{63,7},{40,8},{49... | collective-permute-start | bytes 688136 | tf_op jit(solution)/shard_map/ppermute | solution.py:46
  7.3 0.7 collective-permute-start.3
  8.0 1.7 %collective-permute-start.2 = (f32[4,56,256]{2,1,0:T(8,128)S(1)}, f32[4,56,256]{2,1,0:T(8,128)S(1)}, u32[]{:S(2)}, u32[]{:S(2)}) collective-permute-start(f32[4,56,256]{2,1,0:T(8,128)S(1)} %get-tuple-element.15.s0), channel_id=1, source_target_pairs={{192,0},{193,1},{194,2},{195,3},{196,4},{197,5},{198,6},{199,7},{2... | collective-permute-start | bytes 688136 | tf_op jit(solution)/shard_map/ppermute | solution.py:46
  9.6 2.9 %collective-permute-start.1 = (f32[4,56,256]{2,1,0:T(8,128)S(1)}, f32[4,56,256]{2,1,0:T(8,128)S(1)}, u32[]{:S(2)}, u32[]{:S(2)}) collective-permute-start(f32[4,56,256]{2,1,0:T(8,128)S(1)} %get-tuple-element.15.s0), channel_id=1, source_target_pairs={{128,0},{129,1},{130,2},{131,3},{132,4},{133,5},{134,6},{135,7},{1... | collective-permute-start | bytes 688136 | tf_op jit(solution)/shard_map/ppermute | solution.py:46
  12.5 1.3 %collective-permute-start = (f32[4,56,256]{2,1,0:T(8,128)S(1)}, f32[4,56,256]{2,1,0:T(8,128)S(1)}, u32[]{:S(2)}, u32[]{:S(2)}) collective-permute-start(f32[4,56,256]{2,1,0:T(8,128)S(1)} %get-tuple-element.15.s0), channel_id=1, source_target_pairs={{64,0},{65,1},{66,2},{67,3},{68,4},{69,5},{70,6},{71,7},{72,8},{73... | collective-permute-start | bytes 688136 | tf_op jit(solution)/shard_map/ppermute | solution.py:46
  13.9 4.3 %collective-permute-done.5.t2 = f32[4,56,256]{2,1,0:T(8,128)S(1)} collective-permute-done((f32[4,56,256]{2,1,0:T(8,128)S(1)}, f32[4,56,256]{2,1,0:T(8,128)S(1)}, u32[]{:S(2)}, u32[]{:S(2)}) %collective-permute-start.5) | collective-permute-done | bytes 229408 | tf_op jit(solution)/shard_map/ppermute | solution.py:46
  18.2 0.0 collective-permute-start.6
  18.2 0.5 collective-permute-start.4
  18.7 20.3 %all_to_all.13 = s32[16,1,64]{2,1,0:T(1,128)S(1)} all-to-all(s32[16,1,64]{2,1,0:T(1,128)S(1)} %broadcast_in_dim.2), channel_id=1, replica_groups={{0,64,128,192,1,65,129,193,2,66,130,194,3,67,131,195},{4,68,132,196,5,6..., dimensions={0} | all-to-all | bytes 8192 | tf_op jit(solution)/shard_map/all_to_all | solution.py:62
  39.0 3.3 %rows.1 = (f32[16,4,4,256]{3,2,1,0:T(4,128)S(1)}, s32[80]{0:T(128)S(1)}, bf16[17,128,256]{2,1,0:T(8,128)(2,1)S(1)}, bf16[16,128,256]{2,1,0:T(8,128)(2,1)S(1)}, f...) custom-call(s32[16,64]{1,0:T(8,128)S(1)} %bitcast.6, f32[4,56,256]{2,1,0:T(8,128)S(1)} %get-tuple-element.15.s0, ...), custom_call_target="tpu_custom_call" | custom-call | tf_op jit(solution)/shard_map/rows/pallas_call | solution.py:339
  42.4 11.6 %all_to_all.14.came = f32[16,4,4,256]{3,2,1,0:T(4,128)S(1)} all-to-all(f32[16,4,4,256]{3,2,1,0:T(4,128)S(1)} %get-tuple-element.18), channel_id=1, replica_groups={{0,64,128,192,1,65,129,193,2,66,130,194,3,67,131,195},{4,68,132,196,5,6..., dimensions={0} | all-to-all | bytes 524288 | tf_op jit(solution)/shard_map/all_to_all | solution.py:62
  54.0 2.6 %columns.1 = (f32[8,256]{1,0:T(8,128)S(1)}, f32[8,256]{1,0:T(8,128)S(1)}, f32[4,256]{1,0:T(4,128)S(1)}) custom-call(s32[80]{0:T(128)S(1)} %get-tuple-element.17.list_in, f32[16,4,4,256]{3,2,1,0:T(4,128)S(1)} %all_to_all.14.came, f32[16,256]{1,0:T(8,128)S(1)} %get-tuple-element.19.mass, f32[16,256]{1,0:T(8,128)S(1)} %get-tuple-element.20.square, ...), custom_call_target="tpu_custom_call" | custom-call | tf_op jit(solution)/shard_map/columns/pallas_call | solution.py:363
  56.6 0.1 collective-permute-start.7
  56.7 1.2 %collective-permute-done.7 = f32[8,256]{1,0:T(8,128)S(1)} collective-permute-done((f32[8,256]{1,0:T(8,128)S(1)}, f32[8,256]{1,0:T(8,128)S(1)}, u32[]{:S(2)}, u32[]{:S(2)}) %collective-permute-start.7) | collective-permute-done | bytes 8224 | tf_op jit(solution)/shard_map/ppermute | solution.py:46
  57.9 0.7 collective-permute-start.8
  58.6 6.2 %collective-permute-start.9 = (f32[4,256]{1,0:T(4,128)S(1)}, f32[4,256]{1,0:T(4,128)S(1)}, u32[]{:S(2)}, u32[]{:S(2)}) collective-permute-start(f32[4,256]{1,0:T(4,128)S(1)} %get-tuple-element.27), channel_id=1, source_target_pairs={{32,0},{25,1},{18,2},{11,3},{36,4},{29,5},{22,6},{15,7},{40,8},{33... | collective-permute-start | bytes 12296 | tf_op jit(solution)/shard_map/ppermute | solution.py:46
  64.8 1.6 %collective-permute-done.9 = f32[4,256]{1,0:T(4,128)S(1)} collective-permute-done((f32[4,256]{1,0:T(4,128)S(1)}, f32[4,256]{1,0:T(4,128)S(1)}, u32[]{:S(2)}, u32[]{:S(2)}) %collective-permute-start.9) | collective-permute-done | bytes 4128 | tf_op jit(solution)/shard_map/ppermute | solution.py:46
  66.4 4.8 %collective-permute-start.12 = (f32[4,256]{1,0:T(4,128)S(1)}, f32[4,256]{1,0:T(4,128)S(1)}, u32[]{:S(2)}, u32[]{:S(2)}) collective-permute-start(f32[4,256]{1,0:T(4,128)S(1)} %multiply_add_fusion.1), channel_id=1, source_target_pairs={{3,0},{0,1},{1,2},{2,3},{7,4},{4,5},{5,6},{6,7},{11,8},{8,9},{9,10... | collective-permute-start | bytes 12296 | tf_op jit(solution)/shard_map/ppermute | solution.py:46
  71.2 0.2 collective-permute-start.11
  71.4 2.6 %collective-permute-start.10 = (f32[4,256]{1,0:T(4,128)S(1)}, f32[4,256]{1,0:T(4,128)S(1)}, u32[]{:S(2)}, u32[]{:S(2)}) collective-permute-start(f32[4,256]{1,0:T(4,128)S(1)} %multiply_add_fusion.1), channel_id=1, source_target_pairs={{1,0},{2,1},{3,2},{0,3},{5,4},{6,5},{7,6},{4,7},{9,8},{10,9},{11,1... | collective-permute-start | bytes 12296 | tf_op jit(solution)/shard_map/ppermute | solution.py:46
  74.0 0.6 multiply_subtract_fusion.1
  74.6 1.7 %collective-permute-done.11 = f32[4,256]{1,0:T(4,128)S(1)} collective-permute-done((f32[4,256]{1,0:T(4,128)S(1)}, f32[4,256]{1,0:T(4,128)S(1)}, u32[]{:S(2)}, u32[]{:S(2)}) %collective-permute-start.11) | collective-permute-done | bytes 4128 | tf_op jit(solution)/shard_map/ppermute | solution.py:46
  76.3 0.6 multiply_subtract_fusion
  (19 shorter events, 0.1 us)
Async XLA Ops:
  1.8 16.4 %collective-permute-start.5 = (f32[4,56,256]{2,1,0:T(8,128)S(1)}, f32[4,56,256]{2,1,0:T(8,128)S(1)}, u32[]{:S(2)}, u32[]{:S(2)}) collective-permute-start(f32[4,56,256]{2,1,0:T(8,128)S(1)} %get-tuple-element.16), channel_id=1, source_target_pairs={{32,0},{41,1},{50,2},{59,3},{36,4},{45,5},{54,6},{63,7},{40,8},{49... | collective-permute-start | bytes 688136 | tf_op jit(solution)/shard_map/ppermute | solution.py:46
  7.3 10.9 %collective-permute-start.3 = (f32[4,56,256]{2,1,0:T(8,128)S(1)}, f32[4,56,256]{2,1,0:T(8,128)S(1)}, u32[]{:S(2)}, u32[]{:S(2)}) collective-permute-start(f32[4,56,256]{2,1,0:T(8,128)S(1)} %get-tuple-element.16), channel_id=1, source_target_pairs={{0,0},{9,1},{18,2},{27,3},{4,4},{13,5},{22,6},{31,7},{8,8},{17,9},... | collective-permute-start | bytes 688136 | tf_op jit(solution)/shard_map/ppermute | solution.py:46
  8.0 31.1 %collective-permute-start.2 = (f32[4,56,256]{2,1,0:T(8,128)S(1)}, f32[4,56,256]{2,1,0:T(8,128)S(1)}, u32[]{:S(2)}, u32[]{:S(2)}) collective-permute-start(f32[4,56,256]{2,1,0:T(8,128)S(1)} %get-tuple-element.15.s0), channel_id=1, source_target_pairs={{192,0},{193,1},{194,2},{195,3},{196,4},{197,5},{198,6},{199,7},{2... | collective-permute-start | bytes 688136 | tf_op jit(solution)/shard_map/ppermute | solution.py:46
  9.6 29.4 %collective-permute-start.1 = (f32[4,56,256]{2,1,0:T(8,128)S(1)}, f32[4,56,256]{2,1,0:T(8,128)S(1)}, u32[]{:S(2)}, u32[]{:S(2)}) collective-permute-start(f32[4,56,256]{2,1,0:T(8,128)S(1)} %get-tuple-element.15.s0), channel_id=1, source_target_pairs={{128,0},{129,1},{130,2},{131,3},{132,4},{133,5},{134,6},{135,7},{1... | collective-permute-start | bytes 688136 | tf_op jit(solution)/shard_map/ppermute | solution.py:46
  12.5 26.5 %collective-permute-start = (f32[4,56,256]{2,1,0:T(8,128)S(1)}, f32[4,56,256]{2,1,0:T(8,128)S(1)}, u32[]{:S(2)}, u32[]{:S(2)}) collective-permute-start(f32[4,56,256]{2,1,0:T(8,128)S(1)} %get-tuple-element.15.s0), channel_id=1, source_target_pairs={{64,0},{65,1},{66,2},{67,3},{68,4},{69,5},{70,6},{71,7},{72,8},{73... | collective-permute-start | bytes 688136 | tf_op jit(solution)/shard_map/ppermute | solution.py:46
  18.2 20.8 %collective-permute-start.6 = (f32[4,56,256]{2,1,0:T(8,128)S(1)}, f32[4,56,256]{2,1,0:T(8,128)S(1)}, u32[]{:S(2)}, u32[]{:S(2)}) collective-permute-start(f32[4,56,256]{2,1,0:T(8,128)S(1)} %collective-permute-done.5.t2), channel_id=1, source_target_pairs={{4,0},{5,1},{6,2},{7,3},{0,4},{1,5},{2,6},{3,7},{12,8},{13,9},{14,... | collective-permute-start | bytes 688136 | tf_op jit(solution)/shard_map/ppermute | solution.py:46
  18.2 20.8 %collective-permute-start.4 = (f32[4,56,256]{2,1,0:T(8,128)S(1)}, f32[4,56,256]{2,1,0:T(8,128)S(1)}, u32[]{:S(2)}, u32[]{:S(2)}) collective-permute-start(f32[4,56,256]{2,1,0:T(8,128)S(1)} %collective-permute-done.3.t0), channel_id=1, source_target_pairs={{4,0},{5,1},{6,2},{7,3},{0,4},{1,5},{2,6},{3,7},{12,8},{13,9},{14,... | collective-permute-start | bytes 688136 | tf_op jit(solution)/shard_map/ppermute | solution.py:46
  54.0 20.0 %copy-start = (f32[4,256]{1,0:T(4,128)S(1)}, f32[4,256]{1,0:T(4,128)}, u32[]{:S(2)}) copy-start(f32[4,256]{1,0:T(4,128)} %more_extra_in.1) | copy-start | bytes 12292
  54.0 22.3 %copy-start.1 = (f32[4,256]{1,0:T(4,128)S(1)}, f32[4,256]{1,0:T(4,128)}, u32[]{:S(2)}) copy-start(f32[4,256]{1,0:T(4,128)} %extra_in.1) | copy-start | bytes 12292
  54.0 22.3 %copy-start.2 = (f32[4,256]{1,0:T(4,128)S(1)}, f32[4,256]{1,0:T(4,128)}, u32[]{:S(2)}) copy-start(f32[4,256]{1,0:T(4,128)} %param.10) | copy-start | bytes 12292
  56.6 1.3 %collective-permute-start.7 = (f32[8,256]{1,0:T(8,128)S(1)}, f32[8,256]{1,0:T(8,128)S(1)}, u32[]{:S(2)}, u32[]{:S(2)}) collective-permute-start(f32[8,256]{1,0:T(8,128)S(1)} %get-tuple-element.25), channel_id=1, source_target_pairs={{4,0},{5,1},{6,2},{7,3},{0,4},{1,5},{2,6},{3,7},{12,8},{13,9},{14,... | collective-permute-start | bytes 24584 | tf_op jit(solution)/shard_map/ppermute | solution.py:46
  57.9 6.9 %collective-permute-start.8 = (f32[4,256]{1,0:T(4,128)S(1)}, f32[4,256]{1,0:T(4,128)S(1)}, u32[]{:S(2)}, u32[]{:S(2)}) collective-permute-start(f32[4,256]{1,0:T(4,128)S(1)} %get-tuple-element.26), channel_id=1, source_target_pairs={{0,0},{57,1},{50,2},{43,3},{4,4},{61,5},{54,6},{47,7},{8,8},{1,9},... | collective-permute-start | bytes 12296 | tf_op jit(solution)/shard_map/ppermute | solution.py:46
  58.6 7.8 %collective-permute-start.9 = (f32[4,256]{1,0:T(4,128)S(1)}, f32[4,256]{1,0:T(4,128)S(1)}, u32[]{:S(2)}, u32[]{:S(2)}) collective-permute-start(f32[4,256]{1,0:T(4,128)S(1)} %get-tuple-element.27), channel_id=1, source_target_pairs={{32,0},{25,1},{18,2},{11,3},{36,4},{29,5},{22,6},{15,7},{40,8},{33... | collective-permute-start | bytes 12296 | tf_op jit(solution)/shard_map/ppermute | solution.py:46
  66.4 8.2 %collective-permute-start.12 = (f32[4,256]{1,0:T(4,128)S(1)}, f32[4,256]{1,0:T(4,128)S(1)}, u32[]{:S(2)}, u32[]{:S(2)}) collective-permute-start(f32[4,256]{1,0:T(4,128)S(1)} %multiply_add_fusion.1), channel_id=1, source_target_pairs={{3,0},{0,1},{1,2},{2,3},{7,4},{4,5},{5,6},{6,7},{11,8},{8,9},{9,10... | collective-permute-start | bytes 12296 | tf_op jit(solution)/shard_map/ppermute | solution.py:46
  71.2 5.1 %collective-permute-start.11 = (f32[4,256]{1,0:T(4,128)S(1)}, f32[4,256]{1,0:T(4,128)S(1)}, u32[]{:S(2)}, u32[]{:S(2)}) collective-permute-start(f32[4,256]{1,0:T(4,128)S(1)} %multiply_add_fusion.1), channel_id=1, source_target_pairs={{2,0},{3,1},{0,2},{1,3},{6,4},{7,5},{4,6},{5,7},{10,8},{11,9},{8,1... | collective-permute-start | bytes 12296 | tf_op jit(solution)/shard_map/ppermute | solution.py:46
  71.4 4.9 %collective-permute-start.10 = (f32[4,256]{1,0:T(4,128)S(1)}, f32[4,256]{1,0:T(4,128)S(1)}, u32[]{:S(2)}, u32[]{:S(2)}) collective-permute-start(f32[4,256]{1,0:T(4,128)S(1)} %multiply_add_fusion.1), channel_id=1, source_target_pairs={{1,0},{2,1},{3,2},{0,3},{5,4},{6,5},{7,6},{4,7},{9,8},{10,9},{11,1... | collective-permute-start | bytes 12296 | tf_op jit(solution)/shard_map/ppermute | solution.py:46

commit v11 on v10

--- a/solution.py
+++ b/solution.py
@@ -20,7 +20,8 @@
 NY, NZ, NC, NX = 4, 8, 2, 4
 AXES = ("own", "split")
 
-FAR = NZ // 2
+NEAR = (0, 1, 2, 7)
+FAR = (4, 5, 6, 3)
 
 BLOCK = 64
 DEPTH = 2 * BLOCK
@@ -81,8 +82,9 @@
 def target_owners():
     x, y, z, c = place()
     row = y * (NZ * NC)
-    near = row + ((z + x) % NZ) * NC
-    far = row + ((z + x + NZ // 2) % NZ) * NC
+    last = (x == NX - 1).astype(jnp.int32) * (NZ // 2)
+    near = row + ((z + x + last) % NZ) * NC
+    far = row + ((z + x + NZ // 2 - last) % NZ) * NC
     return near + c, near + 1 - c, far + c, far + 1 - c
 
 
@@ -322,8 +324,8 @@
             )
         )
     )
-    t2 = fetched(t, lambda x, y, z, c: (x, y, z + x + FAR, c))
-    t0 = fetched(t, lambda x, y, z, c: (x, y, z + x, c))
+    t2 = fetched(t, lambda x, y, z, c: (x, y, z + FAR[x], c))
+    t0 = fetched(t, lambda x, y, z, c: (x, y, z + NEAR[x], c))
     s1, s2, s3 = (from_y(s0, k) for k in (1, 2, 3))
     codes = exchanged(jnp.broadcast_to(codes, (MEMBERS, SLOTS)), PLANES)
     t1, t3 = from_core(t0), from_core(t2)
@@ -381,8 +383,8 @@
     )(pairs, rows, mass, square, xn, yn)
 
     kept = merged([kept, from_core(given)])
-    first = fetched(kept[:CL], lambda x, y, z, c: (x, y, z - x, c))
-    second = fetched(kept[CL:], lambda x, y, z, c: (x, y, z - x - FAR, c))
+    first = fetched(kept[:CL], lambda x, y, z, c: (x, y, z - NEAR[x], c))
+    second = fetched(kept[CL:], lambda x, y, z, c: (x, y, z - FAR[x], c))
     part = merged([first, second])
     part = merged([part] + [from_x(part, k) for k in (1, 2, 3)])
     target_potential = EPSILON * target_logmass + target_prior - (EPSILON * LN2) * part

time: 77.2 us -> 74.8 us (0.969); the launches traced: 77 us -> 73.3 us
  blocking collectives: 31.9 us -> 29.8 us
  starting transfers between devices: 27.1 us -> 26 us
    all_to_all x2, blocking collectives: 31.9 us -> 29.8 us  [exchanged(): lax.all_to_all(value, AXES, 0, 0, axis_index_groups=groups, tiled=True)]
    ppermute x13, starting transfers between devices: 27.1 us -> 26 us  [fetched(): return lax.ppermute(value, AXES, pairs)]
where the time goes in v11:
time: 74.8 us; the launch traced here: 73.3 us
  blocking collectives  29.8 us (40%)
  starting transfers between devices  26 us (35%)
  waiting for transfers between devices  8.43 us (11%)
  Pallas kernels  7.07 us (9%)
  other arithmetic  1.26 us (2%)
    all_to_all x2, blocking collectives, exchanged(): lax.all_to_all(value, AXES, 0, 0, axis_index_groups=groups, tiled=True)  29.8 us
    ppermute x13, starting transfers between devices, fetched(): return lax.ppermute(value, AXES, pairs)  26 us
    ppermute x13, waiting for transfers between devices, fetched(): return lax.ppermute(value, AXES, pairs)  8.43 us
    pallas_call x1, Pallas kernels, work(): pl.pallas_call(row_kernel, out_shape=(jax.ShapeDtypeStruct((MEMBERS, 4, C...  3.32 us
    pallas_call x1, Pallas kernels, work(): pl.pallas_call(column_kernel, out_shape=(jax.ShapeDtypeStruct((2 * CL, CE...  2.58 us
  transfers between devices with their start and end apart: 13, of which 4 were waited for; matrix products, arithmetic and copies ran while one was open for 1% of the time, Pallas kernels for 0%

profile of v11, /device:TPU:64, one launch (start us, length us, event | category | flops | bytes accessed | tf_op | source)
XLA Modules:
  0.0 73.3 jit_solution(16757559017560384793)
XLA Ops:
  0.6 1.2 %pack.1 = (f32[4,56,256]{2,1,0:T(8,128)S(1)}, f32[4,56,256]{2,1,0:T(8,128)S(1)}, s32[1,64]{1,0:T(1,128)S(1)}) custom-call(f32[50,4,256]{2,1,0:T(4,128)} %bitcast.8, f32[4,256]{1,0:T(4,128)} %extra_in.1, f32[50,4,256]{2,1,0:T(4,128)} %bitcast.9, f32[4,256]{1,0:T(4,128)} %more_extra_in.1, s32[1,64]{1,0:T(1,128)} %bitcast.10, s32[1,64]{1,0:T(1,128)} %bitcast.11), custom_call_target="tpu_custom_call" | custom-call | tf_op jit(solution)/shard_map/pack/pallas_call | solution.py:304
  1.8 5.5 %collective-permute-start.5 = (f32[4,56,256]{2,1,0:T(8,128)S(1)}, f32[4,56,256]{2,1,0:T(8,128)S(1)}, u32[]{:S(2)}, u32[]{:S(2)}) collective-permute-start(f32[4,56,256]{2,1,0:T(8,128)S(1)} %get-tuple-element.16), channel_id=1, source_target_pairs={{32,0},{41,1},{50,2},{27,3},{36,4},{45,5},{54,6},{31,7},{40,8},{49... | collective-permute-start | bytes 688136 | tf_op jit(solution)/shard_map/ppermute | solution.py:47
  7.3 0.7 collective-permute-start.3
  8.0 1.7 %collective-permute-start.2 = (f32[4,56,256]{2,1,0:T(8,128)S(1)}, f32[4,56,256]{2,1,0:T(8,128)S(1)}, u32[]{:S(2)}, u32[]{:S(2)}) collective-permute-start(f32[4,56,256]{2,1,0:T(8,128)S(1)} %get-tuple-element.15.s0), channel_id=1, source_target_pairs={{192,0},{193,1},{194,2},{195,3},{196,4},{197,5},{198,6},{199,7},{2... | collective-permute-start | bytes 688136 | tf_op jit(solution)/shard_map/ppermute | solution.py:47
  9.6 2.9 %collective-permute-start.1 = (f32[4,56,256]{2,1,0:T(8,128)S(1)}, f32[4,56,256]{2,1,0:T(8,128)S(1)}, u32[]{:S(2)}, u32[]{:S(2)}) collective-permute-start(f32[4,56,256]{2,1,0:T(8,128)S(1)} %get-tuple-element.15.s0), channel_id=1, source_target_pairs={{128,0},{129,1},{130,2},{131,3},{132,4},{133,5},{134,6},{135,7},{1... | collective-permute-start | bytes 688136 | tf_op jit(solution)/shard_map/ppermute | solution.py:47
  12.5 1.3 %collective-permute-start = (f32[4,56,256]{2,1,0:T(8,128)S(1)}, f32[4,56,256]{2,1,0:T(8,128)S(1)}, u32[]{:S(2)}, u32[]{:S(2)}) collective-permute-start(f32[4,56,256]{2,1,0:T(8,128)S(1)} %get-tuple-element.15.s0), channel_id=1, source_target_pairs={{64,0},{65,1},{66,2},{67,3},{68,4},{69,5},{70,6},{71,7},{72,8},{73... | collective-permute-start | bytes 688136 | tf_op jit(solution)/shard_map/ppermute | solution.py:47
  13.9 4.3 %collective-permute-done.5.t2 = f32[4,56,256]{2,1,0:T(8,128)S(1)} collective-permute-done((f32[4,56,256]{2,1,0:T(8,128)S(1)}, f32[4,56,256]{2,1,0:T(8,128)S(1)}, u32[]{:S(2)}, u32[]{:S(2)}) %collective-permute-start.5) | collective-permute-done | bytes 229408 | tf_op jit(solution)/shard_map/ppermute | solution.py:47
  18.2 0.0 collective-permute-start.6
  18.2 0.5 collective-permute-start.4
  18.7 18.3 %all_to_all.13 = s32[16,1,64]{2,1,0:T(1,128)S(1)} all-to-all(s32[16,1,64]{2,1,0:T(1,128)S(1)} %broadcast_in_dim.2), channel_id=1, replica_groups={{0,64,128,192,1,65,129,193,2,66,130,194,3,67,131,195},{4,68,132,196,5,6..., dimensions={0} | all-to-all | bytes 8192 | tf_op jit(solution)/shard_map/all_to_all | solution.py:63
  37.1 3.3 %rows.1 = (f32[16,4,4,256]{3,2,1,0:T(4,128)S(1)}, s32[80]{0:T(128)S(1)}, bf16[17,128,256]{2,1,0:T(8,128)(2,1)S(1)}, bf16[16,128,256]{2,1,0:T(8,128)(2,1)S(1)}, f...) custom-call(s32[16,64]{1,0:T(8,128)S(1)} %bitcast.6, f32[4,56,256]{2,1,0:T(8,128)S(1)} %get-tuple-element.15.s0, ...), custom_call_target="tpu_custom_call" | custom-call | tf_op jit(solution)/shard_map/rows/pallas_call | solution.py:341
  40.4 11.5 %all_to_all.14.came = f32[16,4,4,256]{3,2,1,0:T(4,128)S(1)} all-to-all(f32[16,4,4,256]{3,2,1,0:T(4,128)S(1)} %get-tuple-element.18), channel_id=1, replica_groups={{0,64,128,192,1,65,129,193,2,66,130,194,3,67,131,195},{4,68,132,196,5,6..., dimensions={0} | all-to-all | bytes 524288 | tf_op jit(solution)/shard_map/all_to_all | solution.py:63
  51.9 2.6 %columns.1 = (f32[8,256]{1,0:T(8,128)S(1)}, f32[8,256]{1,0:T(8,128)S(1)}, f32[4,256]{1,0:T(4,128)S(1)}) custom-call(s32[80]{0:T(128)S(1)} %get-tuple-element.17.list_in, f32[16,4,4,256]{3,2,1,0:T(4,128)S(1)} %all_to_all.14.came, f32[16,256]{1,0:T(8,128)S(1)} %get-tuple-element.19.mass, f32[16,256]{1,0:T(8,128)S(1)} %get-tuple-element.20.square, ...), custom_call_target="tpu_custom_call" | custom-call | tf_op jit(solution)/shard_map/columns/pallas_call | solution.py:365
  54.5 0.1 collective-permute-start.7
  54.6 1.2 %collective-permute-done.7 = f32[8,256]{1,0:T(8,128)S(1)} collective-permute-done((f32[8,256]{1,0:T(8,128)S(1)}, f32[8,256]{1,0:T(8,128)S(1)}, u32[]{:S(2)}, u32[]{:S(2)}) %collective-permute-start.7) | collective-permute-done | bytes 8224 | tf_op jit(solution)/shard_map/ppermute | solution.py:47
  55.8 0.7 collective-permute-start.8
  56.4 5.4 %collective-permute-start.9 = (f32[4,256]{1,0:T(4,128)S(1)}, f32[4,256]{1,0:T(4,128)S(1)}, u32[]{:S(2)}, u32[]{:S(2)}) collective-permute-start(f32[4,256]{1,0:T(4,128)S(1)} %get-tuple-element.27), channel_id=1, source_target_pairs={{32,0},{25,1},{18,2},{43,3},{36,4},{29,5},{22,6},{47,7},{40,8},{33... | collective-permute-start | bytes 12296 | tf_op jit(solution)/shard_map/ppermute | solution.py:47
  61.9 2.2 %collective-permute-done.9 = f32[4,256]{1,0:T(4,128)S(1)} collective-permute-done((f32[4,256]{1,0:T(4,128)S(1)}, f32[4,256]{1,0:T(4,128)S(1)}, u32[]{:S(2)}, u32[]{:S(2)}) %collective-permute-start.9) | collective-permute-done | bytes 4128 | tf_op jit(solution)/shard_map/ppermute | solution.py:47
  64.0 3.5 %collective-permute-start.12 = (f32[4,256]{1,0:T(4,128)S(1)}, f32[4,256]{1,0:T(4,128)S(1)}, u32[]{:S(2)}, u32[]{:S(2)}) collective-permute-start(f32[4,256]{1,0:T(4,128)S(1)} %multiply_add_fusion.1), channel_id=1, source_target_pairs={{3,0},{0,1},{1,2},{2,3},{7,4},{4,5},{5,6},{6,7},{11,8},{8,9},{9,10... | collective-permute-start | bytes 12296 | tf_op jit(solution)/shard_map/ppermute | solution.py:47
  67.5 1.2 %collective-permute-start.11 = (f32[4,256]{1,0:T(4,128)S(1)}, f32[4,256]{1,0:T(4,128)S(1)}, u32[]{:S(2)}, u32[]{:S(2)}) collective-permute-start(f32[4,256]{1,0:T(4,128)S(1)} %multiply_add_fusion.1), channel_id=1, source_target_pairs={{2,0},{3,1},{0,2},{1,3},{6,4},{7,5},{4,6},{5,7},{10,8},{11,9},{8,1... | collective-permute-start | bytes 12296 | tf_op jit(solution)/shard_map/ppermute | solution.py:47
  68.8 2.5 %collective-permute-start.10 = (f32[4,256]{1,0:T(4,128)S(1)}, f32[4,256]{1,0:T(4,128)S(1)}, u32[]{:S(2)}, u32[]{:S(2)}) collective-permute-start(f32[4,256]{1,0:T(4,128)S(1)} %multiply_add_fusion.1), channel_id=1, source_target_pairs={{1,0},{2,1},{3,2},{0,3},{5,4},{6,5},{7,6},{4,7},{9,8},{10,9},{11,1... | collective-permute-start | bytes 12296 | tf_op jit(solution)/shard_map/ppermute | solution.py:47
  71.3 0.6 multiply_subtract_fusion.1
  71.9 0.7 %collective-permute-done.11 = f32[4,256]{1,0:T(4,128)S(1)} collective-permute-done((f32[4,256]{1,0:T(4,128)S(1)}, f32[4,256]{1,0:T(4,128)S(1)}, u32[]{:S(2)}, u32[]{:S(2)}) %collective-permute-start.11) | collective-permute-done | bytes 4128 | tf_op jit(solution)/shard_map/ppermute | solution.py:47
  72.7 0.6 multiply_subtract_fusion
  (19 shorter events, 0.1 us)
Async XLA Ops:
  1.8 16.4 %collective-permute-start.5 = (f32[4,56,256]{2,1,0:T(8,128)S(1)}, f32[4,56,256]{2,1,0:T(8,128)S(1)}, u32[]{:S(2)}, u32[]{:S(2)}) collective-permute-start(f32[4,56,256]{2,1,0:T(8,128)S(1)} %get-tuple-element.16), channel_id=1, source_target_pairs={{32,0},{41,1},{50,2},{27,3},{36,4},{45,5},{54,6},{31,7},{40,8},{49... | collective-permute-start | bytes 688136 | tf_op jit(solution)/shard_map/ppermute | solution.py:47
  7.3 10.9 %collective-permute-start.3 = (f32[4,56,256]{2,1,0:T(8,128)S(1)}, f32[4,56,256]{2,1,0:T(8,128)S(1)}, u32[]{:S(2)}, u32[]{:S(2)}) collective-permute-start(f32[4,56,256]{2,1,0:T(8,128)S(1)} %get-tuple-element.16), channel_id=1, source_target_pairs={{0,0},{9,1},{18,2},{59,3},{4,4},{13,5},{22,6},{63,7},{8,8},{17,9},... | collective-permute-start | bytes 688136 | tf_op jit(solution)/shard_map/ppermute | solution.py:47
  8.0 29.1 %collective-permute-start.2 = (f32[4,56,256]{2,1,0:T(8,128)S(1)}, f32[4,56,256]{2,1,0:T(8,128)S(1)}, u32[]{:S(2)}, u32[]{:S(2)}) collective-permute-start(f32[4,56,256]{2,1,0:T(8,128)S(1)} %get-tuple-element.15.s0), channel_id=1, source_target_pairs={{192,0},{193,1},{194,2},{195,3},{196,4},{197,5},{198,6},{199,7},{2... | collective-permute-start | bytes 688136 | tf_op jit(solution)/shard_map/ppermute | solution.py:47
  9.6 27.4 %collective-permute-start.1 = (f32[4,56,256]{2,1,0:T(8,128)S(1)}, f32[4,56,256]{2,1,0:T(8,128)S(1)}, u32[]{:S(2)}, u32[]{:S(2)}) collective-permute-start(f32[4,56,256]{2,1,0:T(8,128)S(1)} %get-tuple-element.15.s0), channel_id=1, source_target_pairs={{128,0},{129,1},{130,2},{131,3},{132,4},{133,5},{134,6},{135,7},{1... | collective-permute-start | bytes 688136 | tf_op jit(solution)/shard_map/ppermute | solution.py:47
  12.5 24.5 %collective-permute-start = (f32[4,56,256]{2,1,0:T(8,128)S(1)}, f32[4,56,256]{2,1,0:T(8,128)S(1)}, u32[]{:S(2)}, u32[]{:S(2)}) collective-permute-start(f32[4,56,256]{2,1,0:T(8,128)S(1)} %get-tuple-element.15.s0), channel_id=1, source_target_pairs={{64,0},{65,1},{66,2},{67,3},{68,4},{69,5},{70,6},{71,7},{72,8},{73... | collective-permute-start | bytes 688136 | tf_op jit(solution)/shard_map/ppermute | solution.py:47
  18.2 18.8 %collective-permute-start.6 = (f32[4,56,256]{2,1,0:T(8,128)S(1)}, f32[4,56,256]{2,1,0:T(8,128)S(1)}, u32[]{:S(2)}, u32[]{:S(2)}) collective-permute-start(f32[4,56,256]{2,1,0:T(8,128)S(1)} %collective-permute-done.5.t2), channel_id=1, source_target_pairs={{4,0},{5,1},{6,2},{7,3},{0,4},{1,5},{2,6},{3,7},{12,8},{13,9},{14,... | collective-permute-start | bytes 688136 | tf_op jit(solution)/shard_map/ppermute | solution.py:47
  18.2 18.8 %collective-permute-start.4 = (f32[4,56,256]{2,1,0:T(8,128)S(1)}, f32[4,56,256]{2,1,0:T(8,128)S(1)}, u32[]{:S(2)}, u32[]{:S(2)}) collective-permute-start(f32[4,56,256]{2,1,0:T(8,128)S(1)} %collective-permute-done.3.t0), channel_id=1, source_target_pairs={{4,0},{5,1},{6,2},{7,3},{0,4},{1,5},{2,6},{3,7},{12,8},{13,9},{14,... | collective-permute-start | bytes 688136 | tf_op jit(solution)/shard_map/ppermute | solution.py:47
  51.9 19.4 %copy-start = (f32[4,256]{1,0:T(4,128)S(1)}, f32[4,256]{1,0:T(4,128)}, u32[]{:S(2)}) copy-start(f32[4,256]{1,0:T(4,128)} %more_extra_in.1) | copy-start | bytes 12292
  51.9 20.8 %copy-start.1 = (f32[4,256]{1,0:T(4,128)S(1)}, f32[4,256]{1,0:T(4,128)}, u32[]{:S(2)}) copy-start(f32[4,256]{1,0:T(4,128)} %extra_in.1) | copy-start | bytes 12292
  51.9 20.8 %copy-start.2 = (f32[4,256]{1,0:T(4,128)S(1)}, f32[4,256]{1,0:T(4,128)}, u32[]{:S(2)}) copy-start(f32[4,256]{1,0:T(4,128)} %param.10) | copy-start | bytes 12292
  54.5 1.3 %collective-permute-start.7 = (f32[8,256]{1,0:T(8,128)S(1)}, f32[8,256]{1,0:T(8,128)S(1)}, u32[]{:S(2)}, u32[]{:S(2)}) collective-permute-start(f32[8,256]{1,0:T(8,128)S(1)} %get-tuple-element.25), channel_id=1, source_target_pairs={{4,0},{5,1},{6,2},{7,3},{0,4},{1,5},{2,6},{3,7},{12,8},{13,9},{14,... | collective-permute-start | bytes 24584 | tf_op jit(solution)/shard_map/ppermute | solution.py:47
  55.8 6.1 %collective-permute-start.8 = (f32[4,256]{1,0:T(4,128)S(1)}, f32[4,256]{1,0:T(4,128)S(1)}, u32[]{:S(2)}, u32[]{:S(2)}) collective-permute-start(f32[4,256]{1,0:T(4,128)S(1)} %get-tuple-element.26), channel_id=1, source_target_pairs={{0,0},{57,1},{50,2},{11,3},{4,4},{61,5},{54,6},{15,7},{8,8},{1,9},... | collective-permute-start | bytes 12296 | tf_op jit(solution)/shard_map/ppermute | solution.py:47
  56.4 7.6 %collective-permute-start.9 = (f32[4,256]{1,0:T(4,128)S(1)}, f32[4,256]{1,0:T(4,128)S(1)}, u32[]{:S(2)}, u32[]{:S(2)}) collective-permute-start(f32[4,256]{1,0:T(4,128)S(1)} %get-tuple-element.27), channel_id=1, source_target_pairs={{32,0},{25,1},{18,2},{43,3},{36,4},{29,5},{22,6},{47,7},{40,8},{33... | collective-permute-start | bytes 12296 | tf_op jit(solution)/shard_map/ppermute | solution.py:47
  64.0 7.9 %collective-permute-start.12 = (f32[4,256]{1,0:T(4,128)S(1)}, f32[4,256]{1,0:T(4,128)S(1)}, u32[]{:S(2)}, u32[]{:S(2)}) collective-permute-start(f32[4,256]{1,0:T(4,128)S(1)} %multiply_add_fusion.1), channel_id=1, source_target_pairs={{3,0},{0,1},{1,2},{2,3},{7,4},{4,5},{5,6},{6,7},{11,8},{8,9},{9,10... | collective-permute-start | bytes 12296 | tf_op jit(solution)/shard_map/ppermute | solution.py:47
  67.5 5.1 %collective-permute-start.11 = (f32[4,256]{1,0:T(4,128)S(1)}, f32[4,256]{1,0:T(4,128)S(1)}, u32[]{:S(2)}, u32[]{:S(2)}) collective-permute-start(f32[4,256]{1,0:T(4,128)S(1)} %multiply_add_fusion.1), channel_id=1, source_target_pairs={{2,0},{3,1},{0,2},{1,3},{6,4},{7,5},{4,6},{5,7},{10,8},{11,9},{8,1... | collective-permute-start | bytes 12296 | tf_op jit(solution)/shard_map/ppermute | solution.py:47
  68.8 3.9 %collective-permute-start.10 = (f32[4,256]{1,0:T(4,128)S(1)}, f32[4,256]{1,0:T(4,128)S(1)}, u32[]{:S(2)}, u32[]{:S(2)}) collective-permute-start(f32[4,256]{1,0:T(4,128)S(1)} %multiply_add_fusion.1), channel_id=1, source_target_pairs={{1,0},{2,1},{3,2},{0,3},{5,4},{6,5},{7,6},{4,7},{9,8},{10,9},{11,1... | collective-permute-start | bytes 12296 | tf_op jit(solution)/shard_map/ppermute | solution.py:47
